TPU v7x, 32 devices: a whole 2x2x4 slice. The times are simulated.
32 devices in a mesh: lat: 8 (over z, y), lon: 4 (over x, core).
Axes of the slice: x: 2, y: 2, z: 4, core: 2. Of those that a mesh axis runs over, the one named last changes fastest.
Arguments:
- block_in: bfloat16 [192, 720, 641], P('lat', 'lon'), may hold values from -6 to 6
- noise: bfloat16 [8, 192, 720], P(None, 'lat', 'lon'), may hold values from -6 to 6
- cotangent: bfloat16 [192, 720, 641], P('lat', 'lon'), may hold values from -6 to 6
- band_heights: int32 [8], replicated, may hold values from 1 to 24, 144 in all
- support_lon: int32 [192, 12], P('lat'), may hold values from -2 to 2
- support_vals: float32 [192, 12, 9], P('lat'), may hold values from -4 to 4
- master: float32 [1658880], P(('lat', 'lon')), as said below
- moment_one: float32 [1658880], P(('lat', 'lon')), may hold values from -1.335144e-05 to 1.335144e-05
- moment_two: float32 [1658880], P(('lat', 'lon')), may hold values from 1.808449e-14 to 1.8084491e-13
- average: float32 [1658880], P(('lat', 'lon')), may hold values from -0.75 to 0.75
- step_count: int32 [1], replicated, may hold values from 1 to 20
Outputs:
- block_out: bfloat16 [192, 720, 641], P('lat', 'lon')
- grad_in: float32 [192, 720, 641], P('lat', 'lon')
- grad_flat: float32 [1658880], P(('lat', 'lon'))
- grad_norm: float32 [1], replicated
- new_master: float32 [1658880], P(('lat', 'lon'))
- new_one: float32 [1658880], P(('lat', 'lon'))
- new_two: float32 [1658880], P(('lat', 'lon'))
- new_avg: float32 [1658880], P(('lat', 'lon'))
- copies: bfloat16 [1658880], P(('lat', 'lon'))
Inputs may be any that keep to these rules, and one draw needn't show every extreme that they name: `band_heights`: every band has at least one used row and together they hold 144 rows; some band is full. `master`: packed weights.
All inputs are finite; a program needn't handle non-finite values.
Results may differ from a plain program's by a relative error of at most 0.0014.
The roundings to bfloat16 on the way count: a program that leaves them out, or rounds other values in their place, can miss the bound.
Values may be sent and summed in bfloat16 or wider, within the bound.
A program may use at most 448 MiB of HBM per device.

v0:
```python
from functools import partial
import math

import jax
import jax.numpy as jnp
from jax import lax
from jax.sharding import PartitionSpec as P

C = 641
FF = 1282
NOISE = 8
K = 9
S = 12
LON_REACH = 2


highest_precision = lax.Precision.HIGHEST


def padded(array, sides, width, wrap):
    for axis, dim in sides:
        count, length = (lax.axis_size(axis), array.shape[dim])
        up = [(i, (i + 1) % count) for i in range(count if wrap else count - 1)]
        down = [(j, i) for i, j in up]
        last = lax.slice_in_dim(array, length - width, length, axis=dim)
        initial = lax.slice_in_dim(array, 0, width, axis=dim)
        before = lax.ppermute(last, axis, up)
        after = lax.ppermute(initial, axis, down)
        array = jnp.concatenate([before, array, after], axis=dim)
    return array


def unpack(flat):
    shapes = ((C, FF), (FF, C), (FF,), (C,), (C,), (K, C), (NOISE, C))
    pieces = []
    offset = 0
    for layout in shapes:
        amount = math.prod(layout)
        pieces.append(flat[offset : offset + amount].reshape(layout))
        offset = offset + amount
    return pieces


def stencil_table(support_vals, support_lon):
    lat_rows = (jnp.arange(S) % 3 - 1)[:, None] == jnp.arange(-1, 2)[None, :]
    lon_rows = support_lon[:, :, None] == jnp.arange(-LON_REACH, LON_REACH + 1)[None, None, :]
    return jnp.einsum(
        "hsk,sl,hsw->hlwk",
        support_vals,
        lat_rows.astype(jnp.float32),
        lon_rows.astype(jnp.float32),
        precision=highest_precision,
    )


def local(
    block_in,
    noise,
    cotangent,
    band_heights,
    support_lon,
    support_vals,
    master,
    moment_one,
    moment_two,
    average,
    step_count,
):
    lat_rows, lon_cols, channels = block_in.shape
    lon_reach = LON_REACH
    gathered = lax.all_gather(master.astype(jnp.bfloat16), ("lat", "lon"), axis=0, tiled=True)
    w_one, w_two, bias_one, bias_two, gain, w_disco, w_noise = unpack(gathered)
    height = lax.dynamic_index_in_dim(band_heights, lax.axis_index("lat"), 0, keepdims=False)
    row_index = lax.iota(jnp.int32, lat_rows)
    row_live = (row_index < height).astype(jnp.float32)[:, None, None]
    inputs = block_in.astype(jnp.float32)
    center = inputs - jnp.mean(inputs, -1, keepdims=True)
    variance = jnp.mean(center * center, -1, keepdims=True)
    inv_std = lax.rsqrt(variance + 1e-05)
    normed = center * inv_std
    gain_float = gain.astype(jnp.float32)
    mixed_in = (normed * gain_float * row_live).astype(jnp.bfloat16)
    stencil = stencil_table(support_vals, support_lon)
    kernel = jnp.einsum(
        "hlwk,kc->hlwc", stencil, w_disco.astype(jnp.float32), precision=highest_precision
    )
    cycle = padded(mixed_in, (("lon", 1),), lon_reach, True)
    edge_rows = jnp.stack(
        [cycle[0], lax.dynamic_index_in_dim(cycle, height - 1, 0, keepdims=False)]
    )
    beside_all = padded(edge_rows, (("lat", 0),), 1, False)
    extended = jnp.concatenate([beside_all[0:1], cycle, jnp.zeros_like(beside_all[0:1])], 0)
    extended = lax.dynamic_update_slice_in_dim(extended, beside_all[3:4], height + 1, 0)
    convolved = jnp.einsum("nhw,nc->hwc", noise, w_noise, preferred_element_type=jnp.float32)
    for lat_tap in range(3):
        for lon_tap in range(2 * lon_reach + 1):
            window = extended[lat_tap : lat_tap + lat_rows, lon_tap : lon_tap + lon_cols].astype(
                jnp.float32
            )
            convolved = convolved + kernel[:, lat_tap, lon_tap][:, None, :] * window
    conv_low = convolved.astype(jnp.bfloat16).reshape(lat_rows * lon_cols, channels)
    hidden = jnp.dot(conv_low, w_one, preferred_element_type=jnp.float32) + bias_one.astype(
        jnp.float32
    )
    active = jax.nn.gelu(hidden, approximate=True).astype(jnp.bfloat16)
    branch = jnp.dot(active, w_two, preferred_element_type=jnp.float32) + bias_two.astype(
        jnp.float32
    )
    flat_live = jnp.broadcast_to(row_live, (lat_rows, lon_cols, 1)).reshape(-1, 1)
    block_out = (
        ((inputs.reshape(-1, channels) + branch) * flat_live)
        .reshape(lat_rows, lon_cols, channels)
        .astype(jnp.bfloat16)
    )
    upstream = (cotangent.astype(jnp.float32) * row_live).reshape(-1, channels)
    upstream_low = upstream.astype(jnp.bfloat16)
    grad_two = lax.dot_general(
        active, upstream_low, (((0,), (0,)), ((), ())), preferred_element_type=jnp.float32
    )
    grad_bias_two = jnp.sum(upstream, 0)
    grad_active = lax.dot_general(
        upstream_low, w_two, (((1,), (1,)), ((), ())), preferred_element_type=jnp.float32
    )
    gelu_value, gelu_pull = jax.vjp(partial(jax.nn.gelu, approximate=True), hidden)
    grad_hidden = gelu_pull(grad_active)[0].astype(jnp.bfloat16)
    grad_one = lax.dot_general(
        conv_low, grad_hidden, (((0,), (0,)), ((), ())), preferred_element_type=jnp.float32
    )
    grad_bias_one = jnp.sum(grad_hidden.astype(jnp.float32), 0)
    grad_conv = lax.dot_general(
        grad_hidden, w_one, (((1,), (1,)), ((), ())), preferred_element_type=jnp.float32
    ).reshape(lat_rows, lon_cols, channels)
    grad_noise = jnp.einsum(
        "nhw,hwc->nc", noise.astype(jnp.float32), grad_conv, precision=highest_precision
    )
    grad_ext = jnp.zeros((lat_rows + 2, lon_cols + 2 * lon_reach, channels), jnp.float32)
    tap_sums = []
    for lat_tap in range(3):
        for lon_tap in range(2 * lon_reach + 1):
            window = extended[lat_tap : lat_tap + lat_rows, lon_tap : lon_tap + lon_cols].astype(
                jnp.float32
            )
            tap_sums.append(jnp.sum(grad_conv * window, 1))
            term = kernel[:, lat_tap, lon_tap][:, None, :] * grad_conv
            grad_ext = grad_ext + jnp.pad(
                term, ((lat_tap, 2 - lat_tap), (lon_tap, 2 * lon_reach - lon_tap), (0, 0))
            )
    tap_grid = jnp.stack(tap_sums, 1).reshape(lat_rows, 3, 2 * lon_reach + 1, channels)
    grad_disco = jnp.einsum("hlwk,hlwc->kc", stencil, tap_grid, precision=highest_precision)
    sent_rows = jnp.stack(
        [grad_ext[0], lax.dynamic_index_in_dim(grad_ext, height + 1, 0, keepdims=False)]
    )
    returned = padded(sent_rows.astype(jnp.bfloat16), (("lat", 0),), 1, False).astype(
        sent_rows.dtype
    )
    first_mask = (row_index == 0).astype(jnp.float32)[:, None, None]
    last_mask = (row_index == height - 1).astype(jnp.float32)[:, None, None]
    own_grads = (
        grad_ext[1 : lat_rows + 1] * row_live
        + first_mask * returned[0][None]
        + last_mask * returned[3][None]
    )
    side_cols = jnp.concatenate([own_grads[:, :lon_reach], own_grads[:, lon_cols + lon_reach :]], 1)
    wrapped = padded(side_cols.astype(jnp.bfloat16), (("lon", 1),), lon_reach, True).astype(
        side_cols.dtype
    )
    grad_mixed = own_grads[:, lon_reach : lon_reach + lon_cols]
    grad_mixed = grad_mixed + jnp.pad(
        wrapped[:, :lon_reach], ((0, 0), (0, lon_cols - lon_reach), (0, 0))
    )
    grad_mixed = grad_mixed + jnp.pad(
        wrapped[:, 3 * lon_reach :], ((0, 0), (lon_cols - lon_reach, 0), (0, 0))
    )
    grad_gain = jnp.sum(grad_mixed * normed, (0, 1))
    grad_normed = grad_mixed * gain_float
    grad_in = inv_std * (
        grad_normed
        - jnp.mean(grad_normed, -1, keepdims=True)
        - normed * jnp.mean(grad_normed * normed, -1, keepdims=True)
    )
    grad_in = grad_in + upstream.reshape(lat_rows, lon_cols, channels)
    local_flat = jnp.concatenate(
        [
            grad_one.reshape(-1),
            grad_two.reshape(-1),
            grad_bias_one,
            grad_bias_two,
            grad_gain,
            grad_disco.reshape(-1),
            grad_noise.reshape(-1),
        ]
    )
    local_flat = jnp.pad(local_flat, (0, gathered.shape[0] - local_flat.shape[0]))
    share_len = master.shape[0]
    summed = lax.psum(local_flat, ("lat", "lon"))
    norm_square = jnp.sum(summed * summed)
    grad_part = lax.dynamic_slice_in_dim(
        summed, lax.axis_index(("lat", "lon")) * share_len, share_len, 0
    )
    grad_norm = jnp.sqrt(norm_square)
    factor = 0.01 / jnp.maximum(grad_norm, 0.01)
    clipped = grad_part * factor
    new_one = 0.9 * moment_one + 0.1 * clipped
    new_two = 0.999 * moment_two + 0.001 * clipped * clipped
    step_float = step_count[0].astype(jnp.float32)
    fix_one = 1.0 - jnp.power(jnp.float32(0.9), step_float)
    fix_two = 1.0 - jnp.power(jnp.float32(0.999), step_float)
    update = new_one / fix_one / (jnp.sqrt(new_two / fix_two) + 1e-08) + 0.1 * master
    new_master = master - 0.02 * update
    new_avg = 0.9 * average + 0.1 * new_master
    return (
        block_out,
        grad_in,
        grad_part,
        grad_norm.reshape(1),
        new_master,
        new_one,
        new_two,
        new_avg,
        new_master.astype(jnp.bfloat16),
    )


def solution(mesh):
    return jax.shard_map(
        local,
        mesh=mesh,
        in_specs=(
            P("lat", "lon", None),
            P(None, "lat", "lon"),
            P("lat", "lon", None),
            P(),
            P("lat", None),
            P("lat", None, None),
            P(("lat", "lon")),
            P(("lat", "lon")),
            P(("lat", "lon")),
            P(("lat", "lon")),
            P(),
        ),
        out_specs=(
            P("lat", "lon", None),
            P("lat", "lon", None),
            P(("lat", "lon")),
            P(),
            P(("lat", "lon")),
            P(("lat", "lon")),
            P(("lat", "lon")),
            P(("lat", "lon")),
            P(("lat", "lon")),
        ),
        check_vma=False,
    )
```

profile of v0, /device:TPU:0, one launch (start us, length us, event | category | flops | bytes accessed | tf_op | source)
XLA Modules:
  0.0 910.0 jit_solution(7539364900613019605)
XLA Ops:
  17.7 9.1 %copy_convert_fusion = f32[24,180,641]{2,1,0:T(8,128)} fusion(bf16[24,180,641]{2,0,1:T(8,128)(2,1)} %param.11), kind=kLoop, calls=%fused_computation.109 | loop fusion | flops 2769120 | bytes 16614720 | tf_op jit(solution)/shard_map/convert_element_type | solution.py:76
  26.8 14.0 %reshape.143 = f32[4320,641]{1,0:T(8,128)} reshape(f32[24,180,641]{2,1,0:T(8,128)} %copy_convert_fusion) | data formatting | bytes 22152960 | tf_op jit(solution)/shard_map/reshape | solution.py:111
  40.8 13.3 %copy.51 = f32[4320,641]{0,1:T(8,128)} copy(f32[4320,641]{1,0:T(8,128)} %reshape.143) | data formatting | bytes 22152960 | tf_op jit(solution)/shard_map/reshape | solution.py:111
  54.8 4.8 convert_reduce_fusion.1
  59.6 6.6 multiply_reduce_fusion.2
  66.2 18.4 %all-gather.3.cloned.1.call-done = bf16[32,1,51840]{2,1,0:T(2,128)(2,1)} async-done(((bf16[1,1,51840]{2,1,0:T(2,128)(2,1)}), bf16[32,1,51840]{2,1,0:T(2,128)(2,1)}) %all-gather.3.cloned.1.call-update) | async-done | bytes 3317776 | tf_op jit(solution)/shard_map/all_gather | solution.py:71
  84.7 21.5 %reduce.1 = bf16[32,51840]{1,0:T(8,128)(2,1)} reduce(bf16[32,1,51840]{2,1,0:T(2,128)(2,1)} %all-gather.3.cloned.1.call-done, bf16[]{:T(256)} %constant.141), dimensions={1}, to_apply=%all-gather.reduce_sub_computation | reduce | bytes 6635522 | tf_op jit(solution)/shard_map/all_gather | solution.py:71
  106.1 6.2 reshape.156
  114.2 2.9 fusion.64
  117.2 11.7 %fusion.40 = (f32[641]{0:T(1024)}, bf16[24,180,641]{2,1,0:T(8,128)(2,1)}, bf16[24,180,641]{2,1,0:T(8,128)(2,1)S(1)}) fusion(f32[24]{0:T(128)S(1)} %compare_convert_fusion.2, bf16[24,180,641]{2,0,1:T(8,128)(2,1)} %param.13, f32[641]{0:T(1024)S(1)} %get-tuple-element.87, f32[24,180]{1,0:T(8,128)S(1)} %add_rsqrt_fusion, ...), kind=kLoop, calls=%fused_computation.82 | loop fusion | flops 27690560 | bytes 22192744 | tf_op jit(solution)/shard_map/reduce_sum | solution.py:120
  132.8 2.7 pad_maximum_fusion
  136.4 4.1 collective-permute-start.2
  142.3 5.1 reshape.160
  147.3 5.1 reshape.147
  152.5 5.9 reshape.148
  158.5 10.5 %convert_element_type.208 = bf16[4320,641]{1,0:T(8,128)(2,1)} reshape(bf16[24,180,641]{2,1,0:T(8,128)(2,1)} %get-tuple-element.85) | data formatting | bytes 11076480 | tf_op jit(solution)/shard_map/convert_element_type | solution.py:116
  169.9 1.7 collective-permute-start.3
  171.6 9.0 maximum_maximum_fusion
  181.6 66.7 %fusion.42 = bf16[24,180,641]{2,1,0:T(8,128)(2,1)} fusion(f32[24,641]{1,0:T(8,128)S(1)} %copy-done.56, f32[24,641]{1,0:T(8,128)S(1)} %copy-done.57, f32[24,641]{1,0:T(8,128)S(1)} %copy-done.58, f32[24,641]{1,0:T(8,128)S(1)} %get-tuple-element.96, f32[24,641]{1,0:T(8,128)S(1)} %get-tuple-element.97, f32[24,641]{1,0:T(8,128)S(1)} %copy-done.22, ...), kind=kOutput, calls=%fused_computation.86 | convolution fusion | flops 171685440 | bytes 89614256 | tf_op jit(solution)/shard_map/nhw,nc->hwc/dot_general | solution.py:94
  248.3 10.3 %reshape.146 = bf16[4320,641]{1,0:T(8,128)(2,1)} reshape(bf16[24,180,641]{2,1,0:T(8,128)(2,1)} %fusion.42) | data formatting | bytes 11076480 | tf_op jit(solution)/shard_map/reshape | solution.py:101
  258.7 23.5 %multiply_convert_fusion = (bf16[4320,1282]{0,1:T(8,128)(2,1)}, f32[4320,1282]{0,1:T(8,128)}) fusion(f32[1282]{0:T(1024)S(1)} %slice_convert_fusion.1, bf16[4320,641]{1,0:T(8,128)(2,1)} %reshape.146, bf16[641,1282]{1,0:T(8,128)(2,1)} %reshape.147), kind=kOutput, calls=%fused_computation.11 | convolution fusion | flops 7155406848 | bytes 40416332 | tf_op jit(solution)/shard_map/dot_general | solution.py:102
  282.2 27.7 %convert_reduce_fusion = (f32[1282]{0:T(1024)}, bf16[4320,1282]{0,1:T(8,128)(2,1)S(1)}) fusion(f32[4320,1282]{0,1:T(8,128)} %get-tuple-element.111, bf16[4320,641]{1,0:T(8,128)(2,1)} %convert_element_type.208, bf16[1282,641]{1,0:T(8,128)(2,1)S(1)} %copy-done.3), kind=kOutput, calls=%fused_computation.10 | convolution fusion | flops 7221864960 | bytes 40416332 | tf_op jit(solution)/shard_map/dot_general | solution.py:121
  309.9 4.3 copy-done.2
  314.2 15.3 %fusion.65 = f32[641,1282]{1,0:T(8,128)} fusion(bf16[4320,641]{1,0:T(8,128)(2,1)} %reshape.146, bf16[4320,1282]{0,1:T(8,128)(2,1)S(1)} %get-tuple-element.114), kind=kOutput, calls=%fused_computation.193 | convolution fusion | flops 7100023808 | bytes 19901768 | tf_op jit(solution)/shard_map/dot_general | solution.py:126
  329.6 15.9 %copy.54 = bf16[4320,1282]{1,0:T(8,128)(2,1)} copy(bf16[4320,1282]{0,1:T(8,128)(2,1)} %copy-done.2) | data formatting | bytes 22152960 | tf_op jit(solution)/shard_map/convert_element_type | solution.py:125
  345.5 14.0 %dot_general.53 = bf16[24,180,1282]{2,1,0:T(8,128)(2,1)} reshape(bf16[4320,1282]{1,0:T(8,128)(2,1)} %copy.54) | data formatting | bytes 22152960 | tf_op jit(solution)/shard_map/dot_general | solution.py:130
  359.4 70.7 %fusion.36 = (f32[24,641]{1,0:T(8,128)}, f32[24,641]{1,0:T(8,128)}, f32[24,641]{1,0:T(8,128)S(1)}, f32[24,641]{1,0:T(8,128)S(1)}, f32[24,641]{1,0:T(8,128)S(1)},...) fusion(bf16[26,184,641]{2,1,0:T(8,128)(2,1)} %constant_dynamic-, ...), kind=kOutput, calls=%fused_computation.72 | convolution fusion | flops 7232700416 | bytes 141207168 | tf_op jit(solution)/shard_map/dot_general | solution.py:130
  430.3 8.5 convolution_bitcast_fusion.2
  438.9 54.2 %broadcast_multiply_fusion.14 = (f32[24,180,641]{2,1,0:T(8,128)}, f32[24,180,641]{2,1,0:T(8,128)}, f32[24,180,641]{2,1,0:T(8,128)}, f32[24,180,641]{2,1,0:T(8,12...) fusion(f32[24,180,641]{2,1,0:T(8,128)} %get-tuple-element.112, ...), kind=kLoop, calls=%fused_computation.107 | loop fusion | flops 33229440 | bytes 144732672 | tf_op jit(solution)/shard_map/mul | solution.py:144
  493.1 15.1 %fusion.66 = f32[1282,641]{1,0:T(8,128)} fusion(bf16[4320,1282]{0,1:T(8,128)(2,1)} %get-tuple-element.110, bf16[4320,641]{1,0:T(8,128)(2,1)} %convert_element_type.208), kind=kOutput, calls=%fused_computation.194 | convolution fusion | flops 7100023808 | bytes 19901768 | tf_op jit(solution)/shard_map/dot_general | solution.py:117
  508.3 69.1 %pad_add_fusion = f32[26,184,641]{2,1,0:T(8,128)} fusion(f32[24,180,641]{2,1,0:T(8,128)} %get-tuple-element.63, f32[24,180,641]{2,1,0:T(8,128)} %get-tuple-element.64, f32[24,180,641]{2,1,0:T(8,128)} %get-tuple-element.65, f32[24,180,641]{2,1,0:T(8,128)} %get-tuple-element.67, f32[24,180,641]{2,1,0:T(8,128)} %get-tuple-element.68, ...), kind=kLoop, calls=%fused_computation.42 | loop fusion | flops 42931616 | bytes 178413376 | tf_op jit(solution)/shard_map/add | solution.py:145
  578.7 4.5 collective-permute-start.4
  590.0 15.9 %multiply_convert_fusion.2 = bf16[4320,641]{0,1:T(8,128)(2,1)} fusion(f32[4320,641]{0,1:T(8,128)} %copy.51, bf16[4320,1282]{0,1:T(8,128)(2,1)} %get-tuple-element.110, bf16[1282,641]{1,0:T(8,128)(2,1)S(1)} %copy-done.4, f32[4320]{0:T(1024)S(1)} %copy-done.64, f32[641]{0:T(1024)S(1)} %copy-done.68), kind=kOutput, calls=%fused_computation.89 | convolution fusion | flops 7111099392 | bytes 29354568 | tf_op jit(solution)/shard_map/dot_general | solution.py:106
  606.2 11.9 %fusion.59 = (bf16[24,184,641]{2,1,0:T(8,128)(2,1)S(1)}, f32[24,184,641]{2,1,0:T(8,128)}) fusion(f32[184,641]{1,0:T(8,128)S(1)} %get-tuple-element.91, f32[24]{0:T(128)S(1)} %copy-done.69, f32[184,641]{1,0:T(8,128)S(1)} %get-tuple-element.90, f32[24]{0:T(128)S(1)} %copy-done.70, f32[24]{0:T(128)S(1)} %copy-done.67, f32[26,184,641]{2,1,0:T(8,128)} %pad_add_fusion), kind=kLoop, calls=%fused_computation.188 | loop fusion | flops 16983936 | bytes 29250400 | tf_op jit(solution)/shard_map/convert.6
  618.4 1.7 collective-permute-start.7
  621.1 4.7 reshape.150
  625.8 5.3 reshape.149
  631.2 15.9 %reshape.165 = bf16[24,180,641]{1,0,2:T(8,128)(2,1)} reshape(bf16[4320,641]{0,1:T(8,128)(2,1)} %multiply_convert_fusion.2) | data formatting | bytes 11076480 | tf_op jit(solution)/shard_map/convert_element_type | solution.py:113
  647.1 13.2 %copy.58 = bf16[24,180,641]{2,0,1:T(8,128)(2,1)} copy(bf16[24,180,641]{1,0,2:T(8,128)(2,1)} %reshape.165) | data formatting | bytes 11076480
  662.4 1.8 maximum_convert_fusion
  664.9 12.1 %multiply_reduce_fusion = (f32[641]{0:T(1024)S(1)}, f32[24,180]{1,0:T(8,128)}, f32[24,180]{1,0:T(8,128)}) fusion(f32[24,180]{1,0:T(8,128)S(1)} %copy-done.15, f32[24,180]{1,0:T(8,128)S(1)} %copy-done.13, bf16[24,180,641]{2,0,1:T(8,128)(2,1)} %param.11, f32[24,2,641]{2,1,0:T(2,128)S(1)} %get-tuple-element.108, f32[24,2,641]{2,1,0:T(2,128)S(1)} %get-tuple-element.107, ...), kind=kLoop, calls=%fused_computation.78 | loop fusion | flops 30451040 | bytes 16935112 | tf_op jit(solution)/shard_map/reduce_sum | solution.py:174
  677.0 50.7 %concatenate.23 = f32[1656985]{0:T(1024)} concatenate(f32[821762]{0:T(1024)} %reshape.149, f32[821762]{0:T(1024)S(1)} %reshape.150, f32[1282]{0:T(1024)} %get-tuple-element.113, f32[641]{0:T(1024)S(1)} %copy-done.65, f32[641]{0:T(1024)S(1)} %get-tuple-element.51, f32[5769]{0:T(1024)S(1)} %copy-done.53, f32[5128]{0:T(1024)S(1)} %copy-done.52), dimensions={0} | concatenate | bytes 13255880 | tf_op jit(solution)/shard_map/concatenate | solution.py:182
  727.7 5.2 pad.89
  733.0 19.6 %multiply_add_fusion = f32[24,180,641]{2,1,0:T(8,128)} fusion(f32[24,180]{1,0:T(8,128)S(1)} %broadcast_multiply_fusion.15, f32[24,180]{1,0:T(8,128)S(1)} %broadcast_multiply_fusion.16, f32[24]{0:T(128)S(1)} %copy-done.67, f32[641]{0:T(1024)S(1)} %copy-done.63, f32[24,180]{1,0:T(8,128)S(1)} %copy-done.15, f32[24,180]{1,0:T(8,128)S(1)} %copy-done.13, ...), kind=kLoop, calls=%fused_computation.79 | loop fusion | flops 35998560 | bytes 33547364 | tf_op jit(solution)/shard_map/add | solution.py:181
  752.6 14.6 %copy.59 = f32[24,180,641]{2,0,1:T(8,128)} copy(f32[24,180,641]{2,1,0:T(8,128)} %multiply_add_fusion) | data formatting | bytes 22152960
  767.1 126.6 %all-reduce.20.cloned.1.call-done = f32[1658880]{0:T(1024)} async-done(((f32[1658880]{0:T(1024)}), f32[1658880]{0:T(1024)}) %all-reduce.20.cloned.1.call-update) | async-done | bytes 6635536 | tf_op jit(solution)/shard_map/psum | solution.py:195
  893.8 4.4 multiply_reduce_fusion.4
  898.9 2.0 fusion.57
  (211 shorter events, 31.1 us)
Async XLA Ops:
  7.2 77.5 %all-gather.3.cloned.1.call-start = ((), (), s32[]{:S(2)}) async-start(), calls=%async_computation.1 | async-start | bytes 6842880 | tf_op jit(solution)/shard_map/all_gather | solution.py:71
  9.0 884.8 %all-reduce.20.cloned.1.call-start = ((), (), s32[]{:S(2)}) async-start(), calls=%async_computation | async-start | bytes 13271040 | tf_op jit(solution)/shard_map/psum | solution.py:195
  15.0 102.1 %copy-start.66 = (f32[24]{0:T(128)}, f32[24]{0:T(128)S(1)}, u32[]{:S(2)}) copy-start(f32[24]{0:T(128)S(1)} %compare_convert_fusion.2) | copy-start | bytes 292
  17.7 113.1 %copy-start.8 = (f32[24,3,5,9]{0,3,2,1:T(8,128)}, f32[24,3,5,9]{0,3,2,1:T(8,128)S(1)}, u32[]{:S(2)}) copy-start(f32[24,3,5,9]{0,3,2,1:T(8,128)S(1)} %copy.50) | copy-start | bytes 38884
  59.6 57.5 %copy-start.12 = (f32[24,180]{1,0:T(8,128)}, f32[24,180]{1,0:T(8,128)S(1)}, u32[]{:S(2)}) copy-start(f32[24,180]{1,0:T(8,128)S(1)} %broadcast_multiply_fusion.17) | copy-start | bytes 51844
  66.2 62.6 %copy-start.14 = (f32[24,180]{1,0:T(8,128)}, f32[24,180]{1,0:T(8,128)S(1)}, u32[]{:S(2)}) copy-start(f32[24,180]{1,0:T(8,128)S(1)} %add_rsqrt_fusion) | copy-start | bytes 51844
  129.0 3.8 collective-permute-start
  129.3 3.5 collective-permute-start.1
  136.4 35.2 %collective-permute-start.2 = (bf16[1,184,641]{2,1,0:T(8,128)(2,1)}, bf16[1,184,641]{2,1,0:T(8,128)(2,1)}, u32[]{:S(2)}, u32[]{:S(2)}) collective-permute-start(bf16[1,184,641]{2,1,0:T(8,128)(2,1)} %get-tuple-element.81), channel_id=1, source_target_pairs={{0,4},{4,8},{8,12},{12,16},{16,20},{20,24},{24,28},{1,5},{5,9},{9,... | collective-permute-start | bytes 707672 | tf_op jit(solution)/shard_map/ppermute | solution.py:27
  141.4 40.1 %copy-start.16 = (f32[24,641]{1,0:T(8,128)}, f32[24,641]{1,0:T(8,128)S(1)}, u32[]{:S(2)}) copy-start(f32[24,641]{1,0:T(8,128)S(1)} %get-tuple-element.92) | copy-start | bytes 184612
  141.4 40.1 %copy-start.18 = (f32[24,641]{1,0:T(8,128)}, f32[24,641]{1,0:T(8,128)S(1)}, u32[]{:S(2)}) copy-start(f32[24,641]{1,0:T(8,128)S(1)} %get-tuple-element.96) | copy-start | bytes 184612
  141.4 40.1 %copy-start.20 = (f32[24,641]{1,0:T(8,128)}, f32[24,641]{1,0:T(8,128)S(1)}, u32[]{:S(2)}) copy-start(f32[24,641]{1,0:T(8,128)S(1)} %get-tuple-element.97) | copy-start | bytes 184612
  152.4 17.4 %copy-start.46 = (bf16[1,184,641]{2,1,0:T(8,128)(2,1)S(1)}, bf16[1,184,641]{2,1,0:T(8,128)(2,1)}, u32[]{:S(2)}) copy-start(bf16[1,184,641]{2,1,0:T(8,128)(2,1)} %get-tuple-element.80) | copy-start | bytes 707668
  152.4 19.2 %copy-start.43 = (bf16[24,2,641]{2,1,0:T(2,128)(2,1)S(1)}, bf16[24,2,641]{2,1,0:T(2,128)(2,1)}, u32[]{:S(2)}) copy-start(bf16[24,2,641]{2,1,0:T(2,128)(2,1)} %copy-done.42) | copy-start | bytes 184612
  152.5 19.2 %copy-start.45 = (bf16[24,2,641]{2,1,0:T(2,128)(2,1)S(1)}, bf16[24,2,641]{2,1,0:T(2,128)(2,1)}, u32[]{:S(2)}) copy-start(bf16[24,2,641]{2,1,0:T(2,128)(2,1)} %copy-done.44) | copy-start | bytes 184612
  158.4 23.0 %copy-start.22 = (f32[24,641]{1,0:T(8,128)S(1)}, f32[24,641]{1,0:T(8,128)}, u32[]{:S(2)}) copy-start(f32[24,641]{1,0:T(8,128)} %get-tuple-element.98) | copy-start | bytes 184612
  158.4 23.0 %copy-start.24 = (f32[24,641]{1,0:T(8,128)S(1)}, f32[24,641]{1,0:T(8,128)}, u32[]{:S(2)}) copy-start(f32[24,641]{1,0:T(8,128)} %get-tuple-element.99) | copy-start | bytes 184612
  158.4 23.1 %copy-start.26 = (f32[24,641]{1,0:T(8,128)S(1)}, f32[24,641]{1,0:T(8,128)}, u32[]{:S(2)}) copy-start(f32[24,641]{1,0:T(8,128)} %get-tuple-element.100) | copy-start | bytes 184612
  158.4 23.1 %copy-start.28 = (f32[24,641]{1,0:T(8,128)S(1)}, f32[24,641]{1,0:T(8,128)}, u32[]{:S(2)}) copy-start(f32[24,641]{1,0:T(8,128)} %get-tuple-element.101) | copy-start | bytes 184612
  158.5 23.1 %copy-start.30 = (f32[24,641]{1,0:T(8,128)S(1)}, f32[24,641]{1,0:T(8,128)}, u32[]{:S(2)}) copy-start(f32[24,641]{1,0:T(8,128)} %get-tuple-element.102) | copy-start | bytes 184612
  158.5 23.1 %copy-start.32 = (f32[24,641]{1,0:T(8,128)S(1)}, f32[24,641]{1,0:T(8,128)}, u32[]{:S(2)}) copy-start(f32[24,641]{1,0:T(8,128)} %get-tuple-element.103) | copy-start | bytes 184612
  158.5 23.1 %copy-start.34 = (f32[24,641]{1,0:T(8,128)S(1)}, f32[24,641]{1,0:T(8,128)}, u32[]{:S(2)}) copy-start(f32[24,641]{1,0:T(8,128)} %get-tuple-element.104) | copy-start | bytes 184612
  158.5 23.1 %copy-start.36 = (f32[24,641]{1,0:T(8,128)S(1)}, f32[24,641]{1,0:T(8,128)}, u32[]{:S(2)}) copy-start(f32[24,641]{1,0:T(8,128)} %get-tuple-element.105) | copy-start | bytes 184612
  158.5 23.1 %copy-start.38 = (f32[24,641]{1,0:T(8,128)S(1)}, f32[24,641]{1,0:T(8,128)}, u32[]{:S(2)}) copy-start(f32[24,641]{1,0:T(8,128)} %get-tuple-element.106) | copy-start | bytes 184612
  158.5 23.1 %copy-start.50 = (bf16[8,24,180]{2,1,0:T(8,128)(2,1)S(1)}, bf16[8,24,180]{2,1,0:T(8,128)(2,1)}, u32[]{:S(2)}) copy-start(bf16[8,24,180]{2,1,0:T(8,128)(2,1)} %param.12) | copy-start | bytes 207364
  158.5 23.1 %copy-start.56 = (f32[24,641]{1,0:T(8,128)S(1)}, f32[24,641]{1,0:T(8,128)}, u32[]{:S(2)}) copy-start(f32[24,641]{1,0:T(8,128)} %get-tuple-element.93) | copy-start | bytes 184612
  158.5 23.1 %copy-start.57 = (f32[24,641]{1,0:T(8,128)S(1)}, f32[24,641]{1,0:T(8,128)}, u32[]{:S(2)}) copy-start(f32[24,641]{1,0:T(8,128)} %get-tuple-element.94) | copy-start | bytes 184612
  158.5 23.1 %copy-start.58 = (f32[24,641]{1,0:T(8,128)S(1)}, f32[24,641]{1,0:T(8,128)}, u32[]{:S(2)}) copy-start(f32[24,641]{1,0:T(8,128)} %get-tuple-element.95) | copy-start | bytes 184612
  169.9 10.9 %collective-permute-start.3 = (bf16[1,184,641]{2,1,0:T(8,128)(2,1)S(1)}, bf16[1,184,641]{2,1,0:T(8,128)(2,1)S(1)}, u32[]{:S(2)}, u32[]{:S(2)}) collective-permute-start(bf16[1,184,641]{2,1,0:T(8,128)(2,1)S(1)} %copy-done.46), channel_id=1, source_target_pairs={{4,0},{8,4},{12,8},{16,12},{20,16},{24,20},{28,24},{5,1},{9,5},{13... | collective-permute-start | bytes 707672 | tf_op jit(solution)/shard_map/ppermute | solution.py:28
  258.7 23.6 %copy-start.3 = (bf16[1282,641]{1,0:T(8,128)(2,1)S(1)}, bf16[1282,641]{1,0:T(8,128)(2,1)}, u32[]{:S(2)}) copy-start(bf16[1282,641]{1,0:T(8,128)(2,1)} %reshape.148) | copy-start | bytes 4930576
  359.4 70.8 %copy-start.51 = (bf16[8,24,180]{2,1,0:T(8,128)(2,1)S(1)}, bf16[8,24,180]{2,1,0:T(8,128)(2,1)}, u32[]{:S(2)}) copy-start(bf16[8,24,180]{2,1,0:T(8,128)(2,1)} %param.12) | copy-start | bytes 207364
  508.3 81.7 %copy-start.4 = (bf16[1282,641]{1,0:T(8,128)(2,1)S(1)}, bf16[1282,641]{1,0:T(8,128)(2,1)}, u32[]{:S(2)}) copy-start(bf16[1282,641]{1,0:T(8,128)(2,1)} %reshape.148) | copy-start | bytes 4930576
  508.3 81.7 %copy-start.64 = (f32[4320]{0:T(1024)S(1)}, f32[4320]{0:T(1024)}, u32[]{:S(2)}) copy-start(f32[4320]{0:T(1024)} %broadcast_in_dim.8) | copy-start | bytes 51844
  508.3 81.7 %copy-start.68 = (f32[641]{0:T(1024)S(1)}, f32[641]{0:T(1024)}, u32[]{:S(2)}) copy-start(f32[641]{0:T(1024)} %get-tuple-element.86) | copy-start | bytes 7696
  578.7 27.3 %collective-permute-start.4 = (bf16[1,184,641]{2,1,0:T(8,128)(2,1)S(1)}, bf16[1,184,641]{2,1,0:T(8,128)(2,1)S(1)}, u32[]{:S(2)}, u32[]{:S(2)}) collective-permute-start(bf16[1,184,641]{2,1,0:T(8,128)(2,1)S(1)} %get-tuple-element.61), channel_id=1, source_target_pairs={{0,4},{4,8},{8,12},{12,16},{16,20},{20,24},{24,28},{1,5},{5,9},{9,... | collective-permute-start | bytes 707672 | tf_op jit(solution)/shard_map/ppermute | solution.py:27
  583.2 22.8 %collective-permute-start.5 = (bf16[1,184,641]{2,1,0:T(8,128)(2,1)S(1)}, bf16[1,184,641]{2,1,0:T(8,128)(2,1)S(1)}, u32[]{:S(2)}, u32[]{:S(2)}) collective-permute-start(bf16[1,184,641]{2,1,0:T(8,128)(2,1)S(1)} %get-tuple-element.62), channel_id=1, source_target_pairs={{4,0},{8,4},{12,8},{16,12},{20,16},{24,20},{28,24},{5,1},{9,5},{13... | collective-permute-start | bytes 707672 | tf_op jit(solution)/shard_map/ppermute | solution.py:28
  618.3 28.8 %copy-start.40 = (bf16[24,2,641]{2,1,0:T(2,128)(2,1)}, bf16[24,2,641]{2,1,0:T(2,128)(2,1)S(1)}, u32[]{:S(2)}) copy-start(bf16[24,2,641]{2,1,0:T(2,128)(2,1)S(1)} %get-tuple-element.78) | copy-start | bytes 184612
  618.3 28.8 %copy-start.41 = (bf16[24,2,641]{2,1,0:T(2,128)(2,1)}, bf16[24,2,641]{2,1,0:T(2,128)(2,1)S(1)}, u32[]{:S(2)}) copy-start(bf16[24,2,641]{2,1,0:T(2,128)(2,1)S(1)} %get-tuple-element.79) | copy-start | bytes 184612
  618.3 44.1 %collective-permute-start.6 = (bf16[24,2,641]{2,1,0:T(2,128)(2,1)S(1)}, bf16[24,2,641]{2,1,0:T(2,128)(2,1)}, u32[]{:S(2)}, u32[]{:S(2)}) collective-permute-start(bf16[24,2,641]{2,1,0:T(2,128)(2,1)S(1)} %get-tuple-element.78), channel_id=1, source_target_pairs={{0,1},{1,2},{2,3},{3,0},{4,5},{5,6},{6,7},{7,4},{8,9},{9,10},{10,1... | collective-permute-start | bytes 184616 | tf_op jit(solution)/shard_map/ppermute | solution.py:27
  618.4 44.1 %collective-permute-start.7 = (bf16[24,2,641]{2,1,0:T(2,128)(2,1)S(1)}, bf16[24,2,641]{2,1,0:T(2,128)(2,1)}, u32[]{:S(2)}, u32[]{:S(2)}) collective-permute-start(bf16[24,2,641]{2,1,0:T(2,128)(2,1)S(1)} %get-tuple-element.79), channel_id=1, source_target_pairs={{1,0},{2,1},{3,2},{0,3},{5,4},{6,5},{7,6},{4,7},{9,8},{10,9},{11,1... | collective-permute-start | bytes 184616 | tf_op jit(solution)/shard_map/ppermute | solution.py:28
  631.2 33.8 %copy-start.13 = (f32[24,180]{1,0:T(8,128)S(1)}, f32[24,180]{1,0:T(8,128)}, u32[]{:S(2)}) copy-start(f32[24,180]{1,0:T(8,128)} %copy-done.12) | copy-start | bytes 51844
  631.2 33.8 %copy-start.15 = (f32[24,180]{1,0:T(8,128)S(1)}, f32[24,180]{1,0:T(8,128)}, u32[]{:S(2)}) copy-start(f32[24,180]{1,0:T(8,128)} %copy-done.14) | copy-start | bytes 51844
  631.2 33.8 %copy-start.63 = (f32[641]{0:T(1024)S(1)}, f32[641]{0:T(1024)}, u32[]{:S(2)}) copy-start(f32[641]{0:T(1024)} %copy-done.62) | copy-start | bytes 7696
  660.3 16.7 %copy-start.65 = (f32[641]{0:T(1024)S(1)}, f32[641]{0:T(1024)}, u32[]{:S(2)}) copy-start(f32[641]{0:T(1024)} %get-tuple-element.84) | copy-start | bytes 7696
  752.6 146.3 %copy-start.11 = (f32[51840]{0:T(1024)S(1)}, f32[51840]{0:T(1024)}, u32[]{:S(2)}) copy-start(f32[51840]{0:T(1024)} %param.17) | copy-start | bytes 622084
  752.6 146.4 %copy-start.47 = (f32[51840]{0:T(1024)S(1)}, f32[51840]{0:T(1024)}, u32[]{:S(2)}) copy-start(f32[51840]{0:T(1024)} %param.19) | copy-start | bytes 622084
  752.6 146.4 %copy-start.48 = (f32[51840]{0:T(1024)S(1)}, f32[51840]{0:T(1024)}, u32[]{:S(2)}) copy-start(f32[51840]{0:T(1024)} %param.18) | copy-start | bytes 622084
  752.6 148.3 %copy-start.49 = (f32[51840]{0:T(1024)S(1)}, f32[51840]{0:T(1024)}, u32[]{:S(2)}) copy-start(f32[51840]{0:T(1024)} %param.20) | copy-start | bytes 622084
  (33 other events, 315.9 us)
Sparse Core Ops, SparseCore 0:
  11.4 73.2 all-gather.2
  733.0 160.6 all-reduce.19
where the time goes:
time: 918 us; the launch traced here: 910 us
  matrix products  246 us (27%)
  other arithmetic  245 us (27%)
  local copies, waits for them, and re-layouts  237 us (26%)
  waiting for transfers between devices  147 us (16%)
  between operations  20.6 us (2%)
  starting transfers between devices  15.3 us (2%)
    psum x1, waiting for transfers between devices, local(): summed = lax.psum(local_flat, ('lat', 'lon'))  127 us
    dot_general x1, matrix products, local(): lax.dot_general(grad_hidden, w_one, (((1,), (1,)), ((), ())), preferred_e...  70.7 us
    add x1, other arithmetic, local(): grad_ext + jnp.pad(term, ((lat_tap, 2 - lat_tap), (lon_tap, 2 * lon_reach...  69.1 us
    dot_general x1, matrix products, local(): jnp.einsum('nhw,nc->hwc', noise, w_noise, preferred_element_type=jnp.floa...  66.7 us
    mul x1, other arithmetic, local(): term = kernel[:, lat_tap, lon_tap][:, None, :] * grad_conv  54.2 us
    concatenate x1, local copies, waits for them, and re-layouts, local(): jnp.concatenate([grad_one.reshape(-1), grad_two.reshape(-1), grad_bias_on...  50.7 us
    unnamed x162, local copies, waits for them, and re-layouts  48.2 us
    dot_general x1, matrix products, local(): lax.dot_general(upstream_low, w_two, (((1,), (1,)), ((), ())), preferred_...  27.7 us
  transfers between devices with their start and end apart: 10, of which 4 were waited for; matrix products, arithmetic and copies ran while one was open for 21% of the time, Pallas kernels for 0%

commit v1 on v0

v1 whole, which is shorter than its diff:
```python
from functools import partial
import math

import jax
import jax.numpy as jnp
from jax import lax
from jax.experimental import pallas as pl
from jax.experimental.pallas import tpu as pltpu
from jax.sharding import PartitionSpec as P

C = 641
FF = 1282
NOISE = 8
K = 9
S = 12
REACH = 2
LANES = 128
CB = 6
CP = CB * LANES
FB = 11
FP = FB * LANES
TAPS = 15
MESH = pl.DeviceIdType.MESH
HIGHEST = lax.Precision.HIGHEST
F32 = jnp.float32
BF16 = jnp.bfloat16
VMEM_LIMIT = 60 * 1024 * 1024
ROW_TWO = (C * FF) // LANES
LANE_TWO = (C * FF) % LANES
TAIL_ROW = (2 * C * FF) // LANES
OFF_B1 = 2 * C * FF
OFF_B2 = OFF_B1 + FF
OFF_GAIN = OFF_B2 + C
OFF_DISCO = OFF_GAIN + C
OFF_NOISE = OFF_DISCO + K * C
END_FLAT = OFF_NOISE + NOISE * C


def params(**kw):
    return pltpu.CompilerParams(vmem_limit_bytes=VMEM_LIMIT, **kw)


def any_spec():
    return pl.BlockSpec(memory_space=pl.ANY)


def vmem_spec():
    return pl.BlockSpec(memory_space=pltpu.VMEM)


def iota(shape, dim):
    return lax.broadcasted_iota(jnp.int32, shape, dim)


def bit_list(mesh):
    bits = []
    for axis in ("lat", "lon"):
        count = int(math.log2(mesh.shape[axis]))
        assert 1 << count == mesh.shape[axis]
        bits += [(axis, b) for b in reversed(range(count))]
    return bits


def my_bits(bits):
    ids = {"lat": lax.axis_index("lat"), "lon": lax.axis_index("lon")}
    return [(ids[a] >> b) & 1 for a, b in bits]


def partner(axis, bit):
    lat, lon = lax.axis_index("lat"), lax.axis_index("lon")
    if axis == "lat":
        return (lat ^ (1 << bit), lon)
    return (lat, lon ^ (1 << bit))


def stage_orders(mesh):
    bits = bit_list(mesh)
    n = len(bits)
    if (mesh.shape["lat"], mesh.shape["lon"]) == (8, 4):
        return [[0, 1, 2, 3, 4], [0, 1, 3, 2, 4]]
    order = list(range(n))
    return [order, order]


def rotl_rows(v, unit):
    row = iota((8, LANES), 0)
    for b in range(3):
        amount = unit << b
        v = jnp.where((row >> b) & 1 == 1, pltpu.roll(v, LANES - amount, 1), v)
    return v


def row_vector(flat_ref, offset, length):
    blocks = -(-length // LANES)
    row, shift = divmod(offset, LANES)
    near = flat_ref[row : row + blocks, :]
    if shift:
        far = flat_ref[row + 1 : row + 1 + blocks, :]
        lane = iota((blocks, LANES), 1)
        near = pltpu.roll(jnp.where(lane >= shift, near, far), LANES - shift, 1)
    index = iota((blocks, LANES), 0) * LANES + iota((blocks, LANES), 1)
    return jnp.where(index < length, near, 0.0)


def put_row(ref, row, value):
    for q in range(value.shape[0]):
        ref[row : row + 1, q * LANES : (q + 1) * LANES] = value[q : q + 1, :].astype(ref.dtype)


def unpack_weights(flat, w1, w2, wn, wd, small, wnf):
    lane = iota((8, LANES), 1)
    row = iota((8, LANES), 0)

    def half_one(r0, q):
        start = 10 * r0 + q + r0 // 64
        near = flat[pl.ds(start, 8, stride=10), :]
        far = flat[pl.ds(start + 1, 8, stride=10), :]
        s0 = (2 * r0) % LANES
        v = jnp.where(lane >= s0 + 2 * row, near, far)
        v = rotl_rows(pltpu.roll(v, (LANES - s0) % LANES, 1), 2)
        ok = r0 + row < C
        if q == FB - 1:
            ok = ok & (lane < FF - (FB - 1) * LANES)
        return jnp.where(ok, v, 0.0)

    def body_one(a, carry):
        r0 = a * 16
        for q in range(FB):
            v = jnp.concatenate([half_one(r0, q), half_one(r0 + 8, q)], 0)
            w1[pl.ds(pl.multiple_of(r0, 16), 16), q * LANES : (q + 1) * LANES] = v.astype(BF16)
        return carry

    groups = -(-C // 16)
    lax.fori_loop(0, groups, body_one, 0)
    w1[groups * 16 :, :] = jnp.zeros((CP - groups * 16, FP), BF16)

    def half_two(r0, q):
        start = ROW_TWO + 5 * r0 + q + (LANE_TWO + r0) // LANES
        v0 = flat[pl.ds(start, 8, stride=5), :]
        v1 = flat[pl.ds(start + 1, 8, stride=5), :]
        v2 = flat[pl.ds(start + 2, 8, stride=5), :]
        s0 = (LANE_TWO + r0) % LANES
        s = s0 + row
        v = jnp.where(lane >= s, v0, jnp.where(lane >= s - LANES, v1, v2))
        v = rotl_rows(pltpu.roll(v, (LANES - s0) % LANES, 1), 1)
        ok = r0 + row < FF
        if q == CB - 1:
            ok = ok & (lane < C - (CB - 1) * LANES)
        return jnp.where(ok, v, 0.0)

    def body_two(a, carry):
        r0 = a * 16
        for q in range(CB):
            v = jnp.concatenate([half_two(r0, q), half_two(r0 + 8, q)], 0)
            w2[pl.ds(pl.multiple_of(r0, 16), 16), q * LANES : (q + 1) * LANES] = v.astype(BF16)
        return carry

    groups = -(-FF // 16)
    lax.fori_loop(0, groups, body_two, 0)
    w2[groups * 16 :, :] = jnp.zeros((FP - groups * 16, CP), BF16)
    small[...] = jnp.zeros_like(small)
    put_row(small, 0, row_vector(flat, OFF_B1, FF))
    put_row(small, 1, row_vector(flat, OFF_B2, C))
    put_row(small, 2, row_vector(flat, OFF_GAIN, C))
    wd[...] = jnp.zeros_like(wd)
    wnf[...] = jnp.zeros_like(wnf)
    for k in range(K):
        put_row(wd, k, row_vector(flat, OFF_DISCO + k * C, C))
    for k in range(NOISE):
        put_row(wnf, 1 + k, row_vector(flat, OFF_NOISE + k * C, C))
    wn[...] = wnf[...].astype(BF16)


def neighbours():
    lat, lon = lax.axis_index("lat"), lax.axis_index("lon")
    nlat, nlon = lax.axis_size("lat"), lax.axis_size("lon")
    return lat, lon, nlat, nlon, lax.rem(lon + 1, nlon), lax.rem(lon + nlon - 1, nlon)


def halo_copies(cols, rows, corners, colh, rowh, cornh, send, recv):
    lat, lon, nlat, nlon, east, west = neighbours()
    out = []

    def add(src, dst, target, k, sends, gets):
        out.append(
            (
                sends,
                gets,
                pltpu.make_async_remote_copy(
                    src_ref=src,
                    dst_ref=dst,
                    send_sem=send.at[k],
                    recv_sem=recv.at[k],
                    device_id=target,
                    device_id_type=MESH,
                ),
            )
        )

    has_up, has_down = lat > 0, lat < nlat - 1
    up, down = lat - 1, lat + 1
    add(rows.at[0], rowh.at[1], (up, lon), 2, has_up, has_down)
    add(rows.at[1], rowh.at[0], (down, lon), 3, has_down, has_up)
    add(cols.at[0], colh.at[1], (lat, west), 0, None, None)
    add(cols.at[1], colh.at[0], (lat, east), 1, None, None)
    add(corners.at[0, 0], cornh.at[1, 1], (up, west), 4, has_up, has_down)
    add(corners.at[0, 1], cornh.at[1, 0], (up, east), 5, has_up, has_down)
    add(corners.at[1, 0], cornh.at[0, 1], (down, west), 6, has_down, has_up)
    add(corners.at[1, 1], cornh.at[0, 0], (down, east), 7, has_down, has_up)
    return out


def start_halo(copies):
    for sends, _, copy in copies:
        if sends is None:
            copy.start()
        else:
            pl.when(sends)(copy.start)


def wait_halo(copies):
    for sends, gets, copy in copies:
        if sends is None:
            copy.wait()
        else:
            pl.when(sends)(copy.wait_send)
            pl.when(gets)(copy.wait_recv)


def greet(bits, halo):
    barrier = pltpu.get_barrier_semaphore()
    lat, lon, nlat, nlon, east, west = neighbours()

    def hello(target):
        pl.semaphore_signal(barrier, inc=1, device_id=target, device_id_type=MESH)

    count = 0
    for axis, bit in bits:
        hello(partner(axis, bit))
        count += 1
    if halo:
        for target in ((lat, east), (lat, west)):
            hello(target)
            count += 1
        for side, cond in ((lat - 1, lat > 0), (lat + 1, lat < nlat - 1)):

            @pl.when(cond)
            def _(side=side):
                for x in (lon, east, west):
                    hello((side, x))

    if halo:
        count = count + 3 * (lat > 0).astype(jnp.int32) + 3 * (lat < nlat - 1).astype(jnp.int32)
    pl.semaphore_wait(barrier, count)


def gather_kernel(
    mesh, share_ref, cols, rows, corners,
    w1, w2, wn, wd, small, colh, rowh, cornh,
    buf, flat, wnf, send, recv, hsend, hrecv, local_sem,
):
    bits = bit_list(mesh)
    orders = stage_orders(mesh)
    mine = my_bits(bits)
    n = len(bits)
    shard_rows = share_ref.shape[0]
    cut = (shard_rows // 2 + 15) // 16 * 16
    spans = [(0, cut), (cut, shard_rows - cut)]
    own = pltpu.make_async_copy(share_ref, buf.at[tuple(mine)], local_sem)
    own.start()
    greet(bits, True)
    halos = halo_copies(cols, rows, corners, colh, rowh, cornh, hsend, hrecv)

    def copy(colour, k):
        order = orders[colour]
        done = order[:k]
        start, count = spans[colour]
        index = tuple(slice(None) if i in done else mine[i] for i in range(n)) + (
            pl.ds(start, count),
        )
        return pltpu.make_async_remote_copy(
            src_ref=buf.at[index],
            dst_ref=buf.at[index],
            send_sem=send.at[colour, k],
            recv_sem=recv.at[colour, k],
            device_id=partner(*bits[order[k]]),
            device_id_type=MESH,
        )

    own.wait()
    for colour in range(2):
        copy(colour, 0).start()
    start_halo(halos)
    for k in range(n):
        for colour in range(2):
            copy(colour, k).wait()
            if k + 1 < n:
                copy(colour, k + 1).start()
    wait_halo(halos)
    lat, _, nlat, *_ = neighbours()
    for r, cond in ((0, lat == 0), (1, lat == nlat - 1)):

        @pl.when(cond)
        def _(r=r):
            rowh[r] = jnp.zeros(rowh.shape[1:], rowh.dtype)
            for s in range(2):
                cornh[r, s] = jnp.zeros(cornh.shape[2:], cornh.dtype)

    total = 1 << n

    def widen(d, carry):
        index = tuple((d >> (n - 1 - i)) & 1 for i in range(n))
        flat[pl.ds(d * shard_rows, shard_rows), :] = buf[index].astype(F32)
        return carry

    lax.fori_loop(0, total, widen, 0)
    flat[total * shard_rows :, :] = jnp.zeros((flat.shape[0] - total * shard_rows, LANES), F32)
    unpack_weights(flat, w1, w2, wn, wd, small, wnf)


def gather_weights(mesh, share, cols, rows, corners):
    bits = bit_list(mesh)
    n = len(bits)
    shard_rows = share.shape[0]
    total = shard_rows << n
    sd = jax.ShapeDtypeStruct
    return pl.pallas_call(
        partial(gather_kernel, mesh),
        name="gather_weights",
        out_shape=(
            sd((CP, FP), BF16),
            sd((FP, CP), BF16),
            sd((LANES, CP), BF16),
            sd((16, CP), F32),
            sd((8, FP), F32),
            sd(cols.shape, BF16),
            sd(rows.shape, BF16),
            sd(corners.shape, BF16),
        ),
        in_specs=[vmem_spec()] * 4,
        out_specs=(vmem_spec(),) * 8,
        scratch_shapes=[
            pltpu.VMEM((2,) * n + (shard_rows, LANES), BF16),
            pltpu.VMEM((total + 96, LANES), F32),
            pltpu.VMEM((LANES, CP), F32),
            pltpu.SemaphoreType.DMA((2, n)),
            pltpu.SemaphoreType.DMA((2, n)),
            pltpu.SemaphoreType.DMA((8,)),
            pltpu.SemaphoreType.DMA((8,)),
            pltpu.SemaphoreType.DMA,
        ],
        compiler_params=params(collective_id=0, has_side_effects=True),
    )(share, cols, rows, corners)


def norm_parts(x):
    mean = jnp.mean(x, -1, keepdims=True)
    center = x - mean
    var = jnp.mean(center * center, -1, keepdims=True)
    return center, lax.rsqrt(var + 1e-05)


def rounded(v):
    return v.astype(BF16).astype(F32)


def stencil_fwd_kernel(
    chunks, cells, height_ref, x_ref, colh, rowh, cornh, table, wd, gain, aug, wn,
    out_ref, m_scr, k_scr, nt_scr,
):
    step = pl.program_id(0)
    rows = x_ref.shape[1]
    width = chunks * cells
    height = height_ref[0]
    slots = m_scr.shape[2] // (width + 2 * REACH) if m_scr.ndim == 3 else 32
    gvec = gain[2:3, :C]

    def bottom_mix(j, base):
        return base

    def put_cell(column, x, top, low):
        center, inv = norm_parts(x)
        mixed = rounded(center * inv * gvec)
        hrow = iota((rows, C), 0)
        mixed = jnp.where(hrow < height, mixed, jnp.where(hrow == height, low, 0.0))
        for g in range(CB):
            lo, hi = g * LANES, min((g + 1) * LANES, C)
            m_scr[g, column, 1 : rows + 1, : hi - lo] = mixed[:, lo:hi]
            m_scr[g, column, 0:1, : hi - lo] = top[:, lo:hi]
            m_scr[g, column, rows + 1 : rows + 2, : hi - lo] = low[:, lo:hi]

    def halo_mix(v):
        center, inv = norm_parts(v.astype(F32))
        return rounded(center * inv * gvec)

    @pl.when(step == 0)
    def _():
        k_scr[...] = jnp.dot(
            table[...], wd[...], preferred_element_type=F32, precision=HIGHEST
        ).reshape(k_scr.shape)
        lat = lax.axis_index("lat")
        for side in range(2):
            for i in range(REACH):
                column = i if side == 0 else width + REACH + i
                top = halo_mix(cornh[0, side])[i : i + 1]
                low = halo_mix(cornh[1, side])[i : i + 1]
                put_cell(column, colh[side, i].astype(F32), top, low)

    @pl.when(step < chunks)
    def _():
        top = halo_mix(rowh[0, 0])
        low = halo_mix(rowh[0, 1])
        nt_scr[0:cells, :C] = top
        nt_scr[32 : 32 + cells, :C] = low

        def cell(j, carry):
            put_cell(
                step * cells + j + REACH,
                x_ref[j].astype(F32),
                nt_scr[pl.ds(j, 1), :C],
                nt_scr[pl.ds(32 + j, 1), :C],
            )
            return carry

        lax.fori_loop(0, cells, cell, 0)

    @pl.when(step >= chunks)
    def _():
        first = (step - chunks) * cells
        nt_scr[...] = jnp.dot(
            aug[...].reshape(cells * rows, LANES), wn[...], preferred_element_type=F32
        )
        lane = iota((8, LANES), 1)
        for g in range(CB):
            lanes = slice(g * LANES, (g + 1) * LANES)
            for hb in range(rows // 8):
                taps = [k_scr[t, 8 * hb : 8 * hb + 8, lanes] for t in range(TAPS)]

                def cell(j, carry):
                    acc = nt_scr[pl.ds(j * rows + 8 * hb, 8), lanes]
                    for t in range(TAPS):
                        l, w = divmod(t, 5)
                        acc = acc + taps[t] * m_scr[g, first + j + w, 8 * hb + l : 8 * hb + l + 8, :]
                    if g == CB - 1:
                        extra = aug[j, 8 * hb : 8 * hb + 8, :].astype(F32)
                        acc = jnp.where(lane == 0, acc, extra)
                    out_ref[j, 8 * hb : 8 * hb + 8, lanes] = acc.astype(BF16)
                    return carry

                lax.fori_loop(0, cells, cell, 0, unroll=2)


def stencil_fwd(height, x, colh, rowh, cornh, table, wd, small, aug, wn, chunks):
    width, rows, _ = x.shape
    cells = width // chunks
    first = lambda i: jnp.where(i < chunks, i, chunks - 1)
    second = lambda i: jnp.where(i < chunks, 0, i - chunks)
    return pl.pallas_call(
        partial(stencil_fwd_kernel, chunks, cells),
        name="stencil_fwd",
        grid=(2 * chunks,),
        out_shape=jax.ShapeDtypeStruct((width, rows, CP), BF16),
        in_specs=[
            pl.BlockSpec(memory_space=pltpu.SMEM),
            pl.BlockSpec((cells, rows, C), lambda i: (first(i), 0, 0)),
            vmem_spec(),
            pl.BlockSpec((1, 2, cells, C), lambda i: (first(i), 0, 0, 0)),
            vmem_spec(),
            vmem_spec(),
            vmem_spec(),
            vmem_spec(),
            pl.BlockSpec((cells, rows, LANES), lambda i: (second(i), 0, 0)),
            vmem_spec(),
        ],
        out_specs=pl.BlockSpec((cells, rows, CP), lambda i: (second(i), 0, 0)),
        scratch_shapes=[
            pltpu.VMEM((CB, width + 2 * REACH, 32, LANES), F32),
            pltpu.VMEM((TAPS, rows, CP), F32),
            pltpu.VMEM((cells * rows, CP), F32),
        ],
        compiler_params=params(dimension_semantics=("arbitrary",)),
    )(height, x, colh, rowh, cornh, table, wd, small, aug, wn)


def pack_weights(one, two, flat):
    lane = iota((8, LANES), 1)
    row = iota((8, LANES), 0)
    flat[...] = jnp.zeros_like(flat)

    def turned(v, s0, unit):
        return pltpu.roll(pltpu.roll(v, s0, 1), 0, 1, stride=unit, stride_axis=0)

    def one_main(a, carry):
        r0 = pl.multiple_of(a * 8, 8)
        s0 = (2 * r0) % LANES
        keep = lane >= s0 + 2 * row
        before = jnp.zeros((8, LANES), F32)
        for q in range(FB - 1):
            now = turned(one[q, pl.ds(r0, 8), :], s0, 2)
            flat[pl.ds(10 * r0 + q + r0 // 64, 8, stride=10), :] = jnp.where(keep, now, before)
            before = now
        return carry

    def one_rest(a, carry):
        r0 = pl.multiple_of(a * 8, 8)
        s0 = (2 * r0) % LANES
        s = s0 + 2 * row
        before = turned(one[FB - 2, pl.ds(r0, 8), :], s0, 2)
        now = turned(one[FB - 1, pl.ds(r0, 8), :], s0, 2)
        v = jnp.where(lane < s, before, jnp.where(lane < s + FF - (FB - 1) * LANES, now, 0.0))
        at = pl.ds(10 * r0 + FB - 1 + r0 // 64, 8, stride=10)
        flat[at, :] = flat[at, :] + v
        return carry

    lax.fori_loop(0, C // 8, one_main, 0)
    last = C - 1
    assert last % 64 == 0 and C % 8 == 1
    for q in range(FB - 1):
        at = 10 * last + q + last // 64
        flat[at : at + 1, :] = one[q, last : last + 1, :]
    lax.fori_loop(0, C // 8, one_rest, 0)

    groups = -(-(FF + LANE_TWO) // 8)

    def two_rolled(q, a):
        v = turned(two[q, pl.ds(8 * a + 8 - LANE_TWO, 8), :], (8 * a) % LANES, 1)
        r = 8 * a - LANE_TWO + row
        return jnp.where((r >= 0) & (r < FF), v, 0.0)

    def two_base(a):
        return ROW_TWO + 5 * (8 * a - LANE_TWO) + a // 16

    def two_main(a, carry, add=False):
        keep = lane >= (8 * a) % LANES + row
        before = jnp.zeros((8, LANES), F32)
        for q in range(CB - 1):
            now = two_rolled(q, a)
            at = pl.ds(two_base(a) + q, 8, stride=5)
            v = jnp.where(keep, now, before)
            flat[at, :] = flat[at, :] + v if add else v
            before = now
        return carry

    def two_rest(a, carry):
        s = (8 * a) % LANES + row
        before = two_rolled(CB - 2, a)
        now = two_rolled(CB - 1, a)
        v = jnp.where(lane < s, before, jnp.where(lane < s + C - (CB - 1) * LANES, now, 0.0))
        at = pl.ds(two_base(a) + CB - 1, 8, stride=5)
        flat[at, :] = flat[at, :] + v
        return carry

    lax.fori_loop(1, groups, two_main, 0)
    two_main(0, 0, add=True)
    at = 10 * last + FB - 1 + last // 64
    lane1 = iota((1, LANES), 1)
    v = jnp.where(lane1 < FF - (FB - 1) * LANES, one[FB - 1, last : last + 1, :], 0.0)
    flat[at : at + 1, :] = flat[at : at + 1, :] + v
    lax.fori_loop(0, groups, two_rest, 0)


GELU_A = math.sqrt(2.0 / math.pi)
GELU_B = 0.044715
WIDE = 256


def dot(a, b, dims=((1,), (0,))):
    return lax.dot_general(a, b, (dims, ((), ())), preferred_element_type=F32)


def mlp_kernel(
    blocks, height_ref, conv_ref, g_ref, x_ref, w1, w2, small,
    out_ref, gconv_ref, rows_ref, cols_ref, corn_ref, flat_ref, extra_ref,
    one, two, g_scr, conv_t, g_t, branch, gc,
):
    step = pl.program_id(0)
    cells, rows, _ = x_ref.shape
    m = cells * rows
    height = height_ref[0]

    @pl.when(step == 0)
    def _():
        one[...] = jnp.zeros_like(one)
        two[...] = jnp.zeros_like(two)
        g_scr[...] = jnp.zeros_like(g_scr)

    live = (iota((1, rows, 1), 1) < height).astype(F32)
    g_scr[:, :C] = (g_ref[...].astype(F32) * live).reshape(m, C).astype(BF16)
    conv = conv_ref[...].reshape(m, CP)
    conv_t[...] = conv.T[: conv_t.shape[0]]
    branch[...] = jnp.zeros_like(branch)
    gc[...] = jnp.zeros_like(gc)
    rows_one = conv_t.shape[0]

    def chunk(start, wide, tail):
        lanes = pl.ds(start, wide)
        conv_block = conv_ref[...].reshape(m, CP)
        g_block = g_scr[...]
        h = dot(conv_block, w1[:, lanes]) + small[0:1, lanes]
        ga = dot(g_block, w2[lanes, :], ((1,), (1,)))
        h2 = h * h
        t = jnp.tanh(h * (GELU_A + (GELU_A * GELU_B) * h2))
        cdf = 0.5 * t + 0.5
        act = (h * cdf).astype(BF16)
        slope = cdf + h * (0.5 - 0.5 * (t * t)) * (GELU_A + (3 * GELU_A * GELU_B) * h2)
        gh = (ga * slope).astype(BF16)
        if tail:
            act = jnp.where(iota((m, wide), 1) == FF - (FB - 1) * LANES, jnp.ones_like(act), act)
        branch[...] += dot(act, w2[lanes, :])
        gc[...] += dot(gh, w1[:, lanes], ((1,), (1,)))
        r1 = dot(conv_t[...], gh)
        r2 = dot(act, g_block, ((0,), (0,)))
        for i in range(wide // LANES):
            one[start // LANES + i] += r1[:, i * LANES : (i + 1) * LANES]
        for q in range(CB):
            two[q, pl.ds(start + 8, wide), :] += r2[:, q * LANES : (q + 1) * LANES]

    def body(f, carry):
        chunk(pl.multiple_of(f * WIDE, WIDE), WIDE, False)
        return carry

    lax.fori_loop(0, FP // WIDE, body, 0)
    chunk(FP // WIDE * WIDE, FP % WIDE, True)

    out = x_ref[...].astype(F32).reshape(m, C) + branch[:, :C] + small[1:2, :C]
    out_ref[...] = (out.reshape(cells, rows, C) * live).astype(BF16)
    gconv_ref[...] = gc[...].reshape(cells, rows, CP)
    onehot = (iota((1, rows, 1), 1) == height - 1).astype(F32)
    block = gc[...].reshape(cells, rows, CP)
    edges = (block[:, 0, :].astype(BF16), jnp.sum(block * onehot, 1).astype(BF16))
    for r in range(2):
        rows_ref[0, r] = edges[r]
    for side, at, first in ((0, 0, 0), (1, blocks - 1, cells - REACH)):

        @pl.when(step == at)
        def _(side=side, first=first):
            for i in range(REACH):
                base = (first + i) * rows
                cols_ref[side, i] = gc[base : base + rows, :].astype(BF16)
            for r in range(2):
                corn_ref[r, side] = edges[r][first : first + REACH]

    @pl.when(step == blocks - 1)
    def _():
        extra_ref[...] = jnp.zeros_like(extra_ref)
        for q in range(FB):
            extra_ref[0 : NOISE + 1, q * LANES : (q + 1) * LANES] = one[q, C : C + NOISE + 1, :]
        for q in range(CB):
            lanes = slice(q * LANES, (q + 1) * LANES)
            extra_ref[NOISE + 1 : NOISE + 2, lanes] = two[q, FF + 8 : FF + 9, :]
        pack_weights(one, two, flat_ref)


def mlp(height, conv, g, x, w1, w2, small, flat_rows, blocks):
    width, rows, _ = x.shape
    cells = width // blocks
    m = cells * rows
    sd = jax.ShapeDtypeStruct
    block = lambda c: pl.BlockSpec((cells, rows, c), lambda i: (i, 0, 0))
    rows_one = -(-(C + NOISE + 1) // 16) * 16
    flops = 12 * width * rows * C * FF
    return pl.pallas_call(
        partial(mlp_kernel, blocks),
        name="mlp",
        grid=(blocks,),
        out_shape=(
            sd((width, rows, C), BF16),
            sd((width, rows, CP), F32),
            sd((blocks, 2, cells, CP), BF16),
            sd((2, REACH, rows, CP), BF16),
            sd((2, 2, REACH, CP), BF16),
            sd((flat_rows, LANES), F32),
            sd((16, FP), F32),
        ),
        in_specs=[
            pl.BlockSpec(memory_space=pltpu.SMEM),
            block(CP),
            block(C),
            block(C),
            vmem_spec(),
            vmem_spec(),
            vmem_spec(),
        ],
        out_specs=(
            block(C),
            block(CP),
            pl.BlockSpec((1, 2, cells, CP), lambda i: (i, 0, 0, 0)),
            vmem_spec(),
            vmem_spec(),
            vmem_spec(),
            vmem_spec(),
        ),
        scratch_shapes=[
            pltpu.VMEM((FB, rows_one, LANES), F32),
            pltpu.VMEM((CB, FP + 16, LANES), F32),
            pltpu.VMEM((m, CP), BF16),
            pltpu.VMEM((rows_one, m), BF16),
            pltpu.VMEM((8, LANES), BF16),
            pltpu.VMEM((m, CP), F32),
            pltpu.VMEM((m, CP), F32),
        ],
        compiler_params=params(dimension_semantics=("arbitrary",)),
        cost_estimate=pl.CostEstimate(flops=flops, bytes_accessed=50_000_000, transcendentals=0),
    )(height, conv, g, x, w1, w2, small)


def exchange_kernel(cols, rows, corners, colh, rowh, cornh, send, recv):
    greet([], True)
    halos = halo_copies(cols, rows, corners, colh, rowh, cornh, send, recv)
    start_halo(halos)
    wait_halo(halos)
    lat, _, nlat, *_ = neighbours()
    for r, cond in ((0, lat == 0), (1, lat == nlat - 1)):

        @pl.when(cond)
        def _(r=r):
            rowh[r] = jnp.zeros(rowh.shape[1:], rowh.dtype)
            for s in range(2):
                cornh[r, s] = jnp.zeros(cornh.shape[2:], cornh.dtype)


def exchange(cols, rows, corners):
    sd = jax.ShapeDtypeStruct
    return pl.pallas_call(
        exchange_kernel,
        name="exchange_edges",
        out_shape=(sd(cols.shape, BF16), sd(rows.shape, BF16), sd(corners.shape, BF16)),
        in_specs=[vmem_spec()] * 3,
        out_specs=(vmem_spec(),) * 3,
        scratch_shapes=[pltpu.SemaphoreType.DMA((8,)), pltpu.SemaphoreType.DMA((8,))],
        compiler_params=params(collective_id=1, has_side_effects=True),
    )(cols, rows, corners)


def scatter_kernel(mesh, flat, out_ref, buf, *rest):
    bits = bit_list(mesh)
    n = len(bits)
    recvs, (send, recv) = rest[:n], rest[n:]
    orders = [order[::-1] for order in stage_orders(mesh)]
    mine = my_bits(bits)
    shard_rows = out_ref.shape[0]
    cut = (shard_rows // 2 + 7) // 8 * 8
    spans = [(0, cut), (cut, shard_rows - cut)]

    def shard_index(d):
        return tuple((d >> (n - 1 - i)) & 1 for i in range(n))

    def fill(d, carry):
        buf[shard_index(d)] = flat[pl.ds(d * shard_rows, shard_rows), :]
        return carry

    lax.fori_loop(0, 1 << n, fill, 0)
    greet(bits, False)

    def copy(colour, k):
        order = orders[colour]
        done, now = order[:k], order[k]
        start, count = spans[colour]
        index = tuple(
            1 - mine[i] if i == now else mine[i] if i in done else slice(None) for i in range(n)
        )
        at = pl.ds(start, count)
        return pltpu.make_async_remote_copy(
            src_ref=buf.at[index + (at,)],
            dst_ref=recvs[k].at[(slice(None),) * (n - 1 - k) + (at,)],
            send_sem=send.at[colour, k],
            recv_sem=recv.at[colour, k],
            device_id=partner(*bits[now]),
            device_id_type=MESH,
        )

    def accumulate(colour, k):
        order = orders[colour]
        start, count = spans[colour]
        free = [i for i in range(n) if i not in order[: k + 1]]

        def add(d, carry):
            sub = tuple((d >> (len(free) - 1 - i)) & 1 for i in range(len(free)))
            index = tuple(sub[free.index(i)] if i in free else mine[i] for i in range(n))
            at = pl.ds(start, count)
            buf[index + (at,)] = buf[index + (at,)] + recvs[k][sub + (at,)]
            return carry

        lax.fori_loop(0, 1 << len(free), add, 0)

    for colour in range(2):
        copy(colour, 0).start()
    for k in range(n):
        for colour in range(2):
            copy(colour, k).wait()
            accumulate(colour, k)
            if k + 1 < n:
                copy(colour, k + 1).start()
    out_ref[...] = buf[tuple(mine)]


def scatter(mesh, flat, shard_rows):
    n = len(bit_list(mesh))
    return pl.pallas_call(
        partial(scatter_kernel, mesh),
        name="reduce_scatter",
        out_shape=jax.ShapeDtypeStruct((shard_rows, LANES), F32),
        in_specs=[vmem_spec()],
        out_specs=vmem_spec(),
        scratch_shapes=[pltpu.VMEM((2,) * n + (shard_rows, LANES), F32)]
        + [pltpu.VMEM((2,) * (n - 1 - k) + (shard_rows, LANES), F32) for k in range(n)]
        + [pltpu.SemaphoreType.DMA((2, n)), pltpu.SemaphoreType.DMA((2, n))],
        compiler_params=params(collective_id=2, has_side_effects=True),
    )(flat)


def add_vector(tail, offset, value):
    row, shift = divmod(offset - TAIL_ROW * LANES, LANES)
    blocks = value.shape[0]
    lane = iota((blocks + 1, LANES), 1)
    zero = jnp.zeros((1, LANES), F32)
    here = pltpu.roll(jnp.concatenate([value, zero], 0), shift, 1) if shift else jnp.concatenate([value, zero], 0)
    back = jnp.concatenate([zero, here[:blocks]], 0)
    at = slice(row, row + blocks + 1)
    tail[at, :] = tail[at, :] + jnp.where(lane >= shift, here, back if shift else here)


def as_blocks(value, length):
    blocks = -(-length // LANES)
    v = jnp.concatenate([value[:, q * LANES : (q + 1) * LANES] for q in range(blocks)], 0)
    index = iota((blocks, LANES), 0) * LANES + iota((blocks, LANES), 1)
    return jnp.where(index < length, v, 0.0)


def stencil_bwd_kernel(
    chunks, cells, height_ref, x_ref, g_ref, gconv_ref, colh, rowh, cornh, table, wd, gain, extra, w1,
    out_ref, tail_ref, g_scr, m_scr, k_scr, e_scr, gg_scr, row_scr,
):
    step = pl.program_id(0)
    rows = x_ref.shape[1]
    width = chunks * cells
    height = height_ref[0]
    gvec = gain[2:3, :C]

    def put_column(column, v, top, low):
        hrow = iota((rows, CP), 0)
        v = jnp.where(hrow == height, low, v)
        for q in range(CB):
            lanes = slice(q * LANES, (q + 1) * LANES)
            g_scr[q, column, 1 : rows + 1, :] = v[:, lanes]
            g_scr[q, column, 0:1, :] = top[:, lanes]
            g_scr[q, column, rows + 1 : rows + 2, :] = low[:, lanes]

    @pl.when(step == 0)
    def _():
        k_scr[...] = jnp.dot(
            table[...], wd[...], preferred_element_type=F32, precision=HIGHEST
        ).reshape(k_scr.shape)
        e_scr[...] = jnp.zeros_like(e_scr)
        gg_scr[...] = jnp.zeros_like(gg_scr)
        for q in range(CB - 1, CB):
            m_scr[q] = jnp.zeros(m_scr.shape[1:], F32)
        for side in range(2):
            for i in range(REACH):
                column = i if side == 0 else width + REACH + i
                put_column(
                    column,
                    colh[side, i].astype(F32),
                    cornh[0, side].astype(F32)[i : i + 1],
                    cornh[1, side].astype(F32)[i : i + 1],
                )

    @pl.when(step < chunks)
    def _():
        row_scr[0:cells, :] = rowh[0, 0].astype(F32)
        row_scr[32 : 32 + cells, :] = rowh[0, 1].astype(F32)

        def cell(j, carry):
            put_column(
                step * cells + j + REACH,
                gconv_ref[j],
                row_scr[pl.ds(j, 1), :],
                row_scr[pl.ds(32 + j, 1), :],
            )
            center, inv = norm_parts(x_ref[j].astype(F32))
            mixed = rounded(center * inv * gvec)
            mixed = jnp.where(iota((rows, C), 0) < height, mixed, 0.0)
            for q in range(CB):
                lo, hi = q * LANES, min((q + 1) * LANES, C)
                m_scr[q, step * cells + j, :, : hi - lo] = mixed[:, lo:hi]
            return carry

        lax.fori_loop(0, cells, cell, 0)

    @pl.when(step == chunks)
    def _():
        for q in range(CB):
            lanes = slice(q * LANES, (q + 1) * LANES)
            for hb in range(rows // 8):
                at = slice(8 * hb, 8 * hb + 8)
                taps = [k_scr[t, at, lanes] for t in range(TAPS)]

                def cell(j, sums):
                    mx = m_scr[q, j, at, :]
                    sums = list(sums)
                    gm = jnp.zeros((8, LANES), F32)
                    for t in range(TAPS):
                        l, w = divmod(t, 5)
                        v = g_scr[q, j + 2 * REACH - w, 8 * hb + 2 - l : 8 * hb + 10 - l, :]
                        gm = gm + taps[t] * v
                        sums[t] = sums[t] + mx * v
                    m_scr[q, j, at, :] = gm
                    return tuple(sums)

                zero = jnp.zeros((8, LANES), F32)
                sums = lax.fori_loop(0, width, cell, (zero,) * TAPS)
                for t in range(TAPS):
                    e_scr[t, at, lanes] = sums[t]

    @pl.when(step > chunks)
    def _():
        first = (step - chunks - 1) * cells
        live = iota((rows, C), 0) < height

        def cell(j, total):
            center, inv = norm_parts(x_ref[j].astype(F32))
            normed = center * inv
            gm = jnp.concatenate([m_scr[q, first + j] for q in range(CB)], 1)[:, :C]
            gm = jnp.where(live, gm, 0.0)
            total = total + gm * normed
            v = gm * gvec
            mean = jnp.mean(v, -1, keepdims=True)
            mean_n = jnp.mean(v * normed, -1, keepdims=True)
            up = jnp.where(live, g_ref[j].astype(F32), 0.0)
            out_ref[j] = inv * (v - mean - normed * mean_n) + up
            return total

        gg_scr[:, :C] = lax.fori_loop(0, cells, cell, gg_scr[:, :C])

    @pl.when(step == 2 * chunks)
    def _():
        tail_ref[...] = jnp.zeros_like(tail_ref)
        add_vector(tail_ref, OFF_B1, as_blocks(extra[NOISE : NOISE + 1, :], FF))
        add_vector(tail_ref, OFF_B2, as_blocks(extra[NOISE + 1 : NOISE + 2, :], C))
        add_vector(tail_ref, OFF_GAIN, as_blocks(jnp.sum(gg_scr[...], 0, keepdims=True), C))
        disco = lax.dot_general(
            table[...], e_scr[...].reshape(TAPS * rows, CP), (((0,), (0,)), ((), ())),
            preferred_element_type=F32, precision=HIGHEST,
        )
        for k in range(K):
            add_vector(tail_ref, OFF_DISCO + k * C, as_blocks(disco[k : k + 1, :], C))
        ng = extra[0:NOISE, :]
        hi = ng.astype(BF16)
        mid = (ng - hi.astype(F32)).astype(BF16)
        lo = (ng - hi.astype(F32) - mid.astype(F32)).astype(BF16)
        parts = [dot(p, w1[...], ((1,), (1,))) for p in (hi, mid, lo)]
        gn = parts[0] + parts[1] + parts[2]
        for k in range(NOISE):
            add_vector(tail_ref, OFF_NOISE + k * C, as_blocks(gn[k : k + 1, :], C))


def stencil_bwd(height, x, g, gconv, colh, rowh, cornh, table, wd, small, extra, w1, tail_rows, chunks):
    width, rows, _ = x.shape
    cells = width // chunks
    first = lambda i: jnp.where(i < chunks, i, chunks - 1)
    third = lambda i: jnp.where(i <= chunks, 0, i - chunks - 1)
    both = lambda i: jnp.where(i < chunks, i, third(i))
    sd = jax.ShapeDtypeStruct
    return pl.pallas_call(
        partial(stencil_bwd_kernel, chunks, cells),
        name="stencil_bwd",
        grid=(2 * chunks + 1,),
        out_shape=(sd((width, rows, C), F32), sd((tail_rows, LANES), F32)),
        in_specs=[
            pl.BlockSpec(memory_space=pltpu.SMEM),
            pl.BlockSpec((cells, rows, C), lambda i: (both(i), 0, 0)),
            pl.BlockSpec((cells, rows, C), lambda i: (third(i), 0, 0)),
            pl.BlockSpec((cells, rows, CP), lambda i: (first(i), 0, 0)),
            vmem_spec(),
            pl.BlockSpec((1, 2, cells, CP), lambda i: (first(i), 0, 0, 0)),
        ]
        + [vmem_spec()] * 6,
        out_specs=(
            pl.BlockSpec((cells, rows, C), lambda i: (third(i), 0, 0)),
            vmem_spec(),
        ),
        scratch_shapes=[
            pltpu.VMEM((CB, width + 2 * REACH, 32, LANES), F32),
            pltpu.VMEM((CB, width, rows, LANES), F32),
            pltpu.VMEM((TAPS, rows, CP), F32),
            pltpu.VMEM((TAPS, rows, CP), F32),
            pltpu.VMEM((rows, CP), F32),
            pltpu.VMEM((64, CP), F32),
        ],
        compiler_params=params(dimension_semantics=("arbitrary",)),
    )(height, x, g, gconv, colh, rowh, cornh, table, wd, small, extra, w1)


def tail_kernel(mesh, part_ref, tail_ref, grad_ref, scale_ref, got, msg, full, place, send, recv):
    nlat, nlon = mesh.shape["lat"], mesh.shape["lon"]
    n = nlat * nlon
    lat, lon = lax.axis_index("lat"), lax.axis_index("lon")
    me = lat * nlon + lon
    piece = tail_ref.shape[1]
    shard_rows = part_ref.shape[0]
    barrier = pltpu.get_barrier_semaphore()

    def others(body):
        def step(i, carry):
            body(lax.rem(me + i, n))
            return carry

        lax.fori_loop(1, n, step, 0)

    def hello(d):
        pl.semaphore_signal(
            barrier, inc=1, device_id=(d // nlon, lax.rem(d, nlon)), device_id_type=MESH
        )

    others(hello)
    pl.semaphore_wait(barrier, n - 1)

    def scatter_piece(d):
        pltpu.make_async_remote_copy(
            src_ref=tail_ref.at[d],
            dst_ref=got.at[me],
            send_sem=send.at[0],
            recv_sem=recv.at[0],
            device_id=(d // nlon, lax.rem(d, nlon)),
            device_id_type=MESH,
        ).start()

    def wait_all(buffer, k):
        pltpu.make_async_remote_copy(
            src_ref=buffer.at[pl.ds(0, n - 1)],
            dst_ref=buffer.at[pl.ds(0, n - 1)],
            send_sem=send.at[k],
            recv_sem=recv.at[k],
            device_id=(lat, lon),
            device_id_type=MESH,
        ).wait()

    others(scatter_piece)
    got[me] = tail_ref[me]
    square = jnp.sum(part_ref[...] * part_ref[...])
    wait_all(got, 0)

    total = lax.fori_loop(
        1, n, lambda i, acc: acc + got[lax.rem(i, n)], got[0]
    )
    square = square + jnp.sum(total * total)
    msg[0:piece, :] = total
    msg[piece : piece + 1, :] = jnp.broadcast_to(square, (1, LANES))

    def share(d):
        pltpu.make_async_remote_copy(
            src_ref=msg,
            dst_ref=full.at[me],
            send_sem=send.at[1],
            recv_sem=recv.at[1],
            device_id=(d // nlon, lax.rem(d, nlon)),
            device_id_type=MESH,
        ).start()

    others(share)
    full[me] = msg[...]
    place[...] = jnp.zeros_like(place)
    wait_all(full, 1)

    def take(d, acc):
        place[pl.ds(shard_rows + d * piece, piece), :] = full[d, 0:piece, :]
        return acc + full[d, piece : piece + 1, :]

    squares = lax.fori_loop(0, n, take, jnp.zeros((1, LANES), F32))
    start = jnp.clip(me * shard_rows - TAIL_ROW + shard_rows, 0, shard_rows + n * piece)
    grad_ref[...] = part_ref[...] + place[pl.ds(start, shard_rows), :]
    scale_ref[...] = jnp.broadcast_to(jnp.sqrt(squares), scale_ref.shape)


def finish(mesh, part, tail):
    n, piece, _ = tail.shape
    shard_rows = part.shape[0]
    sd = jax.ShapeDtypeStruct
    return pl.pallas_call(
        partial(tail_kernel, mesh),
        name="small_gradients",
        out_shape=(sd(part.shape, F32), sd((8, LANES), F32)),
        in_specs=[vmem_spec()] * 2,
        out_specs=(vmem_spec(),) * 2,
        scratch_shapes=[
            pltpu.VMEM((n, piece, LANES), F32),
            pltpu.VMEM((piece + 1, LANES), F32),
            pltpu.VMEM((n, piece + 1, LANES), F32),
            pltpu.VMEM((2 * shard_rows + n * piece + 8, LANES), F32),
            pltpu.SemaphoreType.DMA((2,)),
            pltpu.SemaphoreType.DMA((2,)),
        ],
        compiler_params=params(collective_id=3, has_side_effects=True),
    )(part, tail)


def stencil_table(support_vals, support_lon):
    rows = support_vals.shape[0]
    vals = support_vals.reshape(rows, S // 3, 3, K)
    offsets = jnp.arange(-REACH, REACH + 1)
    hit = support_lon.reshape(rows, S // 3, 3)[:, :, :, None] == offsets
    picked = jnp.where(hit[:, :, :, :, None], vals[:, :, :, None, :], 0.0)
    return jnp.transpose(jnp.sum(picked, 1), (1, 2, 0, 3))


def neighbour_rows(table, height):
    count = lax.axis_size("lat")
    up = [(i, i + 1) for i in range(count - 1)]
    last = lax.dynamic_index_in_dim(table, height - 1, 2, keepdims=True)
    above = lax.ppermute(last, "lat", up)
    below = lax.ppermute(table[:, :, :1], "lat", [(j, i) for i, j in up])
    ext = jnp.concatenate([above, table, jnp.zeros_like(above)], 2)
    ext = jnp.where(jnp.arange(ext.shape[2])[None, None, :, None] == height + 1, below, ext)
    rows = table.shape[2]
    return jnp.stack([ext[l, :, 2 - l : 2 - l + rows] for l in range(3)])


def flat_table(table):
    t = table.reshape(-1, K)
    return jnp.pad(t, ((0, 0), (0, 16 - K)))


def local(
    mesh, block_in, noise, cotangent, band_heights, support_lon, support_vals,
    master, moment_one, moment_two, average, step_count,
):
    rows, width, _ = block_in.shape
    devices = mesh.shape["lat"] * mesh.shape["lon"]
    shard = master.shape[0]
    shard_rows = shard // LANES
    assert shard_rows * LANES == shard
    flat_rows = shard_rows * devices
    chunks = 6
    cells = width // chunks
    height = lax.dynamic_slice_in_dim(band_heights, lax.axis_index("lat"), 1, 0)
    x = jnp.transpose(block_in, (1, 0, 2))
    g = jnp.transpose(cotangent, (1, 0, 2))

    share = master.astype(BF16).reshape(shard_rows, LANES)
    edge = jnp.stack([x[:, 0], lax.dynamic_index_in_dim(x, height[0] - 1, 1, keepdims=False)])
    cols = jnp.stack([x[:REACH], x[width - REACH :]])
    corners = jnp.stack([edge[:, :REACH], edge[:, width - REACH :]], 1)
    edge = jnp.transpose(edge.reshape(2, chunks, cells, C), (0, 1, 2, 3))
    w1, w2, wn, wd, small, colh, rowh, cornh = gather_weights(mesh, share, cols, edge, corners)
    rowh = jnp.transpose(rowh, (1, 0, 2, 3))

    table = stencil_table(support_vals, support_lon)
    aug = jnp.concatenate(
        [
            jnp.zeros((width, rows, 1), BF16),
            jnp.transpose(noise, (2, 1, 0)),
            jnp.ones((width, rows, 1), BF16),
            jnp.zeros((width, rows, LANES - NOISE - 2), BF16),
        ],
        2,
    )
    conv = stencil_fwd(height, x, colh, rowh, cornh, flat_table(table), wd, small, aug, wn, chunks)
    out, gconv, grow, gcol, gcorn, flat, extra = mlp(
        height, conv, g, x, w1, w2, small, flat_rows, chunks
    )
    gcolh, growh, gcornh = exchange(gcol, jnp.transpose(grow, (1, 0, 2, 3)), gcorn)
    growh = jnp.transpose(growh, (1, 0, 2, 3))
    part = scatter(mesh, flat, shard_rows)
    piece = -(-(flat_rows - TAIL_ROW) // devices)
    grad_in, tail = stencil_bwd(
        height, x, g, gconv, gcolh, growh, gcornh,
        flat_table(neighbour_rows(table, height[0])), wd, small, extra, w1, devices * piece, chunks,
    )
    grad, norm = finish(mesh, part, tail.reshape(devices, piece, LANES))
    grad_part = grad.reshape(shard)
    grad_norm = norm[0, :1]
    factor = 0.01 / jnp.maximum(grad_norm, 0.01)
    clipped = grad_part * factor
    new_one = 0.9 * moment_one + 0.1 * clipped
    new_two = 0.999 * moment_two + 0.001 * clipped * clipped
    step_float = step_count[0].astype(F32)
    fix_one = 1.0 - jnp.power(jnp.float32(0.9), step_float)
    fix_two = 1.0 - jnp.power(jnp.float32(0.999), step_float)
    update = new_one / fix_one / (jnp.sqrt(new_two / fix_two) + 1e-08) + 0.1 * master
    new_master = master - 0.02 * update
    new_avg = 0.9 * average + 0.1 * new_master
    return (
        jnp.transpose(out, (1, 0, 2)),
        jnp.transpose(grad_in, (1, 0, 2)),
        grad_part,
        grad_norm,
        new_master,
        new_one,
        new_two,
        new_avg,
        new_master.astype(BF16),
    )


def solution(mesh):
    flat = P(("lat", "lon"))
    field = P("lat", "lon", None)
    return jax.shard_map(
        partial(local, mesh),
        mesh=mesh,
        in_specs=(
            field, P(None, "lat", "lon"), field, P(), P("lat", None), P("lat", None, None),
            flat, flat, flat, flat, P(),
        ),
        out_specs=(field, field, flat, P(), flat, flat, flat, flat, flat),
        check_vma=False,
    )
```

time: 918 us -> 614 us (0.67)
  Pallas kernels: 0 us -> 575 us
  matrix products: 246 us -> 0 us
  other arithmetic: 245 us -> 7.58 us
  local copies, waits for them, and re-layouts: 237 us -> 20 us
  waiting for transfers between devices: 147 us -> 0.01 us
  between operations: 20.6 us -> 4.33 us
    pallas_call x0 -> x7, Pallas kernels: none -> 575 us  [the longest x1 164 us: mlp(): pl.pallas_call(partial(mlp_kernel, blocks), name='mlp', grid=(blocks,), o...]
    dot_general x11 -> x0, matrix products: 246 us -> none  [the longest x1 70.7 us: local(): lax.dot_general(grad_hidden, w_one, (((1,), (1,)), ((), ())), preferred_e...]
    psum x1 -> x0, waiting for transfers between devices: 127 us -> none  [local(): summed = lax.psum(local_flat, ('lat', 'lon'))]
    add x4 -> x1, other arithmetic: 88.7 us -> 0.01 us  [stencil_table(): offsets = jnp.arange(-REACH, REACH + 1)]
    reshape x12 -> x0, local copies, waits for them, and re-layouts: 66 us -> none  [the longest x2 27.3 us: local(): inputs.reshape(-1, channels) + branch]
    mul x2 -> x0, other arithmetic: 54.4 us -> none  [the longest x1 54.2 us: local(): term = kernel[:, lat_tap, lon_tap][:, None, :] * grad_conv]
    concatenate x2 -> x4, local copies, waits for them, and re-layouts: 50.8 us -> 0.23 us  [the longest x3 0.16 us: local(): jnp.concatenate([jnp.zeros((width, rows, 1), BF16), jnp.transpose(noise,...]
    unnamed x162 -> x20, local copies, waits for them, and re-layouts: 48.2 us -> 1.5 us
  transfers between devices with their start and end apart: 10 -> 2, of which waited for: 4 -> 0; matrix products, arithmetic and copies ran while one was open for 21% -> 3% of each run, Pallas kernels for 0% -> 56%
where the time goes in v1:
time: 614 us; the launch traced here: 613 us
  Pallas kernels  575 us (94%)
  local copies, waits for them, and re-layouts  20 us (3%)
  other arithmetic  7.58 us (1%)
  starting transfers between devices  6.19 us (1%)
    pallas_call x1, Pallas kernels, mlp(): pl.pallas_call(partial(mlp_kernel, blocks), name='mlp', grid=(blocks,), o...  164 us
    pallas_call x1, Pallas kernels, stencil_bwd(): pl.pallas_call(partial(stencil_bwd_kernel, chunks, cells), name='stencil_...  158 us
    pallas_call x1, Pallas kernels, stencil_fwd(): pl.pallas_call(partial(stencil_fwd_kernel, chunks, cells), name='stencil_...  80.2 us
    pallas_call x1, Pallas kernels, gather_weights(): pl.pallas_call(partial(gather_kernel, mesh), name='gather_weights', out_s...  80 us
    pallas_call x1, Pallas kernels, scatter(): pl.pallas_call(partial(scatter_kernel, mesh), name='reduce_scatter', out_...  60.1 us
    pallas_call x1, Pallas kernels, exchange(): pl.pallas_call(exchange_kernel, name='exchange_edges', out_shape=(sd(cols...  17.2 us
    pallas_call x1, Pallas kernels, finish(): pl.pallas_call(partial(tail_kernel, mesh), name='small_gradients', out_sh...  14.8 us
  transfers between devices with their start and end apart: 2, of which 0 were waited for; matrix products, arithmetic and copies ran while one was open for 3% of the time, Pallas kernels for 56%

profile of v1, /device:TPU:0, one launch (start us, length us, event | category | flops | bytes accessed | tf_op | source)
XLA Modules:
  0.0 612.9 jit_solution(6387526889779967193)
XLA Ops:
  0.7 1.3 dynamic_slice.9.height_ref
  3.3 0.7 eq.30
  4.0 0.9 broadcast_in_dim.56
  4.9 0.1 broadcast_compare_fusion
  5.0 0.2 select_reduce_fusion
  5.3 0.2 dynamic-slice_reduce_fusion
  5.5 4.9 collective-permute-start.1
  10.4 1.3 collective-permute-start
  11.7 0.2 copy.68
  11.9 2.2 constant_dynamic-slice_fusion
  14.1 0.9 slice_bitcast_fusion.1
  15.0 3.4 fusion.4
  18.4 0.0 copy-start.7
  19.9 0.1 pad.18.clone
  20.0 0.1 pad.17.clone
  20.0 0.7 convert_bitcast_fusion.share_ref
  20.7 0.1 stack.38
  20.9 0.1 stack.36
  21.0 0.7 copy.69
  21.7 0.7 pad_maximum_fusion.1.cols
  22.4 0.6 pad_maximum_fusion.3.corners
  23.0 0.9 pad_maximum_fusion.rows
  23.9 80.0 %gather_weights.1 = (bf16[768,1408]{1,0:T(8,128)(2,1)}, bf16[1408,768]{1,0:T(8,128)(2,1)}, bf16[128,768]{1,0:T(8,128)(2,1)}, f32[16,768]{1,0:T(8,128)}, f32[8,14...) custom-call(bf16[405,128]{1,0:T(8,128)(2,1)} %convert_bitcast_fusion, ...), custom_call_target="tpu_custom_call" | custom-call | tf_op jit(solution)/shard_map/gather_weights/pallas_call | solution.py:327
  103.9 1.9 copy.86
  105.9 0.7 pad.7.table
  106.5 1.6 maximum_maximum_fusion.aug
  108.1 80.2 %stencil_fwd.1.conv_ref = bf16[180,24,768]{2,1,0:T(8,128)(2,1)} custom-call(s32[1]{0:T(128)} %dynamic_slice.9.height_ref, bf16[180,24,641]{2,1,0:T(8,128)(2,1)} %bitcast.53, bf16[2,2,24,641]{3,2,1,0:T(8,128)(2,1)} %get-tuple-element.31.colh, bf16[6,2,30,641]{3,2,1,0:T(8,128)(2,1)} %bitcast.61, bf16[2,2,2,641]{3,2,1,0:T(2,128)(2,1)} %get-tuple-element.33.cornh, ...), custom_call_target="tpu_custom_call" | custom-call | tf_op jit(solution)/shard_map/stencil_fwd/pallas_call | solution.py:458
  188.3 164.4 %mlp.1 = (bf16[180,24,641]{2,1,0:T(8,128)(2,1)}, f32[180,24,768]{2,1,0:T(8,128)}, bf16[6,2,30,768]{3,2,1,0:T(8,128)(2,1)}, bf16[2,2,24,768]{3,2,1,0:T(8,128)(2,1...) custom-call(s32[1]{0:T(128)} %dynamic_slice.9.height_ref, ...), custom_call_target="tpu_custom_call" | custom-call | flops 42600140800 | bytes 50000000 | tf_op jit(solution)/shard_map/mlp/pallas_call | solution.py:662
  352.7 60.1 %reduce_scatter.1.part_ref = f32[405,128]{1,0:T(8,128)} custom-call(f32[12960,128]{1,0:T(8,128)} %get-tuple-element.49.flat), custom_call_target="tpu_custom_call" | custom-call | tf_op jit(solution)/shard_map/reduce_scatter/pallas_call | solution.py:799
  412.8 0.9 copy.85
  413.7 17.2 %exchange_edges.1 = (bf16[2,2,24,768]{3,2,1,0:T(8,128)(2,1)}, bf16[2,6,30,768]{3,2,1,0:T(8,128)(2,1)}, bf16[2,2,2,768]{3,2,1,0:T(2,128)(2,1)}) custom-call(bf16[2,2,24,768]{3,2,1,0:T(8,128)(2,1)} %get-tuple-element.41.cols, bf16[2,6,30,768]{3,2,1,0:T(8,128)(2,1)} %bitcast.59, bf16[2,2,2,768]{3,2,1,0:T(2,128)(2,1)} %get-tuple-element.43.corners), custom_call_target="tpu_custom_call" | custom-call | tf_op jit(solution)/shard_map/exchange_edges/pallas_call | solution.py:724
  430.8 1.9 copy.84
  432.8 0.1 pad.14.clone
  432.8 0.0 collective-permute-done
  432.8 0.2 copy.72
  433.1 0.1 copy.73
  433.2 0.2 copy.74
  433.4 0.2 maximum_select_fusion
  433.6 0.2 fusion.5
  433.7 0.1 pad_maximum_fusion.2
  433.8 0.2 copy.76
  434.0 0.7 pad.8.table
  434.7 158.2 %stencil_bwd.1 = (f32[180,24,641]{2,1,0:T(8,128)}, f32[128,128]{1,0:T(8,128)}) custom-call(s32[1]{0:T(128)} %dynamic_slice.9.height_ref, bf16[180,24,641]{2,1,0:T(8,128)(2,1)} %bitcast.55, bf16[180,24,641]{2,1,0:T(8,128)(2,1)} %bitcast.57, f32[180,24,768]{2,1,0:T(8,128)} %get-tuple-element.40.gconv_ref, bf16[2,2,24,768]{3,2,1,0:T(8,128)(2,1)} %get-tuple-element.44.colh, ...), custom_call_target="tpu_custom_call" | custom-call | tf_op jit(solution)/shard_map/stencil_bwd/pallas_call | solution.py:964
  592.9 14.8 %small_gradients.1 = (f32[405,128]{1,0:T(8,128)}, f32[8,128]{1,0:T(8,128)}) custom-call(f32[405,128]{1,0:T(8,128)} %reduce_scatter.1.part_ref, f32[32,4,128]{2,1,0:T(4,128)} %bitcast.69), custom_call_target="tpu_custom_call" | custom-call | tf_op jit(solution)/shard_map/small_gradients/pallas_call | solution.py:1079
  607.7 1.2 slice.39
  609.6 1.8 fusion.2
  611.4 0.7 multiply_add_fusion
  612.2 0.7 copy.90
  (27 shorter events, 0.2 us)
Async XLA Ops:
  0.6 19.4 %copy-start.1 = (f32[51840]{0:T(1024)S(1)}, f32[51840]{0:T(1024)}, u32[]{:S(2)}) copy-start(f32[51840]{0:T(1024)} %param.17) | copy-start | bytes 622084
  5.5 427.7 %collective-permute-start.1 = (f32[3,5,1,9]{3,2,1,0:T(1,128)S(1)}, f32[3,5,1,9]{3,2,1,0:T(1,128)S(1)}, u32[]{:S(2)}, u32[]{:S(2)}) collective-permute-start(f32[3,5,1,9]{3,2,1,0:T(1,128)S(1)} %dynamic_slice.10), channel_id=1, source_target_pairs={{0,4},{4,8},{8,12},{12,16},{16,20},{20,24},{24,28},{1,5},{5,9},{9,... | collective-permute-start | bytes 1628 | tf_op jit(solution)/shard_map/ppermute | solution.py:1110
  10.4 422.5 %collective-permute-start = (f32[3,5,1,9]{2,3,1,0:T(8,128)S(1)}, f32[3,5,1,9]{2,3,1,0:T(8,128)S(1)}, u32[]{:S(2)}, u32[]{:S(2)}) collective-permute-start(f32[3,5,1,9]{2,3,1,0:T(8,128)S(1)} %bitcast.62), channel_id=1, source_target_pairs={{4,0},{8,4},{12,8},{16,12},{20,16},{24,20},{28,24},{5,1},{9,5},{13... | collective-permute-start | bytes 1628 | tf_op jit(solution)/shard_map/ppermute | solution.py:1111
  18.4 2.6 copy-start.7
  352.7 60.1 %copy-start.3 = (bf16[6,2,30,768]{3,2,1,0:T(8,128)(2,1)S(1)}, bf16[6,2,30,768]{3,2,1,0:T(8,128)(2,1)}, u32[]{:S(2)}) copy-start(bf16[6,2,30,768]{3,2,1,0:T(8,128)(2,1)} %get-tuple-element.42) | copy-start | bytes 1658884
  434.7 174.9 %copy-start.4 = (f32[51840]{0:T(1024)S(1)}, f32[51840]{0:T(1024)}, u32[]{:S(2)}) copy-start(f32[51840]{0:T(1024)} %param.19) | copy-start | bytes 622084
  434.7 174.9 %copy-start.5 = (f32[51840]{0:T(1024)S(1)}, f32[51840]{0:T(1024)}, u32[]{:S(2)}) copy-start(f32[51840]{0:T(1024)} %param.18) | copy-start | bytes 622084
  434.7 176.8 %copy-start.6 = (f32[51840]{0:T(1024)S(1)}, f32[51840]{0:T(1024)}, u32[]{:S(2)}) copy-start(f32[51840]{0:T(1024)} %param.20) | copy-start | bytes 622084
  607.7 4.5 copy-start.2
  611.4 1.4 copy-start

commit v2 on v1

--- a/solution.py
+++ b/solution.py
@@ -25,6 +25,8 @@
 F32 = jnp.float32
 BF16 = jnp.bfloat16
 VMEM_LIMIT = 60 * 1024 * 1024
+SLOTS = 28
+REUSE = 10
 ROW_TWO = (C * FF) // LANES
 LANE_TWO = (C * FF) % LANES
 TAIL_ROW = (2 * C * FF) // LANES
@@ -82,12 +84,13 @@
     return [order, order]
 
 
-def rotl_rows(v, unit):
+def rotl_rows(v, first, unit):
     row = iota((8, LANES), 0)
-    for b in range(3):
-        amount = unit << b
-        v = jnp.where((row >> b) & 1 == 1, pltpu.roll(v, LANES - amount, 1), v)
-    return v
+    left = lambda u, n: pltpu.roll(u, (LANES - n) % LANES, 1) if n % LANES else u
+    low = [left(v, first + unit * b) for b in range(4)]
+    odd = (row & 1) == 1
+    v = jnp.where((row & 2) == 2, jnp.where(odd, low[3], low[2]), jnp.where(odd, low[1], low[0]))
+    return jnp.where((row & 4) == 4, left(v, 4 * unit), v)
 
 
 def row_vector(flat_ref, offset, length):
@@ -111,53 +114,62 @@
     lane = iota((8, LANES), 1)
     row = iota((8, LANES), 0)
 
-    def half_one(r0, q):
-        start = 10 * r0 + q + r0 // 64
-        near = flat[pl.ds(start, 8, stride=10), :]
-        far = flat[pl.ds(start + 1, 8, stride=10), :]
-        s0 = (2 * r0) % LANES
-        v = jnp.where(lane >= s0 + 2 * row, near, far)
-        v = rotl_rows(pltpu.roll(v, (LANES - s0) % LANES, 1), 2)
-        ok = r0 + row < C
-        if q == FB - 1:
-            ok = ok & (lane < FF - (FB - 1) * LANES)
-        return jnp.where(ok, v, 0.0)
-
-    def body_one(a, carry):
-        r0 = a * 16
-        for q in range(FB):
-            v = jnp.concatenate([half_one(r0, q), half_one(r0 + 8, q)], 0)
-            w1[pl.ds(pl.multiple_of(r0, 16), 16), q * LANES : (q + 1) * LANES] = v.astype(BF16)
+    def rows_one(base, first):
+        near = [flat[pl.ds(base + q, 8, stride=10), :] for q in range(FB + 1)]
+        out = [
+            rotl_rows(jnp.where(lane >= first + 2 * row, near[q], near[q + 1]), first, 2)
+            for q in range(FB)
+        ]
+        out[-1] = jnp.where(lane < FF - (FB - 1) * LANES, out[-1], 0.0)
+        return out
+
+    def body_one(b, carry):
+        for k in range(0, 8, 2):
+            pair = [rows_one(641 * b + 80 * (k + h), 16 * (k + h)) for h in range(2)]
+            at = pl.ds(pl.multiple_of(64 * b + 8 * k, 16), 16)
+            for q in range(FB):
+                v = jnp.concatenate([pair[0][q], pair[1][q]], 0)
+                w1[at, q * LANES : (q + 1) * LANES] = v.astype(BF16)
         return carry
 
-    groups = -(-C // 16)
-    lax.fori_loop(0, groups, body_one, 0)
-    w1[groups * 16 :, :] = jnp.zeros((CP - groups * 16, FP), BF16)
-
-    def half_two(r0, q):
-        start = ROW_TWO + 5 * r0 + q + (LANE_TWO + r0) // LANES
-        v0 = flat[pl.ds(start, 8, stride=5), :]
-        v1 = flat[pl.ds(start + 1, 8, stride=5), :]
-        v2 = flat[pl.ds(start + 2, 8, stride=5), :]
-        s0 = (LANE_TWO + r0) % LANES
-        s = s0 + row
-        v = jnp.where(lane >= s, v0, jnp.where(lane >= s - LANES, v1, v2))
-        v = rotl_rows(pltpu.roll(v, (LANES - s0) % LANES, 1), 1)
-        ok = r0 + row < FF
-        if q == CB - 1:
-            ok = ok & (lane < C - (CB - 1) * LANES)
-        return jnp.where(ok, v, 0.0)
-
-    def body_two(a, carry):
-        r0 = a * 16
+    last = C - 1
+    lax.fori_loop(0, last // 64, body_one, 0)
+    zero = jnp.zeros((8, LANES), F32)
+    for q, v in enumerate(rows_one(641 * (last // 64), 0)):
+        v = jnp.concatenate([jnp.where(row == 0, v, 0.0), zero], 0)
+        w1[last : last + 16, q * LANES : (q + 1) * LANES] = v.astype(BF16)
+    w1[last + 16 :, :] = jnp.zeros((CP - last - 16, FP), BF16)
+
+    def rows_two(base, first):
+        count = CB + 2 if first + 7 >= LANES else CB + 1
+        near = [flat[pl.ds(base + q, 8, stride=5), :] for q in range(count)]
+        out = []
         for q in range(CB):
-            v = jnp.concatenate([half_two(r0, q), half_two(r0 + 8, q)], 0)
-            w2[pl.ds(pl.multiple_of(r0, 16), 16), q * LANES : (q + 1) * LANES] = v.astype(BF16)
+            v = jnp.where(lane >= first + row, near[q], near[q + 1])
+            if first + 7 >= LANES:
+                v = jnp.where(lane < first + row - LANES, near[q + 2], v)
+            out.append(rotl_rows(v, first, 1))
+        out[-1] = jnp.where(lane < C - (CB - 1) * LANES, out[-1], 0.0)
+        return out
+
+    def body_two(b, carry):
+        for k in range(0, 16, 2):
+            pair = [
+                rows_two(ROW_TWO + 641 * b + 40 * (k + h), LANE_TWO + 8 * (k + h))
+                for h in range(2)
+            ]
+            at = pl.ds(pl.multiple_of(128 * b + 8 * k, 16), 16)
+            for q in range(CB):
+                v = jnp.concatenate([pair[0][q], pair[1][q]], 0)
+                w2[at, q * LANES : (q + 1) * LANES] = v.astype(BF16)
         return carry
 
-    groups = -(-FF // 16)
-    lax.fori_loop(0, groups, body_two, 0)
-    w2[groups * 16 :, :] = jnp.zeros((FP - groups * 16, CP), BF16)
+    full = FF // LANES
+    lax.fori_loop(0, full, body_two, 0)
+    for q, v in enumerate(rows_two(ROW_TWO + 641 * full, LANE_TWO)):
+        v = jnp.concatenate([jnp.where(row < FF - full * LANES, v, 0.0), zero], 0)
+        w2[full * LANES : full * LANES + 16, q * LANES : (q + 1) * LANES] = v.astype(BF16)
+    w2[full * LANES + 16 :, :] = jnp.zeros((FP - full * LANES - 16, CP), BF16)
     small[...] = jnp.zeros_like(small)
     put_row(small, 0, row_vector(flat, OFF_B1, FF))
     put_row(small, 1, row_vector(flat, OFF_B2, C))
@@ -177,7 +189,7 @@
     return lat, lon, nlat, nlon, lax.rem(lon + 1, nlon), lax.rem(lon + nlon - 1, nlon)
 
 
-def halo_copies(cols, rows, corners, colh, rowh, cornh, send, recv):
+def halo_copies(cols, rows, corners, colh, rowh, cornh, send, recv, trow=None, trowh=None):
     lat, lon, nlat, nlon, east, west = neighbours()
     out = []
 
@@ -199,14 +211,17 @@
 
     has_up, has_down = lat > 0, lat < nlat - 1
     up, down = lat - 1, lat + 1
-    add(rows.at[0], rowh.at[1], (up, lon), 2, has_up, has_down)
-    add(rows.at[1], rowh.at[0], (down, lon), 3, has_down, has_up)
+    add(rows.at[:, 0], rowh.at[:, 1], (up, lon), 2, has_up, has_down)
+    add(rows.at[:, 1], rowh.at[:, 0], (down, lon), 3, has_down, has_up)
     add(cols.at[0], colh.at[1], (lat, west), 0, None, None)
     add(cols.at[1], colh.at[0], (lat, east), 1, None, None)
     add(corners.at[0, 0], cornh.at[1, 1], (up, west), 4, has_up, has_down)
     add(corners.at[0, 1], cornh.at[1, 0], (up, east), 5, has_up, has_down)
     add(corners.at[1, 0], cornh.at[0, 1], (down, west), 6, has_down, has_up)
     add(corners.at[1, 1], cornh.at[0, 0], (down, east), 7, has_down, has_up)
+    if trow is not None:
+        add(trow.at[0], trowh.at[1], (up, lon), 8, has_up, has_down)
+        add(trow.at[1], trowh.at[0], (down, lon), 9, has_down, has_up)
     return out
 
 
@@ -255,8 +270,8 @@
 
 
 def gather_kernel(
-    mesh, share_ref, cols, rows, corners,
-    w1, w2, wn, wd, small, colh, rowh, cornh,
+    mesh, share_ref, cols, rows, corners, trow,
+    w1, w2, wn, wd, small, colh, rowh, cornh, trowh,
     buf, flat, wnf, send, recv, hsend, hrecv, local_sem,
 ):
     bits = bit_list(mesh)
@@ -269,7 +284,7 @@
     own = pltpu.make_async_copy(share_ref, buf.at[tuple(mine)], local_sem)
     own.start()
     greet(bits, True)
-    halos = halo_copies(cols, rows, corners, colh, rowh, cornh, hsend, hrecv)
+    halos = halo_copies(cols, rows, corners, colh, rowh, cornh, hsend, hrecv, trow, trowh)
 
     def copy(colour, k):
         order = orders[colour]
@@ -302,7 +317,9 @@
 
         @pl.when(cond)
         def _(r=r):
-            rowh[r] = jnp.zeros(rowh.shape[1:], rowh.dtype)
+            for i in range(rowh.shape[0]):
+                rowh[i, r] = jnp.zeros(rowh.shape[2:], rowh.dtype)
+            trowh[r] = jnp.zeros(trowh.shape[1:], F32)
             for s in range(2):
                 cornh[r, s] = jnp.zeros(cornh.shape[2:], cornh.dtype)
 
@@ -318,7 +335,7 @@
     unpack_weights(flat, w1, w2, wn, wd, small, wnf)
 
 
-def gather_weights(mesh, share, cols, rows, corners):
+def gather_weights(mesh, share, cols, rows, corners, trow):
     bits = bit_list(mesh)
     n = len(bits)
     shard_rows = share.shape[0]
@@ -336,21 +353,22 @@
             sd(cols.shape, BF16),
             sd(rows.shape, BF16),
             sd(corners.shape, BF16),
+            sd(trow.shape, F32),
         ),
-        in_specs=[vmem_spec()] * 4,
-        out_specs=(vmem_spec(),) * 8,
+        in_specs=[vmem_spec()] * 5,
+        out_specs=(vmem_spec(),) * 9,
         scratch_shapes=[
             pltpu.VMEM((2,) * n + (shard_rows, LANES), BF16),
             pltpu.VMEM((total + 96, LANES), F32),
             pltpu.VMEM((LANES, CP), F32),
             pltpu.SemaphoreType.DMA((2, n)),
             pltpu.SemaphoreType.DMA((2, n)),
-            pltpu.SemaphoreType.DMA((8,)),
-            pltpu.SemaphoreType.DMA((8,)),
+            pltpu.SemaphoreType.DMA((10,)),
+            pltpu.SemaphoreType.DMA((10,)),
             pltpu.SemaphoreType.DMA,
         ],
         compiler_params=params(collective_id=0, has_side_effects=True),
-    )(share, cols, rows, corners)
+    )(share, cols, rows, corners, trow)
 
 
 def norm_parts(x):
@@ -366,28 +384,31 @@
 
 def stencil_fwd_kernel(
     chunks, cells, height_ref, x_ref, colh, rowh, cornh, table, wd, gain, aug, wn,
-    out_ref, m_scr, k_scr, nt_scr,
+    out_ref, mix_ref, mean_ref, inv_ref, m_scr, k_scr, nt_scr,
 ):
     step = pl.program_id(0)
     rows = x_ref.shape[1]
     width = chunks * cells
     height = height_ref[0]
-    slots = m_scr.shape[2] // (width + 2 * REACH) if m_scr.ndim == 3 else 32
     gvec = gain[2:3, :C]
 
-    def bottom_mix(j, base):
-        return base
-
-    def put_cell(column, x, top, low):
-        center, inv = norm_parts(x)
+    def put_cell(column, x, top, low, j=None):
+        mean = jnp.mean(x, -1, keepdims=True)
+        center = x - mean
+        inv = lax.rsqrt(jnp.mean(center * center, -1, keepdims=True) + 1e-05)
         mixed = rounded(center * inv * gvec)
         hrow = iota((rows, C), 0)
+        if j is not None:
+            mean_ref[j] = jnp.broadcast_to(mean, (rows, LANES))
+            inv_ref[j] = jnp.broadcast_to(inv, (rows, LANES))
+            mix_ref[j, :, :C] = jnp.where(hrow < height, mixed, 0.0).astype(BF16)
         mixed = jnp.where(hrow < height, mixed, jnp.where(hrow == height, low, 0.0))
+        at = column * SLOTS
         for g in range(CB):
             lo, hi = g * LANES, min((g + 1) * LANES, C)
-            m_scr[g, column, 1 : rows + 1, : hi - lo] = mixed[:, lo:hi]
-            m_scr[g, column, 0:1, : hi - lo] = top[:, lo:hi]
-            m_scr[g, column, rows + 1 : rows + 2, : hi - lo] = low[:, lo:hi]
+            m_scr[g, pl.ds(at + 1, rows), : hi - lo] = mixed[:, lo:hi]
+            m_scr[g, pl.ds(at, 1), : hi - lo] = top[:, lo:hi]
+            m_scr[g, pl.ds(at + rows + 1, 1), : hi - lo] = low[:, lo:hi]
 
     def halo_mix(v):
         center, inv = norm_parts(v.astype(F32))
@@ -398,7 +419,6 @@
         k_scr[...] = jnp.dot(
             table[...], wd[...], preferred_element_type=F32, precision=HIGHEST
         ).reshape(k_scr.shape)
-        lat = lax.axis_index("lat")
         for side in range(2):
             for i in range(REACH):
                 column = i if side == 0 else width + REACH + i
@@ -408,10 +428,10 @@
 
     @pl.when(step < chunks)
     def _():
-        top = halo_mix(rowh[0, 0])
-        low = halo_mix(rowh[0, 1])
-        nt_scr[0:cells, :C] = top
-        nt_scr[32 : 32 + cells, :C] = low
+        nt_scr[0:cells, :C] = halo_mix(rowh[0, 0])
+        nt_scr[32 : 32 + cells, :C] = halo_mix(rowh[0, 1])
+        lanes = slice((CB - 1) * LANES, CB * LANES)
+        mix_ref[:, :, lanes] = jnp.zeros((cells, rows, LANES), BF16)
 
         def cell(j, carry):
             put_cell(
@@ -419,10 +439,11 @@
                 x_ref[j].astype(F32),
                 nt_scr[pl.ds(j, 1), :C],
                 nt_scr[pl.ds(32 + j, 1), :C],
+                j,
             )
             return carry
 
-        lax.fori_loop(0, cells, cell, 0)
+        lax.fori_loop(0, cells, cell, 0, unroll=3)
 
     @pl.when(step >= chunks)
     def _():
@@ -434,47 +455,63 @@
         for g in range(CB):
             lanes = slice(g * LANES, (g + 1) * LANES)
             for hb in range(rows // 8):
-                taps = [k_scr[t, 8 * hb : 8 * hb + 8, lanes] for t in range(TAPS)]
-
-                def cell(j, carry):
-                    acc = nt_scr[pl.ds(j * rows + 8 * hb, 8), lanes]
-                    for t in range(TAPS):
-                        l, w = divmod(t, 5)
-                        acc = acc + taps[t] * m_scr[g, first + j + w, 8 * hb + l : 8 * hb + l + 8, :]
-                    if g == CB - 1:
-                        extra = aug[j, 8 * hb : 8 * hb + 8, :].astype(F32)
-                        acc = jnp.where(lane == 0, acc, extra)
-                    out_ref[j, 8 * hb : 8 * hb + 8, lanes] = acc.astype(BF16)
+                at = slice(8 * hb, 8 * hb + 8)
+
+                def cell(i, carry):
+                    j = i * REUSE
+                    acc = [nt_scr[pl.ds((j + u) * rows + 8 * hb, 8), lanes] for u in range(REUSE)]
+                    for l in range(3):
+                        near = [
+                            m_scr[g, pl.ds((first + j + u) * SLOTS + 8 * hb + l, 8), :]
+                            for u in range(REUSE + 2 * REACH)
+                        ]
+                        for w in range(5):
+                            tap = k_scr[5 * l + w, at, lanes]
+                            acc = [a + tap * near[u + w] for u, a in enumerate(acc)]
+                    for u in range(REUSE):
+                        v = acc[u]
+                        if g == CB - 1:
+                            v = jnp.where(lane == 0, v, aug[j + u, at, :].astype(F32))
+                        out_ref[j + u, at, lanes] = v.astype(BF16)
                     return carry
 
-                lax.fori_loop(0, cells, cell, 0, unroll=2)
+                lax.fori_loop(0, cells // REUSE, cell, 0)
 
 
 def stencil_fwd(height, x, colh, rowh, cornh, table, wd, small, aug, wn, chunks):
     width, rows, _ = x.shape
     cells = width // chunks
+    assert cells % REUSE == 0
     first = lambda i: jnp.where(i < chunks, i, chunks - 1)
     second = lambda i: jnp.where(i < chunks, 0, i - chunks)
+    sd = jax.ShapeDtypeStruct
+    by_first = lambda c: pl.BlockSpec((cells, rows, c), lambda i: (first(i), 0, 0))
+    by_second = lambda c: pl.BlockSpec((cells, rows, c), lambda i: (second(i), 0, 0))
     return pl.pallas_call(
         partial(stencil_fwd_kernel, chunks, cells),
         name="stencil_fwd",
         grid=(2 * chunks,),
-        out_shape=jax.ShapeDtypeStruct((width, rows, CP), BF16),
+        out_shape=(
+            sd((width, rows, CP), BF16),
+            sd((width, rows, CP), BF16),
+            sd((width, rows, LANES), F32),
+            sd((width, rows, LANES), F32),
+        ),
         in_specs=[
             pl.BlockSpec(memory_space=pltpu.SMEM),
-            pl.BlockSpec((cells, rows, C), lambda i: (first(i), 0, 0)),
+            by_first(C),
             vmem_spec(),
             pl.BlockSpec((1, 2, cells, C), lambda i: (first(i), 0, 0, 0)),
             vmem_spec(),
             vmem_spec(),
             vmem_spec(),
             vmem_spec(),
-            pl.BlockSpec((cells, rows, LANES), lambda i: (second(i), 0, 0)),
+            by_second(LANES),
             vmem_spec(),
         ],
-        out_specs=pl.BlockSpec((cells, rows, CP), lambda i: (second(i), 0, 0)),
+        out_specs=(by_second(CP), by_first(CP), by_first(LANES), by_first(LANES)),
         scratch_shapes=[
-            pltpu.VMEM((CB, width + 2 * REACH, 32, LANES), F32),
+            pltpu.VMEM((CB, (width + 2 * REACH) * SLOTS, LANES), F32),
             pltpu.VMEM((TAPS, rows, CP), F32),
             pltpu.VMEM((cells * rows, CP), F32),
         ],
@@ -487,76 +524,89 @@
     row = iota((8, LANES), 0)
     flat[...] = jnp.zeros_like(flat)
 
-    def turned(v, s0, unit):
-        return pltpu.roll(pltpu.roll(v, s0, 1), 0, 1, stride=unit, stride_axis=0)
-
-    def one_main(a, carry):
-        r0 = pl.multiple_of(a * 8, 8)
-        s0 = (2 * r0) % LANES
-        keep = lane >= s0 + 2 * row
+    def turned(v, first, unit):
+        return pltpu.roll(v, first, 1, stride=unit, stride_axis=0)
+
+    def main(ref, at, first, unit, out, base, step, count):
+        keep = lane >= first + unit * row
         before = jnp.zeros((8, LANES), F32)
-        for q in range(FB - 1):
-            now = turned(one[q, pl.ds(r0, 8), :], s0, 2)
-            flat[pl.ds(10 * r0 + q + r0 // 64, 8, stride=10), :] = jnp.where(keep, now, before)
+        for q in range(count):
+            now = turned(ref[q, at, :], first, unit)
+            flat[pl.ds(base + q, 8, stride=step), :] = jnp.where(keep, now, before)
             before = now
+
+    def rest(ref, at, first, unit, count, width, mask=None):
+        s = first + unit * row
+        before = turned(ref[count - 1, at, :], first, unit)
+        now = turned(ref[count, at, :], first, unit)
+        v = jnp.where(lane < s, before, jnp.where(lane < s + width, now, 0.0))
+        return v if mask is None else jnp.where(mask, v, 0.0)
+
+    shift = 8 - LANE_TWO
+    base_two = ROW_TWO - 5 * LANE_TWO
+    full = FF // LANES
+    extra = C - (CB - 1) * LANES
+
+    def two_main(b, carry):
+        for k in range(16):
+            at = pl.ds(128 * b + 8 * k + shift, 8)
+            main(two, at, 8 * k, 1, flat, base_two + 641 * b + 40 * k, 5, CB - 1)
         return carry
 
-    def one_rest(a, carry):
-        r0 = pl.multiple_of(a * 8, 8)
-        s0 = (2 * r0) % LANES
-        s = s0 + 2 * row
-        before = turned(one[FB - 2, pl.ds(r0, 8), :], s0, 2)
-        now = turned(one[FB - 1, pl.ds(r0, 8), :], s0, 2)
-        v = jnp.where(lane < s, before, jnp.where(lane < s + FF - (FB - 1) * LANES, now, 0.0))
-        at = pl.ds(10 * r0 + FB - 1 + r0 // 64, 8, stride=10)
-        flat[at, :] = flat[at, :] + v
+    lax.fori_loop(0, full, two_main, 0)
+    end = slice(128 * full + shift, 128 * full + shift + 8)
+    mask = row < FF - full * LANES + LANE_TWO
+    before = jnp.zeros((8, LANES), F32)
+    for q in range(CB - 1):
+        now = jnp.where(mask, turned(two[q, end, :], 0, 1), 0.0)
+        at = pl.ds(base_two + 641 * full + q, 8, stride=5)
+        flat[at, :] = jnp.where(lane >= row, now, before)
+        before = now
+
+    def one_main(b, carry):
+        for k in range(8):
+            at = pl.ds(pl.multiple_of(64 * b + 8 * k, 8), 8)
+            main(one, at, 16 * k, 2, flat, 641 * b + 80 * k, 10, FB - 1)
         return carry
 
-    lax.fori_loop(0, C // 8, one_main, 0)
     last = C - 1
-    assert last % 64 == 0 and C % 8 == 1
+    assert last % 64 == 0
+    lax.fori_loop(0, last // 64, one_main, 0)
+    row_last = 641 * (last // 64)
     for q in range(FB - 1):
-        at = 10 * last + q + last // 64
-        flat[at : at + 1, :] = one[q, last : last + 1, :]
-    lax.fori_loop(0, C // 8, one_rest, 0)
-
-    groups = -(-(FF + LANE_TWO) // 8)
-
-    def two_rolled(q, a):
-        v = turned(two[q, pl.ds(8 * a + 8 - LANE_TWO, 8), :], (8 * a) % LANES, 1)
-        r = 8 * a - LANE_TWO + row
-        return jnp.where((r >= 0) & (r < FF), v, 0.0)
-
-    def two_base(a):
-        return ROW_TWO + 5 * (8 * a - LANE_TWO) + a // 16
-
-    def two_main(a, carry, add=False):
-        keep = lane >= (8 * a) % LANES + row
-        before = jnp.zeros((8, LANES), F32)
-        for q in range(CB - 1):
-            now = two_rolled(q, a)
-            at = pl.ds(two_base(a) + q, 8, stride=5)
-            v = jnp.where(keep, now, before)
-            flat[at, :] = flat[at, :] + v if add else v
-            before = now
+        flat[row_last + q : row_last + q + 1, :] = one[q, last : last + 1, :]
+
+    def add_all(places, values):
+        olds = [flat[at, :] for at in places]
+        for at, old, v in zip(places, olds, values):
+            flat[at, :] = old + v
+
+    def one_rest(b, carry):
+        values = [
+            rest(one, pl.ds(pl.multiple_of(64 * b + 8 * k, 8), 8), 16 * k, 2, FB - 1, FF - (FB - 1) * LANES)
+            for k in range(8)
+        ]
+        add_all([pl.ds(641 * b + 80 * k + FB - 1, 8, stride=10) for k in range(8)], values)
         return carry
 
-    def two_rest(a, carry):
-        s = (8 * a) % LANES + row
-        before = two_rolled(CB - 2, a)
-        now = two_rolled(CB - 1, a)
-        v = jnp.where(lane < s, before, jnp.where(lane < s + C - (CB - 1) * LANES, now, 0.0))
-        at = pl.ds(two_base(a) + CB - 1, 8, stride=5)
-        flat[at, :] = flat[at, :] + v
-        return carry
-
-    lax.fori_loop(1, groups, two_main, 0)
-    two_main(0, 0, add=True)
-    at = 10 * last + FB - 1 + last // 64
+    lax.fori_loop(0, last // 64, one_rest, 0)
     lane1 = iota((1, LANES), 1)
     v = jnp.where(lane1 < FF - (FB - 1) * LANES, one[FB - 1, last : last + 1, :], 0.0)
-    flat[at : at + 1, :] = flat[at : at + 1, :] + v
-    lax.fori_loop(0, groups, two_rest, 0)
+    add_all([slice(row_last + FB - 1, row_last + FB)], [v])
+
+    def two_rest(b, carry):
+        values = [
+            rest(two, pl.ds(128 * b + 8 * k + shift, 8), 8 * k, 1, CB - 1, extra) for k in range(16)
+        ]
+        places = [pl.ds(base_two + 641 * b + 40 * k + CB - 1, 8, stride=5) for k in range(16)]
+        add_all(places, values)
+        return carry
+
+    lax.fori_loop(0, full, two_rest, 0)
+    add_all(
+        [pl.ds(base_two + 641 * full + CB - 1, 8, stride=5)],
+        [rest(two, end, 0, 1, CB - 1, extra, mask)],
+    )
 
 
 GELU_A = math.sqrt(2.0 / math.pi)
@@ -571,7 +621,7 @@
 def mlp_kernel(
     blocks, height_ref, conv_ref, g_ref, x_ref, w1, w2, small,
     out_ref, gconv_ref, rows_ref, cols_ref, corn_ref, flat_ref, extra_ref,
-    one, two, g_scr, conv_t, g_t, branch, gc,
+    one, two, g_scr, conv_t, act, gh,
 ):
     step = pl.program_id(0)
     cells, rows, _ = x_ref.shape
@@ -586,47 +636,65 @@
 
     live = (iota((1, rows, 1), 1) < height).astype(F32)
     g_scr[:, :C] = (g_ref[...].astype(F32) * live).reshape(m, C).astype(BF16)
-    conv = conv_ref[...].reshape(m, CP)
-    conv_t[...] = conv.T[: conv_t.shape[0]]
-    branch[...] = jnp.zeros_like(branch)
-    gc[...] = jnp.zeros_like(gc)
     rows_one = conv_t.shape[0]
 
-    def chunk(start, wide, tail):
+    def hidden(start, wide, tail):
         lanes = pl.ds(start, wide)
-        conv_block = conv_ref[...].reshape(m, CP)
-        g_block = g_scr[...]
-        h = dot(conv_block, w1[:, lanes]) + small[0:1, lanes]
-        ga = dot(g_block, w2[lanes, :], ((1,), (1,)))
+        h = dot(conv_ref[...].reshape(m, CP), w1[:, lanes]) + small[0:1, lanes]
+        ga = dot(g_scr[...], w2[lanes, :], ((1,), (1,)))
         h2 = h * h
         t = jnp.tanh(h * (GELU_A + (GELU_A * GELU_B) * h2))
         cdf = 0.5 * t + 0.5
-        act = (h * cdf).astype(BF16)
+        value = (h * cdf).astype(BF16)
         slope = cdf + h * (0.5 - 0.5 * (t * t)) * (GELU_A + (3 * GELU_A * GELU_B) * h2)
-        gh = (ga * slope).astype(BF16)
         if tail:
-            act = jnp.where(iota((m, wide), 1) == FF - (FB - 1) * LANES, jnp.ones_like(act), act)
-        branch[...] += dot(act, w2[lanes, :])
-        gc[...] += dot(gh, w1[:, lanes], ((1,), (1,)))
-        r1 = dot(conv_t[...], gh)
-        r2 = dot(act, g_block, ((0,), (0,)))
+            ones = iota((m, wide), 1) == FF - (FB - 1) * LANES
+            value = jnp.where(ones, jnp.ones_like(value), value)
+        act[:, lanes] = value
+        gh[:, lanes] = (ga * slope).astype(BF16)
+
+    def turn(i, count):
+        part = conv_ref[:, :, pl.ds(i * LANES, LANES)].reshape(m, LANES)
+        conv_t[pl.ds(i * LANES, count), :] = part.T[:count]
+
+    def first(f, carry):
+        turn(pl.multiple_of(f, 1), LANES)
+        hidden(pl.multiple_of(f * WIDE, WIDE), WIDE, False)
+        return carry
+
+    lax.fori_loop(0, FP // WIDE, first, 0)
+    assert FP // WIDE == CB - 1
+    turn(CB - 1, rows_one - (CB - 1) * LANES)
+    hidden(FP // WIDE * WIDE, FP % WIDE, True)
+
+    for n in range(CP // WIDE):
+        lanes = slice(n * WIDE, (n + 1) * WIDE)
+        end = min((n + 1) * WIDE, C)
+        part = slice(n * WIDE, end)
+        branch = dot(act[...], w2[:, lanes])[:, : end - n * WIDE]
+        v = x_ref[:, :, part].astype(F32).reshape(m, -1) + branch + small[1:2, part]
+        out_ref[:, :, part] = (v.reshape(cells, rows, -1) * live).astype(BF16)
+        gc = dot(gh[...], w1[lanes, :], ((1,), (1,)))
+        gconv_ref[:, :, lanes] = gc.reshape(cells, rows, WIDE)
+
+    def weights(start, wide):
+        lanes = pl.ds(start, wide)
+        r1 = dot(conv_t[...], gh[:, lanes])
+        r2 = dot(act[:, lanes], g_scr[...], ((0,), (0,)))
         for i in range(wide // LANES):
             one[start // LANES + i] += r1[:, i * LANES : (i + 1) * LANES]
         for q in range(CB):
             two[q, pl.ds(start + 8, wide), :] += r2[:, q * LANES : (q + 1) * LANES]
 
-    def body(f, carry):
-        chunk(pl.multiple_of(f * WIDE, WIDE), WIDE, False)
+    def third(f, carry):
+        weights(pl.multiple_of(f * WIDE, WIDE), WIDE)
         return carry
 
-    lax.fori_loop(0, FP // WIDE, body, 0)
-    chunk(FP // WIDE * WIDE, FP % WIDE, True)
-
-    out = x_ref[...].astype(F32).reshape(m, C) + branch[:, :C] + small[1:2, :C]
-    out_ref[...] = (out.reshape(cells, rows, C) * live).astype(BF16)
-    gconv_ref[...] = gc[...].reshape(cells, rows, CP)
+    lax.fori_loop(0, FP // WIDE, third, 0)
+    weights(FP // WIDE * WIDE, FP % WIDE)
+
     onehot = (iota((1, rows, 1), 1) == height - 1).astype(F32)
-    block = gc[...].reshape(cells, rows, CP)
+    block = gconv_ref[...]
     edges = (block[:, 0, :].astype(BF16), jnp.sum(block * onehot, 1).astype(BF16))
     for r in range(2):
         rows_ref[0, r] = edges[r]
@@ -635,8 +703,7 @@
         @pl.when(step == at)
         def _(side=side, first=first):
             for i in range(REACH):
-                base = (first + i) * rows
-                cols_ref[side, i] = gc[base : base + rows, :].astype(BF16)
+                cols_ref[side, i] = gconv_ref[first + i].astype(BF16)
             for r in range(2):
                 corn_ref[r, side] = edges[r][first : first + REACH]
 
@@ -695,9 +762,8 @@
             pltpu.VMEM((CB, FP + 16, LANES), F32),
             pltpu.VMEM((m, CP), BF16),
             pltpu.VMEM((rows_one, m), BF16),
-            pltpu.VMEM((8, LANES), BF16),
-            pltpu.VMEM((m, CP), F32),
-            pltpu.VMEM((m, CP), F32),
+            pltpu.VMEM((m, FP), BF16),
+            pltpu.VMEM((m, FP), BF16),
         ],
         compiler_params=params(dimension_semantics=("arbitrary",)),
         cost_estimate=pl.CostEstimate(flops=flops, bytes_accessed=50_000_000, transcendentals=0),
@@ -714,7 +780,8 @@
 
         @pl.when(cond)
         def _(r=r):
-            rowh[r] = jnp.zeros(rowh.shape[1:], rowh.dtype)
+            for i in range(rowh.shape[0]):
+                rowh[i, r] = jnp.zeros(rowh.shape[2:], rowh.dtype)
             for s in range(2):
                 cornh[r, s] = jnp.zeros(cornh.shape[2:], cornh.dtype)
 
@@ -828,8 +895,9 @@
 
 
 def stencil_bwd_kernel(
-    chunks, cells, height_ref, x_ref, g_ref, gconv_ref, colh, rowh, cornh, table, wd, gain, extra, w1,
-    out_ref, tail_ref, g_scr, m_scr, k_scr, e_scr, gg_scr, row_scr,
+    chunks, cells, height_ref, x_ref, mix_ref, mean_ref, inv_ref, g_ref, gconv_ref,
+    colh, rowh, cornh, table, trowh, wd, gain, extra, w1,
+    out_ref, tail_ref, g_scr, m_scr, k_scr, t_scr, e_scr, gg_scr, row_scr,
 ):
     step = pl.program_id(0)
     rows = x_ref.shape[1]
@@ -838,23 +906,31 @@
     gvec = gain[2:3, :C]
 
     def put_column(column, v, top, low):
-        hrow = iota((rows, CP), 0)
-        v = jnp.where(hrow == height, low, v)
+        v = jnp.where(iota((rows, CP), 0) == height, low, v)
+        at = column * SLOTS
         for q in range(CB):
             lanes = slice(q * LANES, (q + 1) * LANES)
-            g_scr[q, column, 1 : rows + 1, :] = v[:, lanes]
-            g_scr[q, column, 0:1, :] = top[:, lanes]
-            g_scr[q, column, rows + 1 : rows + 2, :] = low[:, lanes]
+            g_scr[q, pl.ds(at + 1, rows), :] = v[:, lanes]
+            g_scr[q, pl.ds(at, 1), :] = top[:, lanes]
+            g_scr[q, pl.ds(at + rows + 1, 1), :] = low[:, lanes]
 
     @pl.when(step == 0)
     def _():
+        hrow = iota((rows, 16), 0)
+        for t in range(TAPS):
+            l = t // 5
+            own = table[t * rows : (t + 1) * rows, :]
+            if l == 0:
+                own = jnp.concatenate([own[1:], own[:1]], 0)
+                own = jnp.where(hrow == height - 1, trowh[1, t : t + 1, :], own)
+            if l == 2:
+                own = jnp.concatenate([trowh[0, t : t + 1, :], own[: rows - 1]], 0)
+            t_scr[t * rows : (t + 1) * rows, :] = own
         k_scr[...] = jnp.dot(
-            table[...], wd[...], preferred_element_type=F32, precision=HIGHEST
+            t_scr[...], wd[...], preferred_element_type=F32, precision=HIGHEST
         ).reshape(k_scr.shape)
         e_scr[...] = jnp.zeros_like(e_scr)
         gg_scr[...] = jnp.zeros_like(gg_scr)
-        for q in range(CB - 1, CB):
-            m_scr[q] = jnp.zeros(m_scr.shape[1:], F32)
         for side in range(2):
             for i in range(REACH):
                 column = i if side == 0 else width + REACH + i
@@ -877,15 +953,12 @@
                 row_scr[pl.ds(j, 1), :],
                 row_scr[pl.ds(32 + j, 1), :],
             )
-            center, inv = norm_parts(x_ref[j].astype(F32))
-            mixed = rounded(center * inv * gvec)
-            mixed = jnp.where(iota((rows, C), 0) < height, mixed, 0.0)
+            mixed = mix_ref[j].astype(F32)
             for q in range(CB):
-                lo, hi = q * LANES, min((q + 1) * LANES, C)
-                m_scr[q, step * cells + j, :, : hi - lo] = mixed[:, lo:hi]
+                m_scr[q, step * cells + j] = mixed[:, q * LANES : (q + 1) * LANES]
             return carry
 
-        lax.fori_loop(0, cells, cell, 0)
+        lax.fori_loop(0, cells, cell, 0, unroll=2)
 
     @pl.when(step == chunks)
     def _():
@@ -893,24 +966,34 @@
             lanes = slice(q * LANES, (q + 1) * LANES)
             for hb in range(rows // 8):
                 at = slice(8 * hb, 8 * hb + 8)
-                taps = [k_scr[t, at, lanes] for t in range(TAPS)]
-
-                def cell(j, sums):
-                    mx = m_scr[q, j, at, :]
-                    sums = list(sums)
-                    gm = jnp.zeros((8, LANES), F32)
-                    for t in range(TAPS):
-                        l, w = divmod(t, 5)
-                        v = g_scr[q, j + 2 * REACH - w, 8 * hb + 2 - l : 8 * hb + 10 - l, :]
-                        gm = gm + taps[t] * v
-                        sums[t] = sums[t] + mx * v
-                    m_scr[q, j, at, :] = gm
-                    return tuple(sums)
-
-                zero = jnp.zeros((8, LANES), F32)
-                sums = lax.fori_loop(0, width, cell, (zero,) * TAPS)
-                for t in range(TAPS):
-                    e_scr[t, at, lanes] = sums[t]
+
+                def cell(i, carry):
+                    j = i * REUSE
+                    mixed = [m_scr[q, j + u, at, :] for u in range(REUSE)]
+                    total = [None] * REUSE
+                    for l in range(3):
+                        near = [
+                            g_scr[q, pl.ds((j + u) * SLOTS + 8 * hb + 2 - l, 8), :]
+                            for u in range(REUSE + 2 * REACH)
+                        ]
+                        for w in range(5):
+                            t = 5 * l + w
+                            tap = k_scr[t, at, lanes]
+                            views = near[2 * REACH - w : 2 * REACH - w + REUSE]
+                            terms = [tap * v for v in views]
+                            total = [a if b is None else a + b for a, b in zip(terms, total)]
+                            sums = [m * v for m, v in zip(mixed, views)]
+                            while len(sums) > 1:
+                                sums = [
+                                    sums[k] + sums[k + 1] if k + 1 < len(sums) else sums[k]
+                                    for k in range(0, len(sums), 2)
+                                ]
+                            e_scr[t, at, lanes] = e_scr[t, at, lanes] + sums[0]
+                    for u in range(REUSE):
+                        m_scr[q, j + u, at, :] = total[u]
+                    return carry
+
+                lax.fori_loop(0, width // REUSE, cell, 0)
 
     @pl.when(step > chunks)
     def _():
@@ -918,8 +1001,8 @@
         live = iota((rows, C), 0) < height
 
         def cell(j, total):
-            center, inv = norm_parts(x_ref[j].astype(F32))
-            normed = center * inv
+            inv = inv_ref[j][:, :1]
+            normed = (x_ref[j].astype(F32) - mean_ref[j][:, :1]) * inv
             gm = jnp.concatenate([m_scr[q, first + j] for q in range(CB)], 1)[:, :C]
             gm = jnp.where(live, gm, 0.0)
             total = total + gm * normed
@@ -930,7 +1013,7 @@
             out_ref[j] = inv * (v - mean - normed * mean_n) + up
             return total
 
-        gg_scr[:, :C] = lax.fori_loop(0, cells, cell, gg_scr[:, :C])
+        gg_scr[:, :C] = lax.fori_loop(0, cells, cell, gg_scr[:, :C], unroll=2)
 
     @pl.when(step == 2 * chunks)
     def _():
@@ -939,7 +1022,7 @@
         add_vector(tail_ref, OFF_B2, as_blocks(extra[NOISE + 1 : NOISE + 2, :], C))
         add_vector(tail_ref, OFF_GAIN, as_blocks(jnp.sum(gg_scr[...], 0, keepdims=True), C))
         disco = lax.dot_general(
-            table[...], e_scr[...].reshape(TAPS * rows, CP), (((0,), (0,)), ((), ())),
+            t_scr[...], e_scr[...].reshape(TAPS * rows, CP), (((0,), (0,)), ((), ())),
             preferred_element_type=F32, precision=HIGHEST,
         )
         for k in range(K):
@@ -954,13 +1037,17 @@
             add_vector(tail_ref, OFF_NOISE + k * C, as_blocks(gn[k : k + 1, :], C))
 
 
-def stencil_bwd(height, x, g, gconv, colh, rowh, cornh, table, wd, small, extra, w1, tail_rows, chunks):
+def stencil_bwd(
+    height, x, mixed, mean, inv, g, gconv, colh, rowh, cornh, table, trowh, wd, small, extra, w1,
+    tail_rows, chunks,
+):
     width, rows, _ = x.shape
     cells = width // chunks
     first = lambda i: jnp.where(i < chunks, i, chunks - 1)
     third = lambda i: jnp.where(i <= chunks, 0, i - chunks - 1)
-    both = lambda i: jnp.where(i < chunks, i, third(i))
     sd = jax.ShapeDtypeStruct
+    by_first = lambda c: pl.BlockSpec((cells, rows, c), lambda i: (first(i), 0, 0))
+    by_third = lambda c: pl.BlockSpec((cells, rows, c), lambda i: (third(i), 0, 0))
     return pl.pallas_call(
         partial(stencil_bwd_kernel, chunks, cells),
         name="stencil_bwd",
@@ -968,27 +1055,28 @@
         out_shape=(sd((width, rows, C), F32), sd((tail_rows, LANES), F32)),
         in_specs=[
             pl.BlockSpec(memory_space=pltpu.SMEM),
-            pl.BlockSpec((cells, rows, C), lambda i: (both(i), 0, 0)),
-            pl.BlockSpec((cells, rows, C), lambda i: (third(i), 0, 0)),
-            pl.BlockSpec((cells, rows, CP), lambda i: (first(i), 0, 0)),
+            by_third(C),
+            by_first(CP),
+            by_third(LANES),
+            by_third(LANES),
+            by_third(C),
+            by_first(CP),
             vmem_spec(),
             pl.BlockSpec((1, 2, cells, CP), lambda i: (first(i), 0, 0, 0)),
         ]
-        + [vmem_spec()] * 6,
-        out_specs=(
-            pl.BlockSpec((cells, rows, C), lambda i: (third(i), 0, 0)),
-            vmem_spec(),
-        ),
+        + [vmem_spec()] * 7,
+        out_specs=(by_third(C), vmem_spec()),
         scratch_shapes=[
-            pltpu.VMEM((CB, width + 2 * REACH, 32, LANES), F32),
+            pltpu.VMEM((CB, (width + 2 * REACH) * SLOTS, LANES), F32),
             pltpu.VMEM((CB, width, rows, LANES), F32),
             pltpu.VMEM((TAPS, rows, CP), F32),
+            pltpu.VMEM((TAPS * rows, 16), F32),
             pltpu.VMEM((TAPS, rows, CP), F32),
             pltpu.VMEM((rows, CP), F32),
             pltpu.VMEM((64, CP), F32),
         ],
         compiler_params=params(dimension_semantics=("arbitrary",)),
-    )(height, x, g, gconv, colh, rowh, cornh, table, wd, small, extra, w1)
+    )(height, x, mixed, mean, inv, g, gconv, colh, rowh, cornh, table, trowh, wd, small, extra, w1)
 
 
 def tail_kernel(mesh, part_ref, tail_ref, grad_ref, scale_ref, got, msg, full, place, send, recv):
@@ -1103,18 +1191,6 @@
     return jnp.transpose(jnp.sum(picked, 1), (1, 2, 0, 3))
 
 
-def neighbour_rows(table, height):
-    count = lax.axis_size("lat")
-    up = [(i, i + 1) for i in range(count - 1)]
-    last = lax.dynamic_index_in_dim(table, height - 1, 2, keepdims=True)
-    above = lax.ppermute(last, "lat", up)
-    below = lax.ppermute(table[:, :, :1], "lat", [(j, i) for i, j in up])
-    ext = jnp.concatenate([above, table, jnp.zeros_like(above)], 2)
-    ext = jnp.where(jnp.arange(ext.shape[2])[None, None, :, None] == height + 1, below, ext)
-    rows = table.shape[2]
-    return jnp.stack([ext[l, :, 2 - l : 2 - l + rows] for l in range(3)])
-
-
 def flat_table(table):
     t = table.reshape(-1, K)
     return jnp.pad(t, ((0, 0), (0, 16 - K)))
@@ -1136,15 +1212,19 @@
     x = jnp.transpose(block_in, (1, 0, 2))
     g = jnp.transpose(cotangent, (1, 0, 2))
 
+    table = flat_table(stencil_table(support_vals, support_lon))
+    planes = table.reshape(TAPS, rows, 16)
+    trow = jnp.stack([planes[:, 0], lax.dynamic_index_in_dim(planes, height[0] - 1, 1, keepdims=False)])
+    trow = jnp.pad(trow, ((0, 0), (0, 1), (0, 0)))
     share = master.astype(BF16).reshape(shard_rows, LANES)
-    edge = jnp.stack([x[:, 0], lax.dynamic_index_in_dim(x, height[0] - 1, 1, keepdims=False)])
+    edge = jnp.stack([x[:, 0], lax.dynamic_index_in_dim(x, height[0] - 1, 1, keepdims=False)], 1)
     cols = jnp.stack([x[:REACH], x[width - REACH :]])
-    corners = jnp.stack([edge[:, :REACH], edge[:, width - REACH :]], 1)
-    edge = jnp.transpose(edge.reshape(2, chunks, cells, C), (0, 1, 2, 3))
-    w1, w2, wn, wd, small, colh, rowh, cornh = gather_weights(mesh, share, cols, edge, corners)
-    rowh = jnp.transpose(rowh, (1, 0, 2, 3))
-
-    table = stencil_table(support_vals, support_lon)
+    corners = jnp.stack([edge[:REACH], edge[width - REACH :]], 0)
+    corners = jnp.transpose(corners, (2, 0, 1, 3))
+    edge = jnp.transpose(edge.reshape(chunks, cells, 2, C), (0, 2, 1, 3))
+    w1, w2, wn, wd, small, colh, rowh, cornh, trowh = gather_weights(
+        mesh, share, cols, edge, corners, trow
+    )
     aug = jnp.concatenate(
         [
             jnp.zeros((width, rows, 1), BF16),
@@ -1154,17 +1234,18 @@
         ],
         2,
     )
-    conv = stencil_fwd(height, x, colh, rowh, cornh, flat_table(table), wd, small, aug, wn, chunks)
+    conv, mixed, mean, inv = stencil_fwd(
+        height, x, colh, rowh, cornh, table, wd, small, aug, wn, chunks
+    )
     out, gconv, grow, gcol, gcorn, flat, extra = mlp(
         height, conv, g, x, w1, w2, small, flat_rows, chunks
     )
-    gcolh, growh, gcornh = exchange(gcol, jnp.transpose(grow, (1, 0, 2, 3)), gcorn)
-    growh = jnp.transpose(growh, (1, 0, 2, 3))
+    gcolh, growh, gcornh = exchange(gcol, grow, gcorn)
     part = scatter(mesh, flat, shard_rows)
     piece = -(-(flat_rows - TAIL_ROW) // devices)
     grad_in, tail = stencil_bwd(
-        height, x, g, gconv, gcolh, growh, gcornh,
-        flat_table(neighbour_rows(table, height[0])), wd, small, extra, w1, devices * piece, chunks,
+        height, x, mixed, mean, inv, g, gconv, gcolh, growh, gcornh, table, trowh, wd, small,
+        extra, w1, devices * piece, chunks,
     )
     grad, norm = finish(mesh, part, tail.reshape(devices, piece, LANES))
     grad_part = grad.reshape(shard)

time: 614 us -> 419 us (0.68)
  Pallas kernels: 575 us -> 392 us
  starting transfers between devices: 6.19 us -> 0 us
    pallas_call x1, Pallas kernels: 158 us -> 65.6 us  [stencil_bwd(): pl.pallas_call(partial(stencil_bwd_kernel, chunks, cells), name='stencil_...]
    pallas_call x1, Pallas kernels: 164 us -> 101 us  [mlp(): pl.pallas_call(partial(mlp_kernel, blocks), name='mlp', grid=(blocks,), o...]
    pallas_call x1, Pallas kernels: 80.2 us -> 41.7 us  [stencil_fwd(): pl.pallas_call(partial(stencil_fwd_kernel, chunks, cells), name='stencil_...]
    pallas_call x1, Pallas kernels: 80 us -> 90.9 us  [gather_weights(): pl.pallas_call(partial(gather_kernel, mesh), name='gather_weights', out_s...]
    ppermute x2 -> x0, starting transfers between devices: 6.19 us -> none  [the longest x1 4.9 us: neighbour_rows(): above = lax.ppermute(last, 'lat', up)]
  transfers between devices with their start and end apart: 2 -> 0, of which waited for: 0 -> 0; matrix products, arithmetic and copies ran while one was open for 3% -> 0% of each run, Pallas kernels for 56% -> 0%
where the time goes in v2:
time: 419 us; the launch traced here: 418 us
  Pallas kernels  392 us (94%)
  local copies, waits for them, and re-layouts  14.5 us (3%)
  other arithmetic  8.31 us (2%)
    pallas_call x1, Pallas kernels, mlp(): pl.pallas_call(partial(mlp_kernel, blocks), name='mlp', grid=(blocks,), o...  101 us
    pallas_call x1, Pallas kernels, gather_weights(): pl.pallas_call(partial(gather_kernel, mesh), name='gather_weights', out_s...  90.9 us
    pallas_call x1, Pallas kernels, stencil_bwd(): pl.pallas_call(partial(stencil_bwd_kernel, chunks, cells), name='stencil_...  65.6 us
    pallas_call x1, Pallas kernels, scatter(): pl.pallas_call(partial(scatter_kernel, mesh), name='reduce_scatter', out_...  59.6 us
    pallas_call x1, Pallas kernels, stencil_fwd(): pl.pallas_call(partial(stencil_fwd_kernel, chunks, cells), name='stencil_...  41.7 us
    pallas_call x1, Pallas kernels, exchange(): pl.pallas_call(exchange_kernel, name='exchange_edges', out_shape=(sd(cols...  17.1 us
    pallas_call x1, Pallas kernels, finish(): pl.pallas_call(partial(tail_kernel, mesh), name='small_gradients', out_sh...  15.8 us

profile of v2, /device:TPU:0, one launch (start us, length us, event | category | flops | bytes accessed | tf_op | source)
XLA Modules:
  0.0 418.5 jit_solution(628757049023018137)
XLA Ops:
  1.4 1.2 dynamic_slice.11.height_ref
  3.9 0.1 pad.13.clone
  4.0 0.1 pad.12.clone
  4.1 0.7 eq.19
  4.8 0.1 broadcast_compare_fusion
  4.9 0.9 broadcast_in_dim.34
  5.8 0.2 select_reduce_fusion
  6.1 0.2 copy.38
  6.3 0.0 copy-start
  6.3 0.6 select_maximum_fusion.trow
  6.9 1.6 convert_bitcast_fusion.share_ref
  8.5 0.9 slice_bitcast_fusion.1
  9.5 0.7 pad_maximum_fusion.cols
  10.1 3.5 dynamic-slice_bitcast_fusion
  13.6 0.1 stack.38
  13.7 0.0 copy-start.7
  13.7 3.4 fusion.4
  17.2 0.0 copy-done
  17.2 0.6 copy.41.corners
  17.8 0.1 stack.37
  17.9 0.9 maximum_bitcast_fusion.rows
  18.8 0.0 copy-done.7
  18.8 0.7 copy.42
  19.5 1.6 maximum_maximum_fusion.aug
  21.1 90.9 %gather_weights.1 = (bf16[768,1408]{1,0:T(8,128)(2,1)}, bf16[1408,768]{1,0:T(8,128)(2,1)}, bf16[128,768]{1,0:T(8,128)(2,1)}, f32[16,768]{1,0:T(8,128)}, f32[8,14...) custom-call(bf16[405,128]{1,0:T(8,128)(2,1)} %convert_bitcast_fusion, ...), custom_call_target="tpu_custom_call" | custom-call | tf_op jit(solution)/shard_map/gather_weights/pallas_call | solution.py:344
  112.0 41.7 %stencil_fwd.1 = (bf16[180,24,768]{2,1,0:T(8,128)(2,1)}, bf16[180,24,768]{2,1,0:T(8,128)(2,1)}, f32[180,24,128]{2,1,0:T(8,128)}, f32[180,24,128]{2,1,0:T(8,128)}) custom-call(s32[1]{0:T(128)} %dynamic_slice.11.height_ref, bf16[180,24,641]{2,1,0:T(8,128)(2,1)} %bitcast.48, bf16[2,2,24,641]{3,2,1,0:T(8,128)(2,1)} %get-tuple-element.36.colh, ...), custom_call_target="tpu_custom_call" | custom-call | tf_op jit(solution)/shard_map/stencil_fwd/pallas_call | solution.py:490
  153.7 101.3 %mlp.1 = (bf16[180,24,641]{2,1,0:T(8,128)(2,1)}, f32[180,24,768]{2,1,0:T(8,128)}, bf16[6,2,30,768]{3,2,1,0:T(8,128)(2,1)}, bf16[2,2,24,768]{3,2,1,0:T(8,128)(2,1...) custom-call(s32[1]{0:T(128)} %dynamic_slice.11.height_ref, ...), custom_call_target="tpu_custom_call" | custom-call | flops 42600140800 | bytes 50000000 | tf_op jit(solution)/shard_map/mlp/pallas_call | solution.py:729
  255.0 59.6 %reduce_scatter.1.part_ref = f32[405,128]{1,0:T(8,128)} custom-call(f32[12960,128]{1,0:T(8,128)} %get-tuple-element.59.flat), custom_call_target="tpu_custom_call" | custom-call | tf_op jit(solution)/shard_map/reduce_scatter/pallas_call | solution.py:866
  314.6 17.1 %exchange_edges.1 = (bf16[2,2,24,768]{3,2,1,0:T(8,128)(2,1)}, bf16[6,2,30,768]{3,2,1,0:T(8,128)(2,1)}, bf16[2,2,2,768]{3,2,1,0:T(2,128)(2,1)}) custom-call(bf16[2,2,24,768]{3,2,1,0:T(8,128)(2,1)} %get-tuple-element.50.cols, bf16[6,2,30,768]{3,2,1,0:T(8,128)(2,1)} %get-tuple-element.51.rows, bf16[2,2,2,768]{3,2,1,0:T(2,128)(2,1)} %get-tuple-element.52.corners), custom_call_target="tpu_custom_call" | custom-call | tf_op jit(solution)/shard_map/exchange_edges/pallas_call | solution.py:791
  331.8 0.0 copy-start.2
  331.8 0.0 copy-start.4
  331.8 0.0 copy-start.5
  331.8 0.0 copy-start.6
  331.8 65.6 %stencil_bwd.1 = (f32[180,24,641]{2,1,0:T(8,128)}, f32[128,128]{1,0:T(8,128)}) custom-call(s32[1]{0:T(128)} %dynamic_slice.11.height_ref, bf16[180,24,641]{2,1,0:T(8,128)(2,1)} %bitcast.50, bf16[180,24,768]{2,1,0:T(8,128)(2,1)} %get-tuple-element.46.mix_ref, f32[180,24,128]{2,1,0:T(8,128)} %get-tuple-element.47.mean_ref, ...), custom_call_target="tpu_custom_call" | custom-call | tf_op jit(solution)/shard_map/stencil_bwd/pallas_call | solution.py:1051
  397.4 15.8 %small_gradients.1 = (f32[405,128]{1,0:T(8,128)}, f32[8,128]{1,0:T(8,128)}) custom-call(f32[405,128]{1,0:T(8,128)} %reduce_scatter.1.part_ref, f32[32,4,128]{2,1,0:T(4,128)} %bitcast.60), custom_call_target="tpu_custom_call" | custom-call | tf_op jit(solution)/shard_map/small_gradients/pallas_call | solution.py:1167
  413.2 0.0 copy-start.3
  413.3 1.2 slice.27
  415.2 0.0 copy-done.2
  415.2 0.0 copy-done.4
  415.2 0.0 copy-done.5
  415.2 1.8 fusion.2
  417.0 0.0 copy-start.1
  417.0 0.0 copy-done.6
  417.0 0.7 multiply_add_fusion
  417.8 0.0 copy-done.3
  417.8 0.7 copy.50
  418.5 0.0 copy-done.1
  (11 shorter events, 0.1 us)
Async XLA Ops:
  6.3 10.9 %copy-start = (f32[360,16]{1,0:T(8,128)}, f32[360,16]{1,0:T(8,128)S(1)}, u32[]{:S(2)}) copy-start(f32[360,16]{1,0:T(8,128)S(1)} %pad.8.table) | copy-start | bytes 69124
  13.7 5.1 %copy-start.7 = (bf16[8,24,180]{2,1,0:T(8,128)(2,1)S(1)}, bf16[8,24,180]{2,1,0:T(8,128)(2,1)}, u32[]{:S(2)}) copy-start(bf16[8,24,180]{2,1,0:T(8,128)(2,1)} %param.12) | copy-start | bytes 207364
  331.8 83.4 %copy-start.2 = (f32[51840]{0:T(1024)S(1)}, f32[51840]{0:T(1024)}, u32[]{:S(2)}) copy-start(f32[51840]{0:T(1024)} %param.17) | copy-start | bytes 622084
  331.8 83.4 %copy-start.4 = (f32[51840]{0:T(1024)S(1)}, f32[51840]{0:T(1024)}, u32[]{:S(2)}) copy-start(f32[51840]{0:T(1024)} %param.19) | copy-start | bytes 622084
  331.8 83.4 %copy-start.5 = (f32[51840]{0:T(1024)S(1)}, f32[51840]{0:T(1024)}, u32[]{:S(2)}) copy-start(f32[51840]{0:T(1024)} %param.18) | copy-start | bytes 622084
  331.8 85.2 %copy-start.6 = (f32[51840]{0:T(1024)S(1)}, f32[51840]{0:T(1024)}, u32[]{:S(2)}) copy-start(f32[51840]{0:T(1024)} %param.20) | copy-start | bytes 622084
  413.2 4.5 %copy-start.3 = (f32[405,128]{1,0:T(8,128)S(1)}, f32[405,128]{1,0:T(8,128)}, u32[]{:S(2)}) copy-start(f32[405,128]{1,0:T(8,128)} %get-tuple-element.61) | copy-start | bytes 622084
  417.0 1.4 copy-start.1

commit v3 on v2

--- a/solution.py
+++ b/solution.py
@@ -84,13 +84,16 @@
     return [order, order]
 
 
+def scatter_orders(mesh):
+    n = len(bit_list(mesh))
+    if (mesh.shape["lat"], mesh.shape["lon"]) == (8, 4):
+        return [[4, 3, 2, 1, 0], [4, 2, 3, 1, 0], [4, 1, 0, 3, 2]]
+    return [list(reversed(range(n)))] * 3
+
+
 def rotl_rows(v, first, unit):
-    row = iota((8, LANES), 0)
-    left = lambda u, n: pltpu.roll(u, (LANES - n) % LANES, 1) if n % LANES else u
-    low = [left(v, first + unit * b) for b in range(4)]
-    odd = (row & 1) == 1
-    v = jnp.where((row & 2) == 2, jnp.where(odd, low[3], low[2]), jnp.where(odd, low[1], low[0]))
-    return jnp.where((row & 4) == 4, left(v, 4 * unit), v)
+    index = (iota((8, LANES), 1) + first + unit * iota((8, LANES), 0)) % LANES
+    return jnp.take_along_axis(v, index, axis=1)
 
 
 def row_vector(flat_ref, offset, length):
@@ -620,8 +623,8 @@
 
 def mlp_kernel(
     blocks, height_ref, conv_ref, g_ref, x_ref, w1, w2, small,
-    out_ref, gconv_ref, rows_ref, cols_ref, corn_ref, flat_ref, extra_ref,
-    one, two, g_scr, conv_t, act, gh,
+    out_ref, gconv_ref, rows_ref, cols_ref, corn_ref, shards_ref, extra_ref,
+    one, two, g_scr, conv_t, act, gh, flat,
 ):
     step = pl.program_id(0)
     cells, rows, _ = x_ref.shape
@@ -715,10 +718,19 @@
         for q in range(CB):
             lanes = slice(q * LANES, (q + 1) * LANES)
             extra_ref[NOISE + 1 : NOISE + 2, lanes] = two[q, FF + 8 : FF + 9, :]
-        pack_weights(one, two, flat_ref)
-
-
-def mlp(height, conv, g, x, w1, w2, small, flat_rows, blocks):
+        pack_weights(one, two, flat)
+        bits = len(shards_ref.shape) - 2
+        shard_rows = shards_ref.shape[-2]
+
+        def store(d, carry):
+            index = tuple((d >> (bits - 1 - i)) & 1 for i in range(bits))
+            shards_ref[index] = flat[pl.ds(d * shard_rows, shard_rows), :]
+            return carry
+
+        lax.fori_loop(0, 1 << bits, store, 0)
+
+
+def mlp(height, conv, g, x, w1, w2, small, shards, blocks):
     width, rows, _ = x.shape
     cells = width // blocks
     m = cells * rows
@@ -736,7 +748,7 @@
             sd((blocks, 2, cells, CP), BF16),
             sd((2, REACH, rows, CP), BF16),
             sd((2, 2, REACH, CP), BF16),
-            sd((flat_rows, LANES), F32),
+            sd(shards, F32),
             sd((16, FP), F32),
         ),
         in_specs=[
@@ -764,116 +776,11 @@
             pltpu.VMEM((rows_one, m), BF16),
             pltpu.VMEM((m, FP), BF16),
             pltpu.VMEM((m, FP), BF16),
+            pltpu.VMEM((math.prod(shards[:-1]), LANES), F32),
         ],
         compiler_params=params(dimension_semantics=("arbitrary",)),
         cost_estimate=pl.CostEstimate(flops=flops, bytes_accessed=50_000_000, transcendentals=0),
     )(height, conv, g, x, w1, w2, small)
-
-
-def exchange_kernel(cols, rows, corners, colh, rowh, cornh, send, recv):
-    greet([], True)
-    halos = halo_copies(cols, rows, corners, colh, rowh, cornh, send, recv)
-    start_halo(halos)
-    wait_halo(halos)
-    lat, _, nlat, *_ = neighbours()
-    for r, cond in ((0, lat == 0), (1, lat == nlat - 1)):
-
-        @pl.when(cond)
-        def _(r=r):
-            for i in range(rowh.shape[0]):
-                rowh[i, r] = jnp.zeros(rowh.shape[2:], rowh.dtype)
-            for s in range(2):
-                cornh[r, s] = jnp.zeros(cornh.shape[2:], cornh.dtype)
-
-
-def exchange(cols, rows, corners):
-    sd = jax.ShapeDtypeStruct
-    return pl.pallas_call(
-        exchange_kernel,
-        name="exchange_edges",
-        out_shape=(sd(cols.shape, BF16), sd(rows.shape, BF16), sd(corners.shape, BF16)),
-        in_specs=[vmem_spec()] * 3,
-        out_specs=(vmem_spec(),) * 3,
-        scratch_shapes=[pltpu.SemaphoreType.DMA((8,)), pltpu.SemaphoreType.DMA((8,))],
-        compiler_params=params(collective_id=1, has_side_effects=True),
-    )(cols, rows, corners)
-
-
-def scatter_kernel(mesh, flat, out_ref, buf, *rest):
-    bits = bit_list(mesh)
-    n = len(bits)
-    recvs, (send, recv) = rest[:n], rest[n:]
-    orders = [order[::-1] for order in stage_orders(mesh)]
-    mine = my_bits(bits)
-    shard_rows = out_ref.shape[0]
-    cut = (shard_rows // 2 + 7) // 8 * 8
-    spans = [(0, cut), (cut, shard_rows - cut)]
-
-    def shard_index(d):
-        return tuple((d >> (n - 1 - i)) & 1 for i in range(n))
-
-    def fill(d, carry):
-        buf[shard_index(d)] = flat[pl.ds(d * shard_rows, shard_rows), :]
-        return carry
-
-    lax.fori_loop(0, 1 << n, fill, 0)
-    greet(bits, False)
-
-    def copy(colour, k):
-        order = orders[colour]
-        done, now = order[:k], order[k]
-        start, count = spans[colour]
-        index = tuple(
-            1 - mine[i] if i == now else mine[i] if i in done else slice(None) for i in range(n)
-        )
-        at = pl.ds(start, count)
-        return pltpu.make_async_remote_copy(
-            src_ref=buf.at[index + (at,)],
-            dst_ref=recvs[k].at[(slice(None),) * (n - 1 - k) + (at,)],
-            send_sem=send.at[colour, k],
-            recv_sem=recv.at[colour, k],
-            device_id=partner(*bits[now]),
-            device_id_type=MESH,
-        )
-
-    def accumulate(colour, k):
-        order = orders[colour]
-        start, count = spans[colour]
-        free = [i for i in range(n) if i not in order[: k + 1]]
-
-        def add(d, carry):
-            sub = tuple((d >> (len(free) - 1 - i)) & 1 for i in range(len(free)))
-            index = tuple(sub[free.index(i)] if i in free else mine[i] for i in range(n))
-            at = pl.ds(start, count)
-            buf[index + (at,)] = buf[index + (at,)] + recvs[k][sub + (at,)]
-            return carry
-
-        lax.fori_loop(0, 1 << len(free), add, 0)
-
-    for colour in range(2):
-        copy(colour, 0).start()
-    for k in range(n):
-        for colour in range(2):
-            copy(colour, k).wait()
-            accumulate(colour, k)
-            if k + 1 < n:
-                copy(colour, k + 1).start()
-    out_ref[...] = buf[tuple(mine)]
-
-
-def scatter(mesh, flat, shard_rows):
-    n = len(bit_list(mesh))
-    return pl.pallas_call(
-        partial(scatter_kernel, mesh),
-        name="reduce_scatter",
-        out_shape=jax.ShapeDtypeStruct((shard_rows, LANES), F32),
-        in_specs=[vmem_spec()],
-        out_specs=vmem_spec(),
-        scratch_shapes=[pltpu.VMEM((2,) * n + (shard_rows, LANES), F32)]
-        + [pltpu.VMEM((2,) * (n - 1 - k) + (shard_rows, LANES), F32) for k in range(n)]
-        + [pltpu.SemaphoreType.DMA((2, n)), pltpu.SemaphoreType.DMA((2, n))],
-        compiler_params=params(collective_id=2, has_side_effects=True),
-    )(flat)
 
 
 def add_vector(tail, offset, value):
@@ -894,28 +801,96 @@
     return jnp.where(index < length, v, 0.0)
 
 
+class Scatter:
+    def __init__(self, mesh, shards, buf, recvs, send, recv):
+        self.bits = bit_list(mesh)
+        self.n = len(self.bits)
+        self.orders = scatter_orders(mesh)
+        self.first = self.orders[0][0]
+        assert all(order[0] == self.first for order in self.orders)
+        self.mine = my_bits(self.bits)
+        self.shards, self.buf, self.recvs = shards, buf, recvs
+        self.send, self.recv = send, recv
+        rows = shards.shape[-2]
+        one, two = (int(rows * f) // 8 * 8 for f in (0.36, 0.71))
+        self.spans = [(0, one), (one, two - one), (two, rows - two)]
+
+    def copy(self, colour, k):
+        order, mine, n = self.orders[colour], self.mine, self.n
+        done, now = order[:k], order[k]
+        at = (pl.ds(*self.spans[colour]),)
+        index = tuple(
+            1 - mine[i] if i == now else mine[i] if i in done else slice(None) for i in range(n)
+        )
+        if k == 0:
+            src = self.shards.at[index + at]
+        else:
+            src = self.buf.at[tuple(v for i, v in enumerate(index) if i != self.first) + at]
+        return pltpu.make_async_remote_copy(
+            src_ref=src,
+            dst_ref=self.recvs[k].at[(slice(None),) * (n - 1 - k) + at],
+            send_sem=self.send.at[colour, k],
+            recv_sem=self.recv.at[colour, k],
+            device_id=partner(*self.bits[now]),
+            device_id_type=MESH,
+        )
+
+    def load(self, sem):
+        index = tuple(self.mine[i] if i == self.first else slice(None) for i in range(self.n))
+        return pltpu.make_async_copy(self.shards.at[index], self.buf, sem)
+
+    def advance(self, colour, k):
+        self.copy(colour, k).wait()
+        order, n = self.orders[colour], self.n
+        free = [i for i in range(n) if i not in order[: k + 1]]
+        at = (pl.ds(*self.spans[colour]),)
+
+        def add(d, carry):
+            sub = tuple((d >> (len(free) - 1 - i)) & 1 for i in range(len(free)))
+            index = tuple(
+                sub[free.index(i)] if i in free else self.mine[i]
+                for i in range(n)
+                if i != self.first
+            )
+            self.buf[index + at] = self.buf[index + at] + self.recvs[k][sub + at]
+            return carry
+
+        lax.fori_loop(0, 1 << len(free), add, 0)
+        if k + 1 < n:
+            self.copy(colour, k + 1).start()
+
+    def result(self):
+        return self.buf[tuple(v for i, v in enumerate(self.mine) if i != self.first)]
+
+
+def scatter_plan(n):
+    if n == 5:
+        return {8: [(0, 1), (1, 1), (2, 1)], 13: [(0, 2), (1, 2)], 15: [(2, 2)], 17: [(0, 3), (1, 3), (2, 3)]}
+    return {}
+
+
 def stencil_bwd_kernel(
-    chunks, cells, height_ref, x_ref, mix_ref, mean_ref, inv_ref, g_ref, gconv_ref,
-    colh, rowh, cornh, table, trowh, wd, gain, extra, w1,
-    out_ref, tail_ref, g_scr, m_scr, k_scr, t_scr, e_scr, gg_scr, row_scr,
+    mesh, chunks, cells, height_ref, mix_ref, gconv_ref,
+    cols, edge, corners, table, trowh, wd, extra, w1, shards,
+    tail_ref, part_ref, gm_ref,
+    g_scr, m_scr, k_scr, t_scr, e_scr, colh, rowh, cornh, buf, *rest,
 ):
+    n = len(bit_list(mesh))
+    recvs, (send, recv, hsend, hrecv, load_sem, out_sem) = rest[:n], rest[n:]
+    scatter = Scatter(mesh, shards, buf, recvs, send, recv)
     step = pl.program_id(0)
-    rows = x_ref.shape[1]
+    rows = mix_ref.shape[1]
     width = chunks * cells
     height = height_ref[0]
-    gvec = gain[2:3, :C]
-
-    def put_column(column, v, top, low):
-        v = jnp.where(iota((rows, CP), 0) == height, low, v)
-        at = column * SLOTS
-        for q in range(CB):
-            lanes = slice(q * LANES, (q + 1) * LANES)
-            g_scr[q, pl.ds(at + 1, rows), :] = v[:, lanes]
-            g_scr[q, pl.ds(at, 1), :] = top[:, lanes]
-            g_scr[q, pl.ds(at + rows + 1, 1), :] = low[:, lanes]
+    plan = scatter_plan(n)
 
     @pl.when(step == 0)
     def _():
+        scatter.load(load_sem).start()
+        greet(scatter.bits, True)
+        start_halo(halo_copies(cols, edge, corners, colh, rowh, cornh, hsend, hrecv))
+        for colour in range(3):
+            scatter.copy(colour, 0).start()
         hrow = iota((rows, 16), 0)
         for t in range(TAPS):
             l = t // 5
@@ -930,38 +905,57 @@
             t_scr[...], wd[...], preferred_element_type=F32, precision=HIGHEST
         ).reshape(k_scr.shape)
         e_scr[...] = jnp.zeros_like(e_scr)
-        gg_scr[...] = jnp.zeros_like(gg_scr)
+
+    @pl.when(step < chunks)
+    def _():
+        def cell(j, carry):
+            v = gconv_ref[j]
+            mixed = mix_ref[j].astype(F32)
+            at = (step * cells + j + REACH) * SLOTS
+            for q in range(CB):
+                lanes = slice(q * LANES, (q + 1) * LANES)
+                g_scr[q, pl.ds(at + 1, rows), :] = v[:, lanes]
+                m_scr[q, step * cells + j] = mixed[:, lanes]
+            return carry
+
+        lax.fori_loop(0, cells, cell, 0, unroll=2)
+
+    @pl.when(step == chunks)
+    def _():
+        scatter.load(load_sem).wait()
+        for colour in range(3):
+            scatter.advance(colour, 0)
+        wait_halo(halo_copies(cols, edge, corners, colh, rowh, cornh, hsend, hrecv))
+        lat, _, nlat, *_ = neighbours()
+        keep = ((lat > 0).astype(F32), (lat < nlat - 1).astype(F32))
+
+        def put(column, top, low, fresh=None):
+            at = column * SLOTS
+            here = iota((rows, LANES), 0) == height
+            for q in range(CB):
+                lanes = slice(q * LANES, (q + 1) * LANES)
+                body = pl.ds(at + 1, rows)
+                old = g_scr[q, body, :] if fresh is None else fresh[:, lanes]
+                g_scr[q, body, :] = jnp.where(here, low[:, lanes], old)
+                g_scr[q, pl.ds(at, 1), :] = top[:, lanes]
+                g_scr[q, pl.ds(at + rows + 1, 1), :] = low[:, lanes]
+
+        def beside(ref):
+            return [jnp.where(keep[r] > 0, ref(r).astype(F32), 0.0) for r in range(2)]
+
         for side in range(2):
+            top, low = beside(lambda r: cornh[r, side])
             for i in range(REACH):
                 column = i if side == 0 else width + REACH + i
-                put_column(
-                    column,
-                    colh[side, i].astype(F32),
-                    cornh[0, side].astype(F32)[i : i + 1],
-                    cornh[1, side].astype(F32)[i : i + 1],
-                )
-
-    @pl.when(step < chunks)
-    def _():
-        row_scr[0:cells, :] = rowh[0, 0].astype(F32)
-        row_scr[32 : 32 + cells, :] = rowh[0, 1].astype(F32)
-
-        def cell(j, carry):
-            put_column(
-                step * cells + j + REACH,
-                gconv_ref[j],
-                row_scr[pl.ds(j, 1), :],
-                row_scr[pl.ds(32 + j, 1), :],
-            )
-            mixed = mix_ref[j].astype(F32)
-            for q in range(CB):
-                m_scr[q, step * cells + j] = mixed[:, q * LANES : (q + 1) * LANES]
+                put(column, top[i : i + 1], low[i : i + 1], colh[side, i].astype(F32))
+
+        def strip(c, carry):
+            tops, lows = beside(lambda r: rowh[c, r])
+            for i in range(cells):
+                put(c * cells + i + REACH, tops[i : i + 1], lows[i : i + 1])
             return carry
 
-        lax.fori_loop(0, cells, cell, 0, unroll=2)
-
-    @pl.when(step == chunks)
-    def _():
+        lax.fori_loop(0, chunks, strip, 0)
         for q in range(CB):
             lanes = slice(q * LANES, (q + 1) * LANES)
             for hb in range(rows // 8):
@@ -994,33 +988,13 @@
                     return carry
 
                 lax.fori_loop(0, width // REUSE, cell, 0)
-
-    @pl.when(step > chunks)
-    def _():
-        first = (step - chunks - 1) * cells
-        live = iota((rows, C), 0) < height
-
-        def cell(j, total):
-            inv = inv_ref[j][:, :1]
-            normed = (x_ref[j].astype(F32) - mean_ref[j][:, :1]) * inv
-            gm = jnp.concatenate([m_scr[q, first + j] for q in range(CB)], 1)[:, :C]
-            gm = jnp.where(live, gm, 0.0)
-            total = total + gm * normed
-            v = gm * gvec
-            mean = jnp.mean(v, -1, keepdims=True)
-            mean_n = jnp.mean(v * normed, -1, keepdims=True)
-            up = jnp.where(live, g_ref[j].astype(F32), 0.0)
-            out_ref[j] = inv * (v - mean - normed * mean_n) + up
-            return total
-
-        gg_scr[:, :C] = lax.fori_loop(0, cells, cell, gg_scr[:, :C], unroll=2)
-
-    @pl.when(step == 2 * chunks)
-    def _():
+                for colour, k in plan.get(q * (rows // 8) + hb, []):
+                    scatter.advance(colour, k)
+            pltpu.make_async_copy(m_scr.at[q], gm_ref.at[q], out_sem.at[q]).start()
+
         tail_ref[...] = jnp.zeros_like(tail_ref)
         add_vector(tail_ref, OFF_B1, as_blocks(extra[NOISE : NOISE + 1, :], FF))
         add_vector(tail_ref, OFF_B2, as_blocks(extra[NOISE + 1 : NOISE + 2, :], C))
-        add_vector(tail_ref, OFF_GAIN, as_blocks(jnp.sum(gg_scr[...], 0, keepdims=True), C))
         disco = lax.dot_general(
             t_scr[...], e_scr[...].reshape(TAPS * rows, CP), (((0,), (0,)), ((), ())),
             preferred_element_type=F32, precision=HIGHEST,
@@ -1035,48 +1009,123 @@
         gn = parts[0] + parts[1] + parts[2]
         for k in range(NOISE):
             add_vector(tail_ref, OFF_NOISE + k * C, as_blocks(gn[k : k + 1, :], C))
+        taken = {e for events in plan.values() for e in events}
+        for k in range(1, n):
+            for colour in range(3):
+                if (colour, k) not in taken:
+                    scatter.advance(colour, k)
+        part_ref[...] = scatter.result()
+        for q in range(CB):
+            pltpu.make_async_copy(m_scr.at[q], gm_ref.at[q], out_sem.at[q]).wait()
 
 
 def stencil_bwd(
-    height, x, mixed, mean, inv, g, gconv, colh, rowh, cornh, table, trowh, wd, small, extra, w1,
+    mesh, height, mixed, gconv, cols, edge, corners, table, trowh, wd, extra, w1, shards,
     tail_rows, chunks,
 ):
-    width, rows, _ = x.shape
+    width, rows, _ = mixed.shape
     cells = width // chunks
+    shard_rows = shards.shape[-2]
+    n = len(bit_list(mesh))
     first = lambda i: jnp.where(i < chunks, i, chunks - 1)
-    third = lambda i: jnp.where(i <= chunks, 0, i - chunks - 1)
     sd = jax.ShapeDtypeStruct
     by_first = lambda c: pl.BlockSpec((cells, rows, c), lambda i: (first(i), 0, 0))
-    by_third = lambda c: pl.BlockSpec((cells, rows, c), lambda i: (third(i), 0, 0))
     return pl.pallas_call(
-        partial(stencil_bwd_kernel, chunks, cells),
+        partial(stencil_bwd_kernel, mesh, chunks, cells),
         name="stencil_bwd",
-        grid=(2 * chunks + 1,),
-        out_shape=(sd((width, rows, C), F32), sd((tail_rows, LANES), F32)),
-        in_specs=[
-            pl.BlockSpec(memory_space=pltpu.SMEM),
-            by_third(C),
-            by_first(CP),
-            by_third(LANES),
-            by_third(LANES),
-            by_third(C),
-            by_first(CP),
-            vmem_spec(),
-            pl.BlockSpec((1, 2, cells, CP), lambda i: (first(i), 0, 0, 0)),
-        ]
-        + [vmem_spec()] * 7,
-        out_specs=(by_third(C), vmem_spec()),
+        grid=(chunks + 1,),
+        out_shape=(
+            sd((tail_rows, LANES), F32),
+            sd((shard_rows, LANES), F32),
+            sd((CB, width, rows, LANES), F32),
+        ),
+        in_specs=[pl.BlockSpec(memory_space=pltpu.SMEM), by_first(CP), by_first(CP)]
+        + [vmem_spec()] * 8
+        + [any_spec()],
+        out_specs=(vmem_spec(), vmem_spec(), any_spec()),
         scratch_shapes=[
             pltpu.VMEM((CB, (width + 2 * REACH) * SLOTS, LANES), F32),
             pltpu.VMEM((CB, width, rows, LANES), F32),
             pltpu.VMEM((TAPS, rows, CP), F32),
             pltpu.VMEM((TAPS * rows, 16), F32),
             pltpu.VMEM((TAPS, rows, CP), F32),
-            pltpu.VMEM((rows, CP), F32),
-            pltpu.VMEM((64, CP), F32),
+            pltpu.VMEM(cols.shape, BF16),
+            pltpu.VMEM(edge.shape, BF16),
+            pltpu.VMEM(corners.shape, BF16),
+            pltpu.VMEM((2,) * (n - 1) + (shard_rows, LANES), F32),
+        ]
+        + [pltpu.VMEM((2,) * (n - 1 - k) + (shard_rows, LANES), F32) for k in range(n)]
+        + [
+            pltpu.SemaphoreType.DMA((3, n)),
+            pltpu.SemaphoreType.DMA((3, n)),
+            pltpu.SemaphoreType.DMA((8,)),
+            pltpu.SemaphoreType.DMA((8,)),
+            pltpu.SemaphoreType.DMA,
+            pltpu.SemaphoreType.DMA((CB,)),
         ],
+        compiler_params=params(
+            dimension_semantics=("arbitrary",), collective_id=1, has_side_effects=True
+        ),
+    )(height, mixed, gconv, cols, edge, corners, table, trowh, wd, extra, w1, shards)
+
+
+def norm_bwd_kernel(
+    height_ref, gm_ref, x_ref, mean_ref, inv_ref, g_ref, gain, tail_in, out_ref, tail_ref, gg_scr
+):
+    step = pl.program_id(0)
+    cells, rows, _ = x_ref.shape
+    gvec = gain[2:3, :C]
+    live = iota((rows, C), 0) < height_ref[0]
+
+    @pl.when(step == 0)
+    def _():
+        gg_scr[...] = jnp.zeros_like(gg_scr)
+
+    def cell(j, total):
+        inv = inv_ref[j][:, :1]
+        normed = (x_ref[j].astype(F32) - mean_ref[j][:, :1]) * inv
+        gm = jnp.concatenate([gm_ref[q, j] for q in range(CB)], 1)[:, :C]
+        gm = jnp.where(live, gm, 0.0)
+        total = total + gm * normed
+        v = gm * gvec
+        mean = jnp.mean(v, -1, keepdims=True)
+        mean_n = jnp.mean(v * normed, -1, keepdims=True)
+        up = jnp.where(live, g_ref[j].astype(F32), 0.0)
+        out_ref[j] = inv * (v - mean - normed * mean_n) + up
+        return total
+
+    gg_scr[:, :C] = lax.fori_loop(0, cells, cell, gg_scr[:, :C], unroll=2)
+
+    @pl.when(step == pl.num_programs(0) - 1)
+    def _():
+        tail_ref[...] = tail_in[...]
+        add_vector(tail_ref, OFF_GAIN, as_blocks(jnp.sum(gg_scr[...], 0, keepdims=True), C))
+
+
+def norm_bwd(height, gm, x, mean, inv, g, small, tail, chunks):
+    width, rows, _ = x.shape
+    cells = width // chunks
+    sd = jax.ShapeDtypeStruct
+    block = lambda c: pl.BlockSpec((cells, rows, c), lambda i: (i, 0, 0))
+    return pl.pallas_call(
+        norm_bwd_kernel,
+        name="norm_bwd",
+        grid=(chunks,),
+        out_shape=(sd((width, rows, C), F32), sd(tail.shape, F32)),
+        in_specs=[
+            pl.BlockSpec(memory_space=pltpu.SMEM),
+            pl.BlockSpec((CB, cells, rows, LANES), lambda i: (0, i, 0, 0)),
+            block(C),
+            block(LANES),
+            block(LANES),
+            block(C),
+            vmem_spec(),
+            vmem_spec(),
+        ],
+        out_specs=(block(C), vmem_spec()),
+        scratch_shapes=[pltpu.VMEM((rows, CP), F32)],
         compiler_params=params(dimension_semantics=("arbitrary",)),
-    )(height, x, mixed, mean, inv, g, gconv, colh, rowh, cornh, table, trowh, wd, small, extra, w1)
+    )(height, gm, x, mean, inv, g, small, tail)
 
 
 def tail_kernel(mesh, part_ref, tail_ref, grad_ref, scale_ref, got, msg, full, place, send, recv):
@@ -1237,16 +1286,16 @@
     conv, mixed, mean, inv = stencil_fwd(
         height, x, colh, rowh, cornh, table, wd, small, aug, wn, chunks
     )
-    out, gconv, grow, gcol, gcorn, flat, extra = mlp(
-        height, conv, g, x, w1, w2, small, flat_rows, chunks
+    shards = (2,) * len(bit_list(mesh)) + (shard_rows, LANES)
+    out, gconv, grow, gcol, gcorn, packed, extra = mlp(
+        height, conv, g, x, w1, w2, small, shards, chunks
     )
-    gcolh, growh, gcornh = exchange(gcol, grow, gcorn)
-    part = scatter(mesh, flat, shard_rows)
     piece = -(-(flat_rows - TAIL_ROW) // devices)
-    grad_in, tail = stencil_bwd(
-        height, x, mixed, mean, inv, g, gconv, gcolh, growh, gcornh, table, trowh, wd, small,
-        extra, w1, devices * piece, chunks,
+    tail, part, gm = stencil_bwd(
+        mesh, height, mixed, gconv, gcol, grow, gcorn, table, trowh, wd, extra, w1, packed,
+        devices * piece, chunks,
     )
+    grad_in, tail = norm_bwd(height, gm, x, mean, inv, g, small, tail, chunks)
     grad, norm = finish(mesh, part, tail.reshape(devices, piece, LANES))
     grad_part = grad.reshape(shard)
     grad_norm = norm[0, :1]

time: 419 us -> 318 us (0.76)
  Pallas kernels: 392 us -> 293 us
    pallas_call x3 -> x2, Pallas kernels: 142 us -> 87.2 us  [the longest x1 63.9 us: stencil_bwd(): pl.pallas_call(partial(stencil_bwd_kernel, mesh, chunks, cells), name='st...]
    pallas_call x1, Pallas kernels: 90.9 us -> 46.3 us  [gather_weights(): pl.pallas_call(partial(gather_kernel, mesh), name='gather_weights', out_s...]
where the time goes in v3:
time: 318 us
  Pallas kernels  293 us (92%)
  local copies, waits for them, and re-layouts  12.9 us (4%)
  other arithmetic  8.3 us (3%)
  between operations  3.63 us (1%)
    pallas_call x1, Pallas kernels, mlp(): pl.pallas_call(partial(mlp_kernel, blocks), name='mlp', grid=(blocks,), o...  102 us
    pallas_call x1, Pallas kernels, stencil_bwd(): pl.pallas_call(partial(stencil_bwd_kernel, mesh, chunks, cells), name='st...  63.9 us
    pallas_call x1, Pallas kernels, gather_weights(): pl.pallas_call(partial(gather_kernel, mesh), name='gather_weights', out_s...  46.3 us
    pallas_call x1, Pallas kernels, stencil_fwd(): pl.pallas_call(partial(stencil_fwd_kernel, chunks, cells), name='stencil_...  41.7 us
    pallas_call x1, Pallas kernels, norm_bwd(): pl.pallas_call(norm_bwd_kernel, name='norm_bwd', grid=(chunks,), out_shap...  23.3 us
    pallas_call x1, Pallas kernels, finish(): pl.pallas_call(partial(tail_kernel, mesh), name='small_gradients', out_sh...  15.9 us

profile of v3, /device:TPU:0, one launch (start us, length us, event | category | flops | bytes accessed | tf_op | source)
XLA Modules:
  0.0 317.9 jit_solution(17560261151923682938)
XLA Ops:
  0.6 1.2 dynamic_slice.11.height_ref
  1.9 1.6 convert_bitcast_fusion.share_ref
  3.5 0.9 slice_bitcast_fusion.1
  4.4 0.7 pad_maximum_fusion.cols
  6.4 3.5 %dynamic-slice_bitcast_fusion = (bf16[180,1,641]{2,1,0:T(2,128)(2,1)S(1)}, bf16[180,641]{1,0:T(8,128)(2,1)S(1)}) fusion(bf16[24,180,641]{2,0,1:T(8,128)(2,1)} %param.11, s32[]{:T(128)S(6)} %select_n.14), kind=kLoop, calls=%fused_computation.3 | loop fusion | bytes 692284 | tf_op jit(solution)/shard_map/jit(dynamic_index_in_dim)/dynamic_slice | solution.py:1269
  9.9 0.1 stack.38
  10.0 0.0 copy-start.8
  10.0 0.0 copy-start.9
  10.0 3.4 %fusion.4 = (bf16[180,1,641]{2,1,0:T(2,128)(2,1)S(1)}, bf16[180,641]{1,0:T(8,128)(2,1)S(1)}) fusion(bf16[180,24,641]{2,1,0:T(8,128)(2,1)} %bitcast.47), kind=kLoop, calls=%fused_computation.26 | loop fusion | bytes 692280 | tf_op jit(solution)/shard_map/slice | solution.py:1269
  13.4 0.1 stack.37
  13.5 0.0 copy-start.7
  13.5 0.9 maximum_bitcast_fusion.rows
  14.4 0.6 copy.41.corners
  15.1 0.0 copy-done.8
  15.1 0.0 copy-done.9
  15.2 0.1 broadcast_compare_fusion
  15.2 0.2 select_reduce_fusion
  15.5 0.2 copy.38
  15.7 0.0 copy-start
  15.7 0.6 select_maximum_fusion.trow
  16.4 46.3 %gather_weights.1 = (bf16[768,1408]{1,0:T(8,128)(2,1)}, bf16[1408,768]{1,0:T(8,128)(2,1)}, bf16[128,768]{1,0:T(8,128)(2,1)}, f32[16,768]{1,0:T(8,128)}, f32[8,14...) custom-call(bf16[405,128]{1,0:T(8,128)(2,1)} %convert_bitcast_fusion, ...), custom_call_target="tpu_custom_call" | custom-call | tf_op jit(solution)/shard_map/gather_weights/pallas_call | solution.py:347
  62.6 0.0 copy-done.7
  62.6 0.7 copy.42
  63.4 0.1 pad.13.clone
  63.4 0.1 pad.12.clone
  63.5 1.6 maximum_maximum_fusion.aug
  65.1 0.0 copy-done
  65.1 41.7 %stencil_fwd.1 = (bf16[180,24,768]{2,1,0:T(8,128)(2,1)}, bf16[180,24,768]{2,1,0:T(8,128)(2,1)}, f32[180,24,128]{2,1,0:T(8,128)}, f32[180,24,128]{2,1,0:T(8,128)}) custom-call(s32[1]{0:T(128)} %dynamic_slice.11.height_ref, bf16[180,24,641]{2,1,0:T(8,128)(2,1)} %bitcast.48, bf16[2,2,24,641]{3,2,1,0:T(8,128)(2,1)} %get-tuple-element.36.colh, ...), custom_call_target="tpu_custom_call" | custom-call | tf_op jit(solution)/shard_map/stencil_fwd/pallas_call | solution.py:493
  106.8 102.0 %mlp.1 = (bf16[180,24,641]{2,1,0:T(8,128)(2,1)}, f32[180,24,768]{2,1,0:T(8,128)}, bf16[6,2,30,768]{3,2,1,0:T(8,128)(2,1)}, bf16[2,2,24,768]{3,2,1,0:T(8,128)(2,1...) custom-call(s32[1]{0:T(128)} %dynamic_slice.11.height_ref, ...), custom_call_target="tpu_custom_call" | custom-call | flops 42600140800 | bytes 50000000 | tf_op jit(solution)/shard_map/mlp/pallas_call | solution.py:741
  208.8 63.9 %stencil_bwd.1 = (f32[128,128]{1,0:T(8,128)}, f32[405,128]{1,0:T(8,128)}, f32[6,180,24,128]{3,2,1,0:T(8,128)}) custom-call(s32[1]{0:T(128)} %dynamic_slice.11.height_ref, bf16[180,24,768]{2,1,0:T(8,128)(2,1)} %get-tuple-element.46.mix_ref, f32[180,24,768]{2,1,0:T(8,128)} %get-tuple-element.47.gconv_ref, bf16[2,2,24,768]{3,2,1,0:T(8,128)(2,1)} %get-tuple-element.48.cols, ...), custom_call_target="tpu_custom_call" | custom-call | tf_op jit(solution)/shard_map/stencil_bwd/pallas_call | solution.py:1033
  272.7 0.0 copy-start.2
  272.7 0.0 copy-start.4
  272.7 0.0 copy-start.5
  272.7 0.0 copy-start.6
  272.7 23.3 %norm_bwd.1 = (f32[180,24,641]{2,1,0:T(8,128)}, f32[128,128]{1,0:T(8,128)}) custom-call(s32[1]{0:T(128)} %dynamic_slice.11.height_ref, f32[6,180,24,128]{3,2,1,0:T(8,128)} %get-tuple-element.54.gm_ref, bf16[180,24,641]{2,1,0:T(8,128)(2,1)} %bitcast.50, f32[180,24,128]{2,1,0:T(8,128)} %get-tuple-element.55.mean_ref, ...), custom_call_target="tpu_custom_call" | custom-call | tf_op jit(solution)/shard_map/norm_bwd/pallas_call | solution.py:1110
  296.0 15.9 %small_gradients.1 = (f32[405,128]{1,0:T(8,128)}, f32[8,128]{1,0:T(8,128)}) custom-call(f32[405,128]{1,0:T(8,128)} %get-tuple-element.59.part_ref, f32[32,4,128]{2,1,0:T(4,128)} %bitcast.60), custom_call_target="tpu_custom_call" | custom-call | tf_op jit(solution)/shard_map/small_gradients/pallas_call | solution.py:1216
  312.0 0.0 copy-start.3
  312.0 1.2 slice.27
  314.6 0.0 copy-done.2
  314.6 0.0 copy-done.4
  314.6 0.0 copy-done.5
  314.7 1.8 fusion.2
  316.5 0.0 copy-start.1
  316.5 0.0 copy-done.6
  316.5 0.7 multiply_add_fusion
  317.2 0.0 copy-done.3
  317.2 0.7 copy.50
  317.9 0.0 copy-done.1
  (13 shorter events, 0.2 us)
Async XLA Ops:
  10.0 5.1 %copy-start.8 = (f32[24,12,9]{0,1,2:T(8,128)S(1)}, f32[24,12,9]{0,1,2:T(8,128)}, u32[]{:S(2)}) copy-start(f32[24,12,9]{0,1,2:T(8,128)} %param.16) | copy-start | bytes 31108
  10.0 5.1 %copy-start.9 = (s32[24,12]{0,1:T(8,128)S(1)}, s32[24,12]{0,1:T(8,128)}, u32[]{:S(2)}) copy-start(s32[24,12]{0,1:T(8,128)} %param.15) | copy-start | bytes 3460
  13.5 49.2 %copy-start.7 = (bf16[8,24,180]{2,1,0:T(8,128)(2,1)S(1)}, bf16[8,24,180]{2,1,0:T(8,128)(2,1)}, u32[]{:S(2)}) copy-start(bf16[8,24,180]{2,1,0:T(8,128)(2,1)} %param.12) | copy-start | bytes 207364
  15.7 49.4 %copy-start = (f32[360,16]{1,0:T(8,128)}, f32[360,16]{1,0:T(8,128)S(1)}, u32[]{:S(2)}) copy-start(f32[360,16]{1,0:T(8,128)S(1)} %pad.8.table) | copy-start | bytes 69124
  272.7 41.9 %copy-start.2 = (f32[51840]{0:T(1024)S(1)}, f32[51840]{0:T(1024)}, u32[]{:S(2)}) copy-start(f32[51840]{0:T(1024)} %param.17) | copy-start | bytes 622084
  272.7 41.9 %copy-start.4 = (f32[51840]{0:T(1024)S(1)}, f32[51840]{0:T(1024)}, u32[]{:S(2)}) copy-start(f32[51840]{0:T(1024)} %param.19) | copy-start | bytes 622084
  272.7 41.9 %copy-start.5 = (f32[51840]{0:T(1024)S(1)}, f32[51840]{0:T(1024)}, u32[]{:S(2)}) copy-start(f32[51840]{0:T(1024)} %param.18) | copy-start | bytes 622084
  272.7 43.7 %copy-start.6 = (f32[51840]{0:T(1024)S(1)}, f32[51840]{0:T(1024)}, u32[]{:S(2)}) copy-start(f32[51840]{0:T(1024)} %param.20) | copy-start | bytes 622084
  312.0 5.3 %copy-start.3 = (f32[405,128]{1,0:T(8,128)S(1)}, f32[405,128]{1,0:T(8,128)}, u32[]{:S(2)}) copy-start(f32[405,128]{1,0:T(8,128)} %get-tuple-element.61) | copy-start | bytes 622084
  316.5 1.4 copy-start.1

commit v4 on v3

--- a/solution.py
+++ b/solution.py
@@ -113,7 +113,7 @@
         ref[row : row + 1, q * LANES : (q + 1) * LANES] = value[q : q + 1, :].astype(ref.dtype)
 
 
-def unpack_weights(flat, w1, w2, wn, wd, small, wnf):
+def unpack_weights(flat, w1, w2):
     lane = iota((8, LANES), 1)
     row = iota((8, LANES), 0)
 
@@ -173,16 +173,20 @@
         v = jnp.concatenate([jnp.where(row < FF - full * LANES, v, 0.0), zero], 0)
         w2[full * LANES : full * LANES + 16, q * LANES : (q + 1) * LANES] = v.astype(BF16)
     w2[full * LANES + 16 :, :] = jnp.zeros((FP - full * LANES - 16, CP), BF16)
+
+
+def unpack_small(flat, base, wn, wd, small, wnf):
+    vector = lambda offset, length: row_vector(flat, offset - base * LANES, length)
     small[...] = jnp.zeros_like(small)
-    put_row(small, 0, row_vector(flat, OFF_B1, FF))
-    put_row(small, 1, row_vector(flat, OFF_B2, C))
-    put_row(small, 2, row_vector(flat, OFF_GAIN, C))
+    put_row(small, 0, vector(OFF_B1, FF))
+    put_row(small, 1, vector(OFF_B2, C))
+    put_row(small, 2, vector(OFF_GAIN, C))
     wd[...] = jnp.zeros_like(wd)
     wnf[...] = jnp.zeros_like(wnf)
     for k in range(K):
-        put_row(wd, k, row_vector(flat, OFF_DISCO + k * C, C))
+        put_row(wd, k, vector(OFF_DISCO + k * C, C))
     for k in range(NOISE):
-        put_row(wnf, 1 + k, row_vector(flat, OFF_NOISE + k * C, C))
+        put_row(wnf, 1 + k, vector(OFF_NOISE + k * C, C))
     wn[...] = wnf[...].astype(BF16)
 
 
@@ -272,106 +276,96 @@
     pl.semaphore_wait(barrier, count)
 
 
-def gather_kernel(
-    mesh, share_ref, cols, rows, corners, trow,
-    w1, w2, wn, wd, small, colh, rowh, cornh, trowh,
-    buf, flat, wnf, send, recv, hsend, hrecv, local_sem,
-):
-    bits = bit_list(mesh)
-    orders = stage_orders(mesh)
-    mine = my_bits(bits)
-    n = len(bits)
-    shard_rows = share_ref.shape[0]
-    cut = (shard_rows // 2 + 15) // 16 * 16
-    spans = [(0, cut), (cut, shard_rows - cut)]
-    own = pltpu.make_async_copy(share_ref, buf.at[tuple(mine)], local_sem)
-    own.start()
-    greet(bits, True)
-    halos = halo_copies(cols, rows, corners, colh, rowh, cornh, hsend, hrecv, trow, trowh)
-
-    def copy(colour, k):
-        order = orders[colour]
-        done = order[:k]
-        start, count = spans[colour]
-        index = tuple(slice(None) if i in done else mine[i] for i in range(n)) + (
-            pl.ds(start, count),
-        )
+class Gather:
+    def __init__(self, mesh, share, buf, early, send, recv, bsend, brecv):
+        self.bits = bit_list(mesh)
+        self.n = len(self.bits)
+        self.orders = stage_orders(mesh)
+        self.mine = my_bits(self.bits)
+        self.share, self.buf, self.early = share, buf, early
+        self.send, self.recv, self.bsend, self.brecv = send, recv, bsend, brecv
+        rows = share.shape[0]
+        cut = (rows // 2 + 15) // 16 * 16
+        self.spans = [(0, cut), (cut, rows - cut)]
+        self.roots, self.start = early_shards(1 << self.n, rows)
+
+    def own(self, sem):
+        return pltpu.make_async_copy(self.share, self.buf.at[tuple(self.mine)], sem)
+
+    def copy(self, colour, k):
+        order = self.orders[colour]
+        index = tuple(
+            slice(None) if i in order[:k] else self.mine[i] for i in range(self.n)
+        ) + (pl.ds(*self.spans[colour]),)
         return pltpu.make_async_remote_copy(
-            src_ref=buf.at[index],
-            dst_ref=buf.at[index],
-            send_sem=send.at[colour, k],
-            recv_sem=recv.at[colour, k],
-            device_id=partner(*bits[order[k]]),
+            src_ref=self.buf.at[index],
+            dst_ref=self.buf.at[index],
+            send_sem=self.send.at[colour, k],
+            recv_sem=self.recv.at[colour, k],
+            device_id=partner(*self.bits[order[k]]),
             device_id_type=MESH,
         )
 
-    own.wait()
-    for colour in range(2):
-        copy(colour, 0).start()
-    start_halo(halos)
-    for k in range(n):
+    def advance(self, k):
         for colour in range(2):
-            copy(colour, k).wait()
-            if k + 1 < n:
-                copy(colour, k + 1).start()
-    wait_halo(halos)
-    lat, _, nlat, *_ = neighbours()
-    for r, cond in ((0, lat == 0), (1, lat == nlat - 1)):
-
-        @pl.when(cond)
-        def _(r=r):
-            for i in range(rowh.shape[0]):
-                rowh[i, r] = jnp.zeros(rowh.shape[2:], rowh.dtype)
-            trowh[r] = jnp.zeros(trowh.shape[1:], F32)
-            for s in range(2):
-                cornh[r, s] = jnp.zeros(cornh.shape[2:], cornh.dtype)
-
-    total = 1 << n
-
-    def widen(d, carry):
-        index = tuple((d >> (n - 1 - i)) & 1 for i in range(n))
-        flat[pl.ds(d * shard_rows, shard_rows), :] = buf[index].astype(F32)
-        return carry
-
-    lax.fori_loop(0, total, widen, 0)
-    flat[total * shard_rows :, :] = jnp.zeros((flat.shape[0] - total * shard_rows, LANES), F32)
-    unpack_weights(flat, w1, w2, wn, wd, small, wnf)
-
-
-def gather_weights(mesh, share, cols, rows, corners, trow):
-    bits = bit_list(mesh)
-    n = len(bits)
-    shard_rows = share.shape[0]
-    total = shard_rows << n
-    sd = jax.ShapeDtypeStruct
-    return pl.pallas_call(
-        partial(gather_kernel, mesh),
-        name="gather_weights",
-        out_shape=(
-            sd((CP, FP), BF16),
-            sd((FP, CP), BF16),
-            sd((LANES, CP), BF16),
-            sd((16, CP), F32),
-            sd((8, FP), F32),
-            sd(cols.shape, BF16),
-            sd(rows.shape, BF16),
-            sd(corners.shape, BF16),
-            sd(trow.shape, F32),
-        ),
-        in_specs=[vmem_spec()] * 5,
-        out_specs=(vmem_spec(),) * 9,
-        scratch_shapes=[
-            pltpu.VMEM((2,) * n + (shard_rows, LANES), BF16),
-            pltpu.VMEM((total + 96, LANES), F32),
-            pltpu.VMEM((LANES, CP), F32),
-            pltpu.SemaphoreType.DMA((2, n)),
-            pltpu.SemaphoreType.DMA((2, n)),
-            pltpu.SemaphoreType.DMA((10,)),
-            pltpu.SemaphoreType.DMA((10,)),
-            pltpu.SemaphoreType.DMA,
-        ],
-        compiler_params=params(collective_id=0, has_side_effects=True),
-    )(share, cols, rows, corners, trow)
+            self.copy(colour, k).wait()
+            if k + 1 < self.n:
+                self.copy(colour, k + 1).start()
+
+    def same(self, root, indices):
+        cond = True
+        for i in indices:
+            cond = jnp.logical_and(cond, self.mine[i] == ((root >> (self.n - 1 - i)) & 1))
+        return cond
+
+    def early_own(self, sem):
+        for r, root in enumerate(self.roots):
+
+            @pl.when(self.same(root, range(self.n)))
+            def _(r=r):
+                rows = self.share.shape[0] - self.start
+                copy = pltpu.make_async_copy(
+                    self.share.at[pl.ds(self.start, rows)], self.early.at[r], sem
+                )
+                copy.start()
+                copy.wait()
+
+    def early_copies(self, k):
+        order = self.orders[0]
+        for r, root in enumerate(self.roots):
+            sends = self.same(root, order[k:])
+            now = order[k]
+            other = self.mine[now] != ((root >> (self.n - 1 - now)) & 1)
+            gets = jnp.logical_and(other, self.same(root, order[k + 1 :]))
+            yield sends, gets, pltpu.make_async_remote_copy(
+                src_ref=self.early.at[r],
+                dst_ref=self.early.at[r],
+                send_sem=self.bsend.at[r, k],
+                recv_sem=self.brecv.at[r, k],
+                device_id=partner(*self.bits[now]),
+                device_id_type=MESH,
+            )
+
+    def early_start(self, k):
+        for sends, _, copy in self.early_copies(k):
+            pl.when(sends)(copy.start)
+
+    def early_wait(self, k):
+        for sends, gets, copy in self.early_copies(k):
+            pl.when(sends)(copy.wait_send)
+            pl.when(gets)(copy.wait_recv)
+
+
+def early_shards(devices, shard_rows):
+    roots = list(range(TAIL_ROW // shard_rows, (END_FLAT - 1) // LANES // shard_rows + 1))
+    start = (TAIL_ROW - roots[0] * shard_rows) // 16 * 16 if len(roots) == 1 else 0
+    return roots, start
+
+
+def gather_plan(n):
+    if n == 5:
+        return {0: (0, -1), 1: (1, -1), 2: (2, 8), 3: (4, 14)}
+    return {}
 
 
 def norm_parts(x):
@@ -386,67 +380,127 @@
 
 
 def stencil_fwd_kernel(
-    chunks, cells, height_ref, x_ref, colh, rowh, cornh, table, wd, gain, aug, wn,
-    out_ref, mix_ref, mean_ref, inv_ref, m_scr, k_scr, nt_scr,
+    mesh, chunks, cells, height_ref, x_ref, share, cols, edge, corners, trow, table, aug,
+    out_ref, mean_ref, inv_ref, mix_hbm, w1, w2, wd, small, trowh,
+    m_scr, k_scr, nt_scr, mix_scr, wnf, wn, colh, rowh, cornh, trh, buf, early, flat, eflat,
+    send, recv, bsend, brecv, hsend, hrecv, own_sem, mix_sem,
 ):
+    gather = Gather(mesh, share, buf, early, send, recv, bsend, brecv)
+    n = gather.n
+    plan = gather_plan(n)
     step = pl.program_id(0)
     rows = x_ref.shape[1]
     width = chunks * cells
     height = height_ref[0]
-    gvec = gain[2:3, :C]
-
-    def put_cell(column, x, top, low, j=None):
-        mean = jnp.mean(x, -1, keepdims=True)
-        center = x - mean
-        inv = lax.rsqrt(jnp.mean(center * center, -1, keepdims=True) + 1e-05)
-        mixed = rounded(center * inv * gvec)
-        hrow = iota((rows, C), 0)
-        if j is not None:
+    shard_rows = share.shape[0]
+    halos = lambda: halo_copies(cols, edge, corners, colh, rowh, cornh, hsend, hrecv, trow, trh)
+    mix_copy = lambda: pltpu.make_async_copy(mix_scr, mix_hbm, mix_sem)
+
+    @pl.when(step == 0)
+    def _():
+        gather.own(own_sem).start()
+        gather.early_own(mix_sem)
+        gather.own(own_sem).wait()
+        greet(gather.bits, True)
+        gather.early_start(0)
+        for colour in range(2):
+            gather.copy(colour, 0).start()
+        start_halo(halos())
+
+    for k in range(n):
+
+        @pl.when(step == min(k + 1, chunks))
+        def _(k=k):
+            gather.early_wait(k)
+            if k + 1 < n:
+                gather.early_start(k + 1)
+
+    @pl.when(step < chunks)
+    def _():
+        def cell(j, carry):
+            x = x_ref[j].astype(F32)
+            mean = jnp.mean(x, -1, keepdims=True)
+            center = x - mean
+            inv = lax.rsqrt(jnp.mean(center * center, -1, keepdims=True) + 1e-05)
+            normed = center * inv
             mean_ref[j] = jnp.broadcast_to(mean, (rows, LANES))
             inv_ref[j] = jnp.broadcast_to(inv, (rows, LANES))
-            mix_ref[j, :, :C] = jnp.where(hrow < height, mixed, 0.0).astype(BF16)
-        mixed = jnp.where(hrow < height, mixed, jnp.where(hrow == height, low, 0.0))
-        at = column * SLOTS
-        for g in range(CB):
-            lo, hi = g * LANES, min((g + 1) * LANES, C)
-            m_scr[g, pl.ds(at + 1, rows), : hi - lo] = mixed[:, lo:hi]
-            m_scr[g, pl.ds(at, 1), : hi - lo] = top[:, lo:hi]
-            m_scr[g, pl.ds(at + rows + 1, 1), : hi - lo] = low[:, lo:hi]
-
-    def halo_mix(v):
-        center, inv = norm_parts(v.astype(F32))
-        return rounded(center * inv * gvec)
-
-    @pl.when(step == 0)
+            at = pl.ds((step * cells + j + REACH) * SLOTS + 1, rows)
+            for g in range(CB):
+                lo, hi = g * LANES, min((g + 1) * LANES, C)
+                m_scr[g, at, : hi - lo] = normed[:, lo:hi]
+            return carry
+
+        lax.fori_loop(0, cells, cell, 0, unroll=3)
+
+    @pl.when(step == chunks)
     def _():
+        if 0 in plan:
+            gather.advance(0)
+        lat, _, nlat, *_ = neighbours()
+        wait_halo(halos())
+        keep = (lat > 0, lat < nlat - 1)
+        for r in range(2):
+            trowh[r] = jnp.where(keep[r], trh[r], 0.0)
+
+        base = gather.roots[0] * shard_rows + gather.start
+        count = shard_rows - gather.start
+        eflat[...] = jnp.zeros_like(eflat)
+        for r in range(len(gather.roots)):
+            eflat[r * count : (r + 1) * count, :] = early[r].astype(F32)
+        unpack_small(eflat, base, wn, wd, small, wnf)
         k_scr[...] = jnp.dot(
             table[...], wd[...], preferred_element_type=F32, precision=HIGHEST
         ).reshape(k_scr.shape)
+        gvec = small[2:3, :C]
+
+        def mix(v):
+            center, inv = norm_parts(v.astype(F32))
+            return rounded(center * inv * gvec)
+
+        def beside(ref):
+            return [jnp.where(keep[r], mix(ref(r)), 0.0) for r in range(2)]
+
+        def put(column, top, low, fresh=None):
+            at = column * SLOTS
+            hrow = iota((rows, LANES), 0)
+            for q in range(CB):
+                lo, hi = q * LANES, min((q + 1) * LANES, C)
+                body = pl.ds(at + 1, rows)
+                wide = slice(0, hi - lo)
+                if fresh is None:
+                    v = rounded(m_scr[q, body, wide] * gvec[:, lo:hi])
+                    v = jnp.where(hrow[:, wide] < height, v, 0.0)
+                    mix_scr[column - REACH, :, lo:hi] = v.astype(BF16)
+                else:
+                    v = jnp.where(hrow[:, wide] < height, fresh[:, lo:hi], 0.0)
+                m_scr[q, body, wide] = jnp.where(hrow[:, wide] == height, low[:, lo:hi], v)
+                m_scr[q, pl.ds(at, 1), wide] = top[:, lo:hi]
+                m_scr[q, pl.ds(at + rows + 1, 1), wide] = low[:, lo:hi]
+
+        lanes = slice((CB - 1) * LANES, CB * LANES)
+        mix_scr[:, :, lanes] = jnp.zeros((width, rows, LANES), BF16)
         for side in range(2):
+            top, low = beside(lambda r: cornh[r, side])
             for i in range(REACH):
                 column = i if side == 0 else width + REACH + i
-                top = halo_mix(cornh[0, side])[i : i + 1]
-                low = halo_mix(cornh[1, side])[i : i + 1]
-                put_cell(column, colh[side, i].astype(F32), top, low)
-
-    @pl.when(step < chunks)
-    def _():
-        nt_scr[0:cells, :C] = halo_mix(rowh[0, 0])
-        nt_scr[32 : 32 + cells, :C] = halo_mix(rowh[0, 1])
-        lanes = slice((CB - 1) * LANES, CB * LANES)
-        mix_ref[:, :, lanes] = jnp.zeros((cells, rows, LANES), BF16)
-
-        def cell(j, carry):
-            put_cell(
-                step * cells + j + REACH,
-                x_ref[j].astype(F32),
-                nt_scr[pl.ds(j, 1), :C],
-                nt_scr[pl.ds(32 + j, 1), :C],
-                j,
-            )
+                put(column, top[i : i + 1], low[i : i + 1], mix(colh[side, i]))
+
+        def strip(c, carry):
+            tops, lows = beside(lambda r: rowh[c, r])
+            for i in range(cells):
+                put(c * cells + i + REACH, tops[i : i + 1], lows[i : i + 1])
             return carry
 
-        lax.fori_loop(0, cells, cell, 0, unroll=3)
+        lax.fori_loop(0, chunks, strip, 0)
+        mix_copy().start()
+
+    for k, (at, loop) in plan.items():
+        if k > 0 and loop < 0:
+
+            @pl.when(step == chunks + at)
+            def _(k=k):
+                gather.advance(k)
 
     @pl.when(step >= chunks)
     def _():
@@ -479,47 +533,94 @@
                     return carry
 
                 lax.fori_loop(0, cells // REUSE, cell, 0)
-
-
-def stencil_fwd(height, x, colh, rowh, cornh, table, wd, small, aug, wn, chunks):
+                for k, (past, loop) in plan.items():
+                    if loop == g * (rows // 8) + hb:
+
+                        @pl.when(step == chunks + past)
+                        def _(k=k):
+                            gather.advance(k)
+
+    @pl.when(step == 2 * chunks - 1)
+    def _():
+        for k in range(n):
+            if k not in plan:
+                gather.advance(k)
+        total = 1 << n
+
+        def widen(d, carry):
+            index = tuple((d >> (n - 1 - i)) & 1 for i in range(n))
+            flat[pl.ds(d * shard_rows, shard_rows), :] = buf[index].astype(F32)
+            return carry
+
+        lax.fori_loop(0, total, widen, 0)
+        flat[total * shard_rows :, :] = jnp.zeros((flat.shape[0] - total * shard_rows, LANES), F32)
+        unpack_weights(flat, w1, w2)
+        mix_copy().wait()
+
+
+def stencil_fwd(mesh, height, x, share, cols, edge, corners, trow, table, aug, chunks):
     width, rows, _ = x.shape
     cells = width // chunks
     assert cells % REUSE == 0
+    n = len(bit_list(mesh))
+    shard_rows = share.shape[0]
+    total = shard_rows << n
+    roots, start = early_shards(1 << n, shard_rows)
+    count = shard_rows - start
     first = lambda i: jnp.where(i < chunks, i, chunks - 1)
     second = lambda i: jnp.where(i < chunks, 0, i - chunks)
     sd = jax.ShapeDtypeStruct
     by_first = lambda c: pl.BlockSpec((cells, rows, c), lambda i: (first(i), 0, 0))
     by_second = lambda c: pl.BlockSpec((cells, rows, c), lambda i: (second(i), 0, 0))
+    dma = pltpu.SemaphoreType.DMA
     return pl.pallas_call(
-        partial(stencil_fwd_kernel, chunks, cells),
+        partial(stencil_fwd_kernel, mesh, chunks, cells),
         name="stencil_fwd",
         grid=(2 * chunks,),
         out_shape=(
             sd((width, rows, CP), BF16),
-            sd((width, rows, CP), BF16),
             sd((width, rows, LANES), F32),
             sd((width, rows, LANES), F32),
+            sd((width, rows, CP), BF16),
+            sd((CP, FP), BF16),
+            sd((FP, CP), BF16),
+            sd((16, CP), F32),
+            sd((8, FP), F32),
+            sd(trow.shape, F32),
         ),
-        in_specs=[
-            pl.BlockSpec(memory_space=pltpu.SMEM),
-            by_first(C),
-            vmem_spec(),
-            pl.BlockSpec((1, 2, cells, C), lambda i: (first(i), 0, 0, 0)),
-            vmem_spec(),
-            vmem_spec(),
-            vmem_spec(),
-            vmem_spec(),
-            by_second(LANES),
-            vmem_spec(),
-        ],
-        out_specs=(by_second(CP), by_first(CP), by_first(LANES), by_first(LANES)),
+        in_specs=[pl.BlockSpec(memory_space=pltpu.SMEM), by_first(C)]
+        + [vmem_spec()] * 6
+        + [by_second(LANES)],
+        out_specs=(by_second(CP), by_first(LANES), by_first(LANES), any_spec())
+        + (vmem_spec(),) * 5,
         scratch_shapes=[
             pltpu.VMEM((CB, (width + 2 * REACH) * SLOTS, LANES), F32),
             pltpu.VMEM((TAPS, rows, CP), F32),
             pltpu.VMEM((cells * rows, CP), F32),
+            pltpu.VMEM((width, rows, CP), BF16),
+            pltpu.VMEM((LANES, CP), F32),
+            pltpu.VMEM((LANES, CP), BF16),
+            pltpu.VMEM(cols.shape, BF16),
+            pltpu.VMEM(edge.shape, BF16),
+            pltpu.VMEM(corners.shape, BF16),
+            pltpu.VMEM(trow.shape, F32),
+            pltpu.VMEM((2,) * n + (shard_rows, LANES), BF16),
+            pltpu.VMEM((len(roots), count, LANES), BF16),
+            pltpu.VMEM((total + 96, LANES), F32),
+            pltpu.VMEM((len(roots) * count + 16, LANES), F32),
+            dma((2, n)),
+            dma((2, n)),
+            dma((len(roots), n)),
+            dma((len(roots), n)),
+            dma((10,)),
+            dma((10,)),
+            dma,
+            dma,
         ],
-        compiler_params=params(dimension_semantics=("arbitrary",)),
-    )(height, x, colh, rowh, cornh, table, wd, small, aug, wn)
+        compiler_params=params(
+            dimension_semantics=("arbitrary",), collective_id=0, has_side_effects=True
+        ),
+    )(height, x, share, cols, edge, corners, trow, table, aug)
 
 
 def pack_weights(one, two, flat):
@@ -1271,9 +1372,6 @@
     corners = jnp.stack([edge[:REACH], edge[width - REACH :]], 0)
     corners = jnp.transpose(corners, (2, 0, 1, 3))
     edge = jnp.transpose(edge.reshape(chunks, cells, 2, C), (0, 2, 1, 3))
-    w1, w2, wn, wd, small, colh, rowh, cornh, trowh = gather_weights(
-        mesh, share, cols, edge, corners, trow
-    )
     aug = jnp.concatenate(
         [
             jnp.zeros((width, rows, 1), BF16),
@@ -1283,8 +1381,8 @@
         ],
         2,
     )
-    conv, mixed, mean, inv = stencil_fwd(
-        height, x, colh, rowh, cornh, table, wd, small, aug, wn, chunks
+    conv, mean, inv, mixed, w1, w2, wd, small, trowh = stencil_fwd(
+        mesh, height, x, share, cols, edge, corners, trow, table, aug, chunks
     )
     shards = (2,) * len(bit_list(mesh)) + (shard_rows, LANES)
     out, gconv, grow, gcol, gcorn, packed, extra = mlp(

time: 318 us -> 293 us (0.921)
  Pallas kernels: 293 us -> 268 us
    pallas_call x2 -> x1, Pallas kernels: 87.9 us -> 62.5 us  [stencil_fwd(): pl.pallas_call(partial(stencil_fwd_kernel, mesh, chunks, cells), name='st...]
where the time goes in v4:
time: 293 us
  Pallas kernels  268 us (91%)
  local copies, waits for them, and re-layouts  12.9 us (4%)
  other arithmetic  8.3 us (3%)
  between operations  3.62 us (1%)
    pallas_call x1, Pallas kernels, mlp(): pl.pallas_call(partial(mlp_kernel, blocks), name='mlp', grid=(blocks,), o...  102 us
    pallas_call x1, Pallas kernels, stencil_bwd(): pl.pallas_call(partial(stencil_bwd_kernel, mesh, chunks, cells), name='st...  65.7 us
    pallas_call x1, Pallas kernels, stencil_fwd(): pl.pallas_call(partial(stencil_fwd_kernel, mesh, chunks, cells), name='st...  62.5 us
    pallas_call x1, Pallas kernels, norm_bwd(): pl.pallas_call(norm_bwd_kernel, name='norm_bwd', grid=(chunks,), out_shap...  23.3 us
    pallas_call x1, Pallas kernels, finish(): pl.pallas_call(partial(tail_kernel, mesh), name='small_gradients', out_sh...  14.3 us

profile of v4, /device:TPU:0, one launch (start us, length us, event | category | flops | bytes accessed | tf_op | source)
XLA Modules:
  0.0 292.5 jit_solution(12153606099255635813)
XLA Ops:
  0.6 1.2 dynamic_slice.11.height_ref
  1.9 1.6 convert_bitcast_fusion.share
  3.5 0.9 slice_bitcast_fusion.1
  4.4 0.7 pad_maximum_fusion.cols
  6.4 3.5 %dynamic-slice_bitcast_fusion = (bf16[180,1,641]{2,1,0:T(2,128)(2,1)S(1)}, bf16[180,641]{1,0:T(8,128)(2,1)S(1)}) fusion(bf16[24,180,641]{2,0,1:T(8,128)(2,1)} %param.11, s32[]{:T(128)S(6)} %select_n.14), kind=kLoop, calls=%fused_computation.3 | loop fusion | bytes 692284 | tf_op jit(solution)/shard_map/jit(dynamic_index_in_dim)/dynamic_slice | solution.py:1370
  9.9 0.1 stack.38
  10.0 0.0 copy-start.8
  10.0 0.0 copy-start.9
  10.0 3.4 %fusion.4 = (bf16[180,1,641]{2,1,0:T(2,128)(2,1)S(1)}, bf16[180,641]{1,0:T(8,128)(2,1)S(1)}) fusion(bf16[180,24,641]{2,1,0:T(8,128)(2,1)} %bitcast.47), kind=kLoop, calls=%fused_computation.26 | loop fusion | bytes 692280 | tf_op jit(solution)/shard_map/slice | solution.py:1370
  13.4 0.0 copy-start.7
  13.4 0.1 stack.37
  13.5 0.9 maximum_bitcast_fusion.edge
  14.4 0.6 copy.42.corners
  15.1 0.0 copy-done.8
  15.1 0.0 copy-done.9
  15.2 0.1 broadcast_compare_fusion
  15.2 0.2 select_reduce_fusion
  15.5 0.2 copy.38
  15.7 0.0 copy-start
  15.7 0.6 select_maximum_fusion.trow
  16.4 0.0 copy-done.7
  16.4 0.7 copy.41
  17.1 0.1 pad.13.clone
  17.2 0.1 pad.12.clone
  17.2 1.6 maximum_maximum_fusion.aug
  18.8 0.0 copy-done
  18.8 62.5 %stencil_fwd.1 = (bf16[180,24,768]{2,1,0:T(8,128)(2,1)}, f32[180,24,128]{2,1,0:T(8,128)}, f32[180,24,128]{2,1,0:T(8,128)}, bf16[180,24,768]{2,1,0:T(8,128)(2,1)}...) custom-call(s32[1]{0:T(128)} %dynamic_slice.11.height_ref, ...), custom_call_target="tpu_custom_call" | custom-call | tf_op jit(solution)/shard_map/stencil_fwd/pallas_call | solution.py:576
  81.3 102.0 %mlp.1 = (bf16[180,24,641]{2,1,0:T(8,128)(2,1)}, f32[180,24,768]{2,1,0:T(8,128)}, bf16[6,2,30,768]{3,2,1,0:T(8,128)(2,1)}, bf16[2,2,24,768]{3,2,1,0:T(8,128)(2,1...) custom-call(s32[1]{0:T(128)} %dynamic_slice.11.height_ref, ...), custom_call_target="tpu_custom_call" | custom-call | flops 42600140800 | bytes 50000000 | tf_op jit(solution)/shard_map/mlp/pallas_call | solution.py:842
  183.3 65.7 %stencil_bwd.1 = (f32[128,128]{1,0:T(8,128)}, f32[405,128]{1,0:T(8,128)}, f32[6,180,24,128]{3,2,1,0:T(8,128)}) custom-call(s32[1]{0:T(128)} %dynamic_slice.11.height_ref, bf16[180,24,768]{2,1,0:T(8,128)(2,1)} %get-tuple-element.37.mix_ref, f32[180,24,768]{2,1,0:T(8,128)} %get-tuple-element.38.gconv_ref, bf16[2,2,24,768]{3,2,1,0:T(8,128)(2,1)} %get-tuple-element.39.cols, ...), custom_call_target="tpu_custom_call" | custom-call | tf_op jit(solution)/shard_map/stencil_bwd/pallas_call | solution.py:1134
  249.0 0.0 copy-start.2
  249.0 0.0 copy-start.4
  249.0 0.0 copy-start.5
  249.0 0.0 copy-start.6
  249.0 23.3 %norm_bwd.1 = (f32[180,24,641]{2,1,0:T(8,128)}, f32[128,128]{1,0:T(8,128)}) custom-call(s32[1]{0:T(128)} %dynamic_slice.11.height_ref, f32[6,180,24,128]{3,2,1,0:T(8,128)} %get-tuple-element.46.gm_ref, bf16[180,24,641]{2,1,0:T(8,128)(2,1)} %bitcast.50, f32[180,24,128]{2,1,0:T(8,128)} %get-tuple-element.47.mean_ref, ...), custom_call_target="tpu_custom_call" | custom-call | tf_op jit(solution)/shard_map/norm_bwd/pallas_call | solution.py:1211
  272.3 14.3 %small_gradients.1 = (f32[405,128]{1,0:T(8,128)}, f32[8,128]{1,0:T(8,128)}) custom-call(f32[405,128]{1,0:T(8,128)} %get-tuple-element.51.part_ref, f32[32,4,128]{2,1,0:T(4,128)} %bitcast.60), custom_call_target="tpu_custom_call" | custom-call | tf_op jit(solution)/shard_map/small_gradients/pallas_call | solution.py:1317
  286.6 0.0 copy-start.3
  286.6 1.2 slice.27
  289.2 0.0 copy-done.2
  289.3 0.0 copy-done.4
  289.3 0.0 copy-done.5
  289.3 1.8 fusion.2
  291.1 0.0 copy-start.1
  291.1 0.0 copy-done.6
  291.1 0.7 multiply_add_fusion
  291.8 0.0 copy-done.3
  291.8 0.7 copy.50
  292.5 0.0 copy-done.1
  (13 shorter events, 0.2 us)
Async XLA Ops:
  10.0 5.1 %copy-start.8 = (f32[24,12,9]{0,1,2:T(8,128)S(1)}, f32[24,12,9]{0,1,2:T(8,128)}, u32[]{:S(2)}) copy-start(f32[24,12,9]{0,1,2:T(8,128)} %param.16) | copy-start | bytes 31108
  10.0 5.1 %copy-start.9 = (s32[24,12]{0,1:T(8,128)S(1)}, s32[24,12]{0,1:T(8,128)}, u32[]{:S(2)}) copy-start(s32[24,12]{0,1:T(8,128)} %param.15) | copy-start | bytes 3460
  13.4 3.0 %copy-start.7 = (bf16[8,24,180]{2,1,0:T(8,128)(2,1)S(1)}, bf16[8,24,180]{2,1,0:T(8,128)(2,1)}, u32[]{:S(2)}) copy-start(bf16[8,24,180]{2,1,0:T(8,128)(2,1)} %param.12) | copy-start | bytes 207364
  15.7 3.2 %copy-start = (f32[360,16]{1,0:T(8,128)}, f32[360,16]{1,0:T(8,128)S(1)}, u32[]{:S(2)}) copy-start(f32[360,16]{1,0:T(8,128)S(1)} %pad.8.table) | copy-start | bytes 69124
  249.0 40.3 %copy-start.2 = (f32[51840]{0:T(1024)S(1)}, f32[51840]{0:T(1024)}, u32[]{:S(2)}) copy-start(f32[51840]{0:T(1024)} %param.17) | copy-start | bytes 622084
  249.0 40.3 %copy-start.4 = (f32[51840]{0:T(1024)S(1)}, f32[51840]{0:T(1024)}, u32[]{:S(2)}) copy-start(f32[51840]{0:T(1024)} %param.19) | copy-start | bytes 622084
  249.0 40.3 %copy-start.5 = (f32[51840]{0:T(1024)S(1)}, f32[51840]{0:T(1024)}, u32[]{:S(2)}) copy-start(f32[51840]{0:T(1024)} %param.18) | copy-start | bytes 622084
  249.0 42.1 %copy-start.6 = (f32[51840]{0:T(1024)S(1)}, f32[51840]{0:T(1024)}, u32[]{:S(2)}) copy-start(f32[51840]{0:T(1024)} %param.20) | copy-start | bytes 622084
  286.6 5.3 %copy-start.3 = (f32[405,128]{1,0:T(8,128)S(1)}, f32[405,128]{1,0:T(8,128)}, u32[]{:S(2)}) copy-start(f32[405,128]{1,0:T(8,128)} %get-tuple-element.53) | copy-start | bytes 622084
  291.1 1.4 copy-start.1

commit v5 on v4

--- a/solution.py
+++ b/solution.py
@@ -249,6 +249,32 @@
             pl.when(gets)(copy.wait_recv)
 
 
+def for_others(mesh, body):
+    nlat, nlon = mesh.shape["lat"], mesh.shape["lon"]
+    lat, lon = lax.axis_index("lat"), lax.axis_index("lon")
+    beside = [(lon + b) & (nlon - 1) for b in range(nlon)]
+    for x in beside[1:]:
+        body((lat, x), lat * nlon + x)
+
+    def row(a, carry):
+        y = (lat + a) & (nlat - 1)
+        for x in beside:
+            body((y, x), y * nlon + x)
+        return carry
+
+    lax.fori_loop(1, nlat, row, 0)
+
+
+def greet_all(mesh):
+    barrier = pltpu.get_barrier_semaphore()
+
+    def hello(target, d):
+        pl.semaphore_signal(barrier, inc=1, device_id=target, device_id_type=MESH)
+
+    for_others(mesh, hello)
+    pl.semaphore_wait(barrier, mesh.shape["lat"] * mesh.shape["lon"] - 1)
+
+
 def greet(bits, halo):
     barrier = pltpu.get_barrier_semaphore()
     lat, lon, nlat, nlon, east, west = neighbours()
@@ -285,7 +311,7 @@
         self.share, self.buf, self.early = share, buf, early
         self.send, self.recv, self.bsend, self.brecv = send, recv, bsend, brecv
         rows = share.shape[0]
-        cut = (rows // 2 + 15) // 16 * 16
+        cut = (rows * 2 // 3 + 15) // 16 * 16
         self.spans = [(0, cut), (cut, rows - cut)]
         self.roots, self.start = early_shards(1 << self.n, rows)
 
@@ -381,7 +407,7 @@
 
 def stencil_fwd_kernel(
     mesh, chunks, cells, height_ref, x_ref, share, cols, edge, corners, trow, table, aug,
-    out_ref, mean_ref, inv_ref, mix_hbm, w1, w2, wd, small, trowh,
+    out_ref, mix_hbm, w1, w2, wd, small, trowh,
     m_scr, k_scr, nt_scr, mix_scr, wnf, wn, colh, rowh, cornh, trh, buf, early, flat, eflat,
     send, recv, bsend, brecv, hsend, hrecv, own_sem, mix_sem,
 ):
@@ -423,15 +449,13 @@
             center = x - mean
             inv = lax.rsqrt(jnp.mean(center * center, -1, keepdims=True) + 1e-05)
             normed = center * inv
-            mean_ref[j] = jnp.broadcast_to(mean, (rows, LANES))
-            inv_ref[j] = jnp.broadcast_to(inv, (rows, LANES))
             at = pl.ds((step * cells + j + REACH) * SLOTS + 1, rows)
             for g in range(CB):
                 lo, hi = g * LANES, min((g + 1) * LANES, C)
                 m_scr[g, at, : hi - lo] = normed[:, lo:hi]
             return carry
 
-        lax.fori_loop(0, cells, cell, 0, unroll=3)
+        lax.fori_loop(0, cells, cell, 0, unroll=10)
 
     @pl.when(step == chunks)
     def _():
@@ -579,8 +603,6 @@
         grid=(2 * chunks,),
         out_shape=(
             sd((width, rows, CP), BF16),
-            sd((width, rows, LANES), F32),
-            sd((width, rows, LANES), F32),
             sd((width, rows, CP), BF16),
             sd((CP, FP), BF16),
             sd((FP, CP), BF16),
@@ -591,7 +613,7 @@
         in_specs=[pl.BlockSpec(memory_space=pltpu.SMEM), by_first(C)]
         + [vmem_spec()] * 6
         + [by_second(LANES)],
-        out_specs=(by_second(CP), by_first(LANES), by_first(LANES), any_spec())
+        out_specs=(by_second(CP), any_spec())
         + (vmem_spec(),) * 5,
         scratch_shapes=[
             pltpu.VMEM((CB, (width + 2 * REACH) * SLOTS, LANES), F32),
@@ -725,7 +747,7 @@
 def mlp_kernel(
     blocks, height_ref, conv_ref, g_ref, x_ref, w1, w2, small,
     out_ref, gconv_ref, rows_ref, cols_ref, corn_ref, shards_ref, extra_ref,
-    one, two, g_scr, conv_t, act, gh, flat,
+    one, two, g_scr, conv_t, act, gh, flat, w1_rest,
 ):
     step = pl.program_id(0)
     cells, rows, _ = x_ref.shape
@@ -737,6 +759,7 @@
         one[...] = jnp.zeros_like(one)
         two[...] = jnp.zeros_like(two)
         g_scr[...] = jnp.zeros_like(g_scr)
+        w1_rest[...] = w1[:, FP // WIDE * WIDE :].astype(F32).T[: w1_rest.shape[0]]
 
     live = (iota((1, rows, 1), 1) < height).astype(F32)
     g_scr[:, :C] = (g_ref[...].astype(F32) * live).reshape(m, C).astype(BF16)
@@ -761,25 +784,32 @@
         part = conv_ref[:, :, pl.ds(i * LANES, LANES)].reshape(m, LANES)
         conv_t[pl.ds(i * LANES, count), :] = part.T[:count]
 
-    def first(f, carry):
-        turn(pl.multiple_of(f, 1), LANES)
-        hidden(pl.multiple_of(f * WIDE, WIDE), WIDE, False)
-        return carry
-
-    lax.fori_loop(0, FP // WIDE, first, 0)
-    assert FP // WIDE == CB - 1
+    full = FP // WIDE
+    assert full == CB - 1
+    for f in range(full):
+        turn(f, LANES)
+        hidden(f * WIDE, WIDE, False)
     turn(CB - 1, rows_one - (CB - 1) * LANES)
-    hidden(FP // WIDE * WIDE, FP % WIDE, True)
-
+    hidden(full * WIDE, FP % WIDE, True)
+
+    main = full * WIDE
+    spare = [
+        (act[:, main + i : main + i + 1].astype(F32), gh[:, main + i : main + i + 1].astype(F32))
+        for i in range(FF - main)
+    ]
     for n in range(CP // WIDE):
         lanes = slice(n * WIDE, (n + 1) * WIDE)
         end = min((n + 1) * WIDE, C)
         part = slice(n * WIDE, end)
-        branch = dot(act[...], w2[:, lanes])[:, : end - n * WIDE]
-        v = x_ref[:, :, part].astype(F32).reshape(m, -1) + branch + small[1:2, part]
+        branch = dot(act[:, :main], w2[:main, lanes])
+        gc = dot(gh[:, :main], w1[lanes, :main], ((1,), (1,)))
+        for i, (a, b) in enumerate(spare):
+            branch = branch + a * w2[main : main + 16, lanes].astype(F32)[i : i + 1]
+            gc = gc + b * w1_rest[i : i + 1, lanes]
+        v = x_ref[:, :, part].astype(F32).reshape(m, -1) + branch[:, : end - n * WIDE] + small[1:2, part]
         out_ref[:, :, part] = (v.reshape(cells, rows, -1) * live).astype(BF16)
-        gc = dot(gh[...], w1[lanes, :], ((1,), (1,)))
-        gconv_ref[:, :, lanes] = gc.reshape(cells, rows, WIDE)
+        for i in range(WIDE // LANES):
+            gconv_ref[n * (WIDE // LANES) + i] = gc[:, i * LANES : (i + 1) * LANES]
 
     def weights(start, wide):
         lanes = pl.ds(start, wide)
@@ -797,19 +827,31 @@
     lax.fori_loop(0, FP // WIDE, third, 0)
     weights(FP // WIDE * WIDE, FP % WIDE)
 
-    onehot = (iota((1, rows, 1), 1) == height - 1).astype(F32)
-    block = gconv_ref[...]
-    edges = (block[:, 0, :].astype(BF16), jnp.sum(block * onehot, 1).astype(BF16))
-    for r in range(2):
-        rows_ref[0, r] = edges[r]
+    whole, left = divmod(cells, 8)
+    for r, slot in ((0, 0), (1, height - 1)):
+        for q in range(CB):
+            lanes = slice(q * LANES, (q + 1) * LANES)
+            pick = lambda c: gconv_ref[q, pl.ds(slot + c * rows, 8, stride=rows), :]
+            v = [pick(8 * i) for i in range(whole)]
+            if left:
+                v.append(pltpu.roll(pick(cells - 8), left, 0))
+            v = jnp.concatenate(v, 0).astype(BF16)
+            rows_ref[0, r, :, lanes] = v
+            for side, at, first in ((0, 0, 0), (1, blocks - 1, cells - REACH)):
+
+                @pl.when(step == at)
+                def _(side=side, first=first, v=v, lanes=lanes, r=r):
+                    corn_ref[r, side, :, lanes] = v[first : first + REACH]
+
     for side, at, first in ((0, 0, 0), (1, blocks - 1, cells - REACH)):
 
         @pl.when(step == at)
         def _(side=side, first=first):
             for i in range(REACH):
-                cols_ref[side, i] = gconv_ref[first + i].astype(BF16)
-            for r in range(2):
-                corn_ref[r, side] = edges[r][first : first + REACH]
+                base = (first + i) * rows
+                for q in range(CB):
+                    lanes = slice(q * LANES, (q + 1) * LANES)
+                    cols_ref[side, i, :, lanes] = gconv_ref[q, base : base + rows, :].astype(BF16)
 
     @pl.when(step == blocks - 1)
     def _():
@@ -845,8 +887,8 @@
         grid=(blocks,),
         out_shape=(
             sd((width, rows, C), BF16),
-            sd((width, rows, CP), F32),
-            sd((blocks, 2, cells, CP), BF16),
+            sd((CB, width * rows, LANES), F32),
+            sd((blocks, 2, -(-cells // 8) * 8, CP), BF16),
             sd((2, REACH, rows, CP), BF16),
             sd((2, 2, REACH, CP), BF16),
             sd(shards, F32),
@@ -863,8 +905,8 @@
         ],
         out_specs=(
             block(C),
-            block(CP),
-            pl.BlockSpec((1, 2, cells, CP), lambda i: (i, 0, 0, 0)),
+            pl.BlockSpec((CB, m, LANES), lambda i: (0, i, 0)),
+            pl.BlockSpec((1, 2, -(-cells // 8) * 8, CP), lambda i: (i, 0, 0, 0)),
             vmem_spec(),
             vmem_spec(),
             vmem_spec(),
@@ -878,6 +920,7 @@
             pltpu.VMEM((m, FP), BF16),
             pltpu.VMEM((m, FP), BF16),
             pltpu.VMEM((math.prod(shards[:-1]), LANES), F32),
+            pltpu.VMEM((8, CP), F32),
         ],
         compiler_params=params(dimension_semantics=("arbitrary",)),
         cost_estimate=pl.CostEstimate(flops=flops, bytes_accessed=50_000_000, transcendentals=0),
@@ -966,32 +1009,111 @@
 
 def scatter_plan(n):
     if n == 5:
-        return {8: [(0, 1), (1, 1), (2, 1)], 13: [(0, 2), (1, 2)], 15: [(2, 2)], 17: [(0, 3), (1, 3), (2, 3)]}
+        return {
+            7: [(0, 1), (1, 1), (2, 1)],
+            12: [(0, 2), (1, 2)],
+            13: [(2, 2)],
+            17: [(0, 3), (1, 3), (2, 3)],
+        }
     return {}
 
 
-def stencil_bwd_kernel(
-    mesh, chunks, cells, height_ref, mix_ref, gconv_ref,
-    cols, edge, corners, table, trowh, wd, extra, w1, shards,
-    tail_ref, part_ref, gm_ref,
-    g_scr, m_scr, k_scr, t_scr, e_scr, colh, rowh, cornh, buf, *rest,
+class Tail:
+    def __init__(self, mesh, pieces, got, msg, full, place, send, recv):
+        self.mesh = mesh
+        self.n = mesh.shape["lat"] * mesh.shape["lon"]
+        self.lat, self.lon = lax.axis_index("lat"), lax.axis_index("lon")
+        self.me = self.lat * mesh.shape["lon"] + self.lon
+        self.pieces, self.got, self.msg, self.full, self.place = pieces, got, msg, full, place
+        self.send, self.recv = send, recv
+
+    def others(self, source, target, k):
+        def send(device, d):
+            pltpu.make_async_remote_copy(
+                src_ref=source(d),
+                dst_ref=target.at[self.me],
+                send_sem=self.send.at[k],
+                recv_sem=self.recv.at[k],
+                device_id=device,
+                device_id_type=MESH,
+            ).start()
+
+        for_others(self.mesh, send)
+
+    def wait_all(self, buffer, k):
+        pltpu.make_async_remote_copy(
+            src_ref=buffer.at[pl.ds(0, self.n - 1)],
+            dst_ref=buffer.at[pl.ds(0, self.n - 1)],
+            send_sem=self.send.at[k],
+            recv_sem=self.recv.at[k],
+            device_id=(self.lat, self.lon),
+            device_id_type=MESH,
+        ).wait()
+
+    def scatter(self, flat):
+        piece = self.pieces.shape[1]
+
+        def split(d, carry):
+            self.pieces[d] = flat[pl.ds(d * piece, piece), :]
+            return carry
+
+        lax.fori_loop(0, self.n, split, 0)
+        self.others(lambda d: self.pieces.at[d], self.got, 0)
+        self.got[self.me] = self.pieces[self.me]
+        self.place[...] = jnp.zeros_like(self.place)
+
+    def finish(self, part, grad_ref, norm_ref):
+        n, piece = self.n, self.pieces.shape[1]
+        shard_rows = part.shape[0]
+        square = jnp.sum(part * part)
+        self.wait_all(self.got, 0)
+        total = lax.fori_loop(1, n, lambda i, acc: acc + self.got[i], self.got[0])
+        square = square + jnp.sum(total * total)
+        self.msg[0:piece, :] = total
+        self.msg[piece : piece + 1, :] = jnp.broadcast_to(square, (1, LANES))
+        self.others(lambda d: self.msg, self.full, 1)
+        self.full[self.me] = self.msg[...]
+        self.wait_all(self.full, 1)
+
+        def take(d, acc):
+            self.place[pl.ds(shard_rows + d * piece, piece), :] = self.full[d, 0:piece, :]
+            return acc + self.full[d, piece : piece + 1, :]
+
+        squares = lax.fori_loop(0, n, take, jnp.zeros((1, LANES), F32))
+        start = jnp.clip(self.me * shard_rows - TAIL_ROW + shard_rows, 0, shard_rows + n * piece)
+        grad_ref[...] = part + self.place[pl.ds(start, shard_rows), :]
+        norm_ref[...] = jnp.broadcast_to(jnp.sqrt(squares), norm_ref.shape)
+
+
+def backward_kernel(
+    mesh, chunks, cells, strip_cells, height_ref, mix_ref, gconv_ref, x_hbm, g_hbm,
+    cols, edge, corners, table, trowh, wd, gain, extra, w1, shards,
+    out_ref, grad_ref, norm_ref,
+    x_scr, up_scr, st_scr, g_scr, m_scr, k_scr, t_scr, e_scr, gg_scr, tail_scr, colh, rowh, cornh,
+    pieces, got, msg, full, place, buf, *rest,
 ):
     n = len(bit_list(mesh))
-    recvs, (send, recv, hsend, hrecv, load_sem, out_sem) = rest[:n], rest[n:]
+    recvs, (send, recv, hsend, hrecv, tsend, trecv, load_sem) = rest[:n], rest[n:]
     scatter = Scatter(mesh, shards, buf, recvs, send, recv)
+    tail = Tail(mesh, pieces, got, msg, full, place, tsend, trecv)
     step = pl.program_id(0)
-    rows = mix_ref.shape[1]
-    width = chunks * cells
+    width, rows, _ = mix_ref.shape
     height = height_ref[0]
     plan = scatter_plan(n)
+    gvec = gain[2:3, :C]
+    halos = lambda: halo_copies(cols, edge, corners, colh, rowh, cornh, hsend, hrecv)
+    load_x = lambda: pltpu.make_async_copy(x_hbm, x_scr, load_sem.at[1])
+    load_up = lambda: pltpu.make_async_copy(g_hbm, up_scr, load_sem.at[2])
 
     @pl.when(step == 0)
     def _():
-        scatter.load(load_sem).start()
-        greet(scatter.bits, True)
-        start_halo(halo_copies(cols, edge, corners, colh, rowh, cornh, hsend, hrecv))
+        load_x().start()
+        greet_all(mesh)
+        start_halo(halos())
         for colour in range(3):
             scatter.copy(colour, 0).start()
+        scatter.load(load_sem.at[0]).start()
+        load_up().start()
         hrow = iota((rows, 16), 0)
         for t in range(TAPS):
             l = t // 5
@@ -1002,106 +1124,120 @@
             if l == 2:
                 own = jnp.concatenate([trowh[0, t : t + 1, :], own[: rows - 1]], 0)
             t_scr[t * rows : (t + 1) * rows, :] = own
-        k_scr[...] = jnp.dot(
-            t_scr[...], wd[...], preferred_element_type=F32, precision=HIGHEST
-        ).reshape(k_scr.shape)
+        kernel = jnp.dot(t_scr[...], wd[...], preferred_element_type=F32, precision=HIGHEST)
+        for q in range(CB):
+            k_scr[q] = kernel[:, q * LANES : (q + 1) * LANES].reshape(k_scr.shape[1:])
         e_scr[...] = jnp.zeros_like(e_scr)
-
-    @pl.when(step < chunks)
+        gg_scr[...] = jnp.zeros_like(gg_scr)
+        load_x().wait()
+        first_lane = iota((rows, LANES), 1) == 0
+
+        def stats(j, carry):
+            x = x_scr[j].astype(F32)
+            mean = jnp.mean(x, -1, keepdims=True)
+            center = x - mean
+            inv = lax.rsqrt(jnp.mean(center * center, -1, keepdims=True) + 1e-05)
+            st_scr[j] = jnp.where(first_lane, mean, inv)
+            return carry
+
+        lax.fori_loop(0, width, stats, 0, unroll=10)
+
+    @pl.when(step == 1)
     def _():
-        def cell(j, carry):
-            v = gconv_ref[j]
-            mixed = mix_ref[j].astype(F32)
-            at = (step * cells + j + REACH) * SLOTS
-            for q in range(CB):
-                lanes = slice(q * LANES, (q + 1) * LANES)
-                g_scr[q, pl.ds(at + 1, rows), :] = v[:, lanes]
-                m_scr[q, step * cells + j] = mixed[:, lanes]
-            return carry
-
-        lax.fori_loop(0, cells, cell, 0, unroll=2)
-
-    @pl.when(step == chunks)
-    def _():
-        scatter.load(load_sem).wait()
+        wait_halo(halos())
+        scatter.load(load_sem.at[0]).wait()
         for colour in range(3):
             scatter.advance(colour, 0)
-        wait_halo(halo_copies(cols, edge, corners, colh, rowh, cornh, hsend, hrecv))
+
+    @pl.when((step >= 1) & (step <= CB))
+    def _():
+        q = step - 1
+        lanes = pl.ds(pl.multiple_of(q * LANES, LANES), LANES)
         lat, _, nlat, *_ = neighbours()
-        keep = ((lat > 0).astype(F32), (lat < nlat - 1).astype(F32))
-
-        def put(column, top, low, fresh=None):
+        keep = (lat > 0, lat < nlat - 1)
+        here = iota((rows, LANES), 0) == height
+
+        def put(column, top, low, v):
             at = column * SLOTS
-            here = iota((rows, LANES), 0) == height
-            for q in range(CB):
-                lanes = slice(q * LANES, (q + 1) * LANES)
-                body = pl.ds(at + 1, rows)
-                old = g_scr[q, body, :] if fresh is None else fresh[:, lanes]
-                g_scr[q, body, :] = jnp.where(here, low[:, lanes], old)
-                g_scr[q, pl.ds(at, 1), :] = top[:, lanes]
-                g_scr[q, pl.ds(at + rows + 1, 1), :] = low[:, lanes]
+            g_scr[pl.ds(at + 1, rows), :] = jnp.where(here, low, v)
+            g_scr[pl.ds(at, 1), :] = top
+            g_scr[pl.ds(at + rows + 1, 1), :] = low
 
         def beside(ref):
-            return [jnp.where(keep[r] > 0, ref(r).astype(F32), 0.0) for r in range(2)]
+            return [jnp.where(keep[r], ref(r).astype(F32), 0.0) for r in range(2)]
 
         for side in range(2):
-            top, low = beside(lambda r: cornh[r, side])
+            top, low = beside(lambda r: cornh[r, side, :, lanes])
             for i in range(REACH):
                 column = i if side == 0 else width + REACH + i
-                put(column, top[i : i + 1], low[i : i + 1], colh[side, i].astype(F32))
+                put(column, top[i : i + 1], low[i : i + 1], colh[side, i, :, lanes].astype(F32))
 
         def strip(c, carry):
-            tops, lows = beside(lambda r: rowh[c, r])
-            for i in range(cells):
-                put(c * cells + i + REACH, tops[i : i + 1], lows[i : i + 1])
+            tops, lows = beside(lambda r: rowh[c, r, :, lanes])
+            for i in range(strip_cells):
+                j = c * strip_cells + i
+                v = gconv_ref[0, pl.ds(pl.multiple_of(j * rows, 8), rows), :]
+                put(j + REACH, tops[i : i + 1], lows[i : i + 1], v)
+                m_scr[q, j] = mix_ref[j].astype(F32)
             return carry
 
-        lax.fori_loop(0, chunks, strip, 0)
-        for q in range(CB):
-            lanes = slice(q * LANES, (q + 1) * LANES)
-            for hb in range(rows // 8):
-                at = slice(8 * hb, 8 * hb + 8)
-
-                def cell(i, carry):
-                    j = i * REUSE
-                    mixed = [m_scr[q, j + u, at, :] for u in range(REUSE)]
-                    total = [None] * REUSE
-                    for l in range(3):
-                        near = [
-                            g_scr[q, pl.ds((j + u) * SLOTS + 8 * hb + 2 - l, 8), :]
-                            for u in range(REUSE + 2 * REACH)
-                        ]
-                        for w in range(5):
-                            t = 5 * l + w
-                            tap = k_scr[t, at, lanes]
-                            views = near[2 * REACH - w : 2 * REACH - w + REUSE]
-                            terms = [tap * v for v in views]
-                            total = [a if b is None else a + b for a, b in zip(terms, total)]
-                            sums = [m * v for m, v in zip(mixed, views)]
-                            while len(sums) > 1:
-                                sums = [
-                                    sums[k] + sums[k + 1] if k + 1 < len(sums) else sums[k]
-                                    for k in range(0, len(sums), 2)
-                                ]
-                            e_scr[t, at, lanes] = e_scr[t, at, lanes] + sums[0]
-                    for u in range(REUSE):
-                        m_scr[q, j + u, at, :] = total[u]
-                    return carry
-
-                lax.fori_loop(0, width // REUSE, cell, 0)
-                for colour, k in plan.get(q * (rows // 8) + hb, []):
-                    scatter.advance(colour, k)
-            pltpu.make_async_copy(m_scr.at[q], gm_ref.at[q], out_sem.at[q]).start()
-
-        tail_ref[...] = jnp.zeros_like(tail_ref)
-        add_vector(tail_ref, OFF_B1, as_blocks(extra[NOISE : NOISE + 1, :], FF))
-        add_vector(tail_ref, OFF_B2, as_blocks(extra[NOISE + 1 : NOISE + 2, :], C))
-        disco = lax.dot_general(
-            t_scr[...], e_scr[...].reshape(TAPS * rows, CP), (((0,), (0,)), ((), ())),
-            preferred_element_type=F32, precision=HIGHEST,
+        lax.fori_loop(0, edge.shape[0], strip, 0)
+        for hb in range(rows // 8):
+            at = slice(8 * hb, 8 * hb + 8)
+
+            def cell(i, carry):
+                j = i * REUSE
+                mixed = [m_scr[q, j + u, at, :] for u in range(REUSE)]
+                total = [None] * REUSE
+                for l in range(3):
+                    near = [
+                        g_scr[pl.ds((j + u) * SLOTS + 8 * hb + 2 - l, 8), :]
+                        for u in range(REUSE + 2 * REACH)
+                    ]
+                    for w in range(5):
+                        t = 5 * l + w
+                        tap = k_scr[q, t, at, :]
+                        views = near[2 * REACH - w : 2 * REACH - w + REUSE]
+                        terms = [tap * v for v in views]
+                        total = [a if b is None else a + b for a, b in zip(terms, total)]
+                        sums = [m * v for m, v in zip(mixed, views)]
+                        while len(sums) > 1:
+                            sums = [
+                                sums[k] + sums[k + 1] if k + 1 < len(sums) else sums[k]
+                                for k in range(0, len(sums), 2)
+                            ]
+                        e_scr[q, t, at, :] = e_scr[q, t, at, :] + sums[0]
+                for u in range(REUSE):
+                    m_scr[q, j + u, at, :] = total[u]
+                return carry
+
+            lax.fori_loop(0, width // REUSE, cell, 0)
+            for loop, events in plan.items():
+                if loop % (rows // 8) == hb:
+
+                    @pl.when(q == loop // (rows // 8))
+                    def _(events=events):
+                        for colour, k in events:
+                            scatter.advance(colour, k)
+
+    @pl.when(step == CB)
+    def _():
+        load_up().wait()
+        tail_scr[...] = jnp.zeros_like(tail_scr)
+        add_vector(tail_scr, OFF_B1, as_blocks(extra[NOISE : NOISE + 1, :], FF))
+        add_vector(tail_scr, OFF_B2, as_blocks(extra[NOISE + 1 : NOISE + 2, :], C))
+        disco = jnp.concatenate(
+            [
+                lax.dot_general(
+                    t_scr[...], e_scr[q].reshape(TAPS * rows, LANES), (((0,), (0,)), ((), ())),
+                    preferred_element_type=F32, precision=HIGHEST,
+                )
+                for q in range(CB)
+            ],
+            1,
         )
         for k in range(K):
-            add_vector(tail_ref, OFF_DISCO + k * C, as_blocks(disco[k : k + 1, :], C))
+            add_vector(tail_scr, OFF_DISCO + k * C, as_blocks(disco[k : k + 1, :], C))
         ng = extra[0:NOISE, :]
         hi = ng.astype(BF16)
         mid = (ng - hi.astype(F32)).astype(BF16)
@@ -1109,227 +1245,107 @@
         parts = [dot(p, w1[...], ((1,), (1,))) for p in (hi, mid, lo)]
         gn = parts[0] + parts[1] + parts[2]
         for k in range(NOISE):
-            add_vector(tail_ref, OFF_NOISE + k * C, as_blocks(gn[k : k + 1, :], C))
+            add_vector(tail_scr, OFF_NOISE + k * C, as_blocks(gn[k : k + 1, :], C))
+
+    @pl.when(step > CB)
+    def _():
+        first = (step - CB - 1) * cells
+        live = iota((rows, C), 0) < height
+
+        def cell(i, total):
+            j = first + i
+            st = st_scr[j]
+            inv = st[:, 1:2]
+            normed = (x_scr[j].astype(F32) - st[:, :1]) * inv
+            gm = jnp.concatenate([m_scr[q, j] for q in range(CB)], 1)[:, :C]
+            gm = jnp.where(live, gm, 0.0)
+            total = total + gm * normed
+            v = gm * gvec
+            mean = jnp.mean(v, -1, keepdims=True)
+            mean_n = jnp.mean(v * normed, -1, keepdims=True)
+            up = jnp.where(live, up_scr[j].astype(F32), 0.0)
+            out_ref[i] = inv * (v - mean - normed * mean_n) + up
+            return total
+
+        gg_scr[:, :C] = lax.fori_loop(0, cells, cell, gg_scr[:, :C], unroll=4)
+
+    @pl.when(step == CB + chunks)
+    def _():
+        add_vector(tail_scr, OFF_GAIN, as_blocks(jnp.sum(gg_scr[...], 0, keepdims=True), C))
+        tail.scatter(tail_scr)
         taken = {e for events in plan.values() for e in events}
         for k in range(1, n):
             for colour in range(3):
                 if (colour, k) not in taken:
                     scatter.advance(colour, k)
-        part_ref[...] = scatter.result()
-        for q in range(CB):
-            pltpu.make_async_copy(m_scr.at[q], gm_ref.at[q], out_sem.at[q]).wait()
-
-
-def stencil_bwd(
-    mesh, height, mixed, gconv, cols, edge, corners, table, trowh, wd, extra, w1, shards,
-    tail_rows, chunks,
+        tail.finish(scatter.result(), grad_ref, norm_ref)
+
+
+def backward(
+    mesh, height, mixed, gconv, x, g, cols, edge, corners, table, trowh, wd, small, extra,
+    w1, shards, piece, chunks,
 ):
     width, rows, _ = mixed.shape
     cells = width // chunks
     shard_rows = shards.shape[-2]
     n = len(bit_list(mesh))
-    first = lambda i: jnp.where(i < chunks, i, chunks - 1)
+    devices = 1 << n
+    group = lambda i: jnp.clip(i - 1, 0, CB - 1)
+    last = lambda i: jnp.where(i <= CB, 0, i - CB - 1)
     sd = jax.ShapeDtypeStruct
-    by_first = lambda c: pl.BlockSpec((cells, rows, c), lambda i: (first(i), 0, 0))
+    dma = pltpu.SemaphoreType.DMA
     return pl.pallas_call(
-        partial(stencil_bwd_kernel, mesh, chunks, cells),
-        name="stencil_bwd",
-        grid=(chunks + 1,),
+        partial(backward_kernel, mesh, chunks, cells, width // edge.shape[0]),
+        name="backward",
+        grid=(1 + CB + chunks,),
         out_shape=(
-            sd((tail_rows, LANES), F32),
+            sd((width, rows, C), F32),
             sd((shard_rows, LANES), F32),
-            sd((CB, width, rows, LANES), F32),
+            sd((8, LANES), F32),
         ),
-        in_specs=[pl.BlockSpec(memory_space=pltpu.SMEM), by_first(CP), by_first(CP)]
-        + [vmem_spec()] * 8
+        in_specs=[
+            pl.BlockSpec(memory_space=pltpu.SMEM),
+            pl.BlockSpec((width, rows, LANES), lambda i: (0, 0, group(i))),
+            pl.BlockSpec((1, width * rows, LANES), lambda i: (group(i), 0, 0)),
+            any_spec(),
+            any_spec(),
+        ]
+        + [vmem_spec()] * 9
         + [any_spec()],
-        out_specs=(vmem_spec(), vmem_spec(), any_spec()),
+        out_specs=(
+            pl.BlockSpec((cells, rows, C), lambda i: (last(i), 0, 0)),
+            vmem_spec(),
+            vmem_spec(),
+        ),
         scratch_shapes=[
-            pltpu.VMEM((CB, (width + 2 * REACH) * SLOTS, LANES), F32),
+            pltpu.VMEM(x.shape, BF16),
+            pltpu.VMEM(x.shape, BF16),
+            pltpu.VMEM((width, rows, LANES), F32),
+            pltpu.VMEM(((width + 2 * REACH) * SLOTS, LANES), F32),
             pltpu.VMEM((CB, width, rows, LANES), F32),
-            pltpu.VMEM((TAPS, rows, CP), F32),
+            pltpu.VMEM((CB, TAPS, rows, LANES), F32),
             pltpu.VMEM((TAPS * rows, 16), F32),
-            pltpu.VMEM((TAPS, rows, CP), F32),
+            pltpu.VMEM((CB, TAPS, rows, LANES), F32),
+            pltpu.VMEM((rows, CP), F32),
+            pltpu.VMEM((devices * piece, LANES), F32),
             pltpu.VMEM(cols.shape, BF16),
             pltpu.VMEM(edge.shape, BF16),
             pltpu.VMEM(corners.shape, BF16),
+            pltpu.VMEM((devices, piece, LANES), F32),
+            pltpu.VMEM((devices, piece, LANES), F32),
+            pltpu.VMEM((piece + 1, LANES), F32),
+            pltpu.VMEM((devices, piece + 1, LANES), F32),
+            pltpu.VMEM((2 * shard_rows + devices * piece + 8, LANES), F32),
             pltpu.VMEM((2,) * (n - 1) + (shard_rows, LANES), F32),
         ]
         + [pltpu.VMEM((2,) * (n - 1 - k) + (shard_rows, LANES), F32) for k in range(n)]
-        + [
-            pltpu.SemaphoreType.DMA((3, n)),
-            pltpu.SemaphoreType.DMA((3, n)),
-            pltpu.SemaphoreType.DMA((8,)),
-            pltpu.SemaphoreType.DMA((8,)),
-            pltpu.SemaphoreType.DMA,
-            pltpu.SemaphoreType.DMA((CB,)),
-        ],
+        + [dma((3, n)), dma((3, n)), dma((8,)), dma((8,)), dma((2,)), dma((2,)), dma((3,))],
         compiler_params=params(
             dimension_semantics=("arbitrary",), collective_id=1, has_side_effects=True
         ),
-    )(height, mixed, gconv, cols, edge, corners, table, trowh, wd, extra, w1, shards)
-
-
-def norm_bwd_kernel(
-    height_ref, gm_ref, x_ref, mean_ref, inv_ref, g_ref, gain, tail_in, out_ref, tail_ref, gg_scr
-):
-    step = pl.program_id(0)
-    cells, rows, _ = x_ref.shape
-    gvec = gain[2:3, :C]
-    live = iota((rows, C), 0) < height_ref[0]
-
-    @pl.when(step == 0)
-    def _():
-        gg_scr[...] = jnp.zeros_like(gg_scr)
-
-    def cell(j, total):
-        inv = inv_ref[j][:, :1]
-        normed = (x_ref[j].astype(F32) - mean_ref[j][:, :1]) * inv
-        gm = jnp.concatenate([gm_ref[q, j] for q in range(CB)], 1)[:, :C]
-        gm = jnp.where(live, gm, 0.0)
-        total = total + gm * normed
-        v = gm * gvec
-        mean = jnp.mean(v, -1, keepdims=True)
-        mean_n = jnp.mean(v * normed, -1, keepdims=True)
-        up = jnp.where(live, g_ref[j].astype(F32), 0.0)
-        out_ref[j] = inv * (v - mean - normed * mean_n) + up
-        return total
-
-    gg_scr[:, :C] = lax.fori_loop(0, cells, cell, gg_scr[:, :C], unroll=2)
-
-    @pl.when(step == pl.num_programs(0) - 1)
-    def _():
-        tail_ref[...] = tail_in[...]
-        add_vector(tail_ref, OFF_GAIN, as_blocks(jnp.sum(gg_scr[...], 0, keepdims=True), C))
-
-
-def norm_bwd(height, gm, x, mean, inv, g, small, tail, chunks):
-    width, rows, _ = x.shape
-    cells = width // chunks
-    sd = jax.ShapeDtypeStruct
-    block = lambda c: pl.BlockSpec((cells, rows, c), lambda i: (i, 0, 0))
-    return pl.pallas_call(
-        norm_bwd_kernel,
-        name="norm_bwd",
-        grid=(chunks,),
-        out_shape=(sd((width, rows, C), F32), sd(tail.shape, F32)),
-        in_specs=[
-            pl.BlockSpec(memory_space=pltpu.SMEM),
-            pl.BlockSpec((CB, cells, rows, LANES), lambda i: (0, i, 0, 0)),
-            block(C),
-            block(LANES),
-            block(LANES),
-            block(C),
-            vmem_spec(),
-            vmem_spec(),
-        ],
-        out_specs=(block(C), vmem_spec()),
-        scratch_shapes=[pltpu.VMEM((rows, CP), F32)],
-        compiler_params=params(dimension_semantics=("arbitrary",)),
-    )(height, gm, x, mean, inv, g, small, tail)
-
-
-def tail_kernel(mesh, part_ref, tail_ref, grad_ref, scale_ref, got, msg, full, place, send, recv):
-    nlat, nlon = mesh.shape["lat"], mesh.shape["lon"]
-    n = nlat * nlon
-    lat, lon = lax.axis_index("lat"), lax.axis_index("lon")
-    me = lat * nlon + lon
-    piece = tail_ref.shape[1]
-    shard_rows = part_ref.shape[0]
-    barrier = pltpu.get_barrier_semaphore()
-
-    def others(body):
-        def step(i, carry):
-            body(lax.rem(me + i, n))
-            return carry
-
-        lax.fori_loop(1, n, step, 0)
-
-    def hello(d):
-        pl.semaphore_signal(
-            barrier, inc=1, device_id=(d // nlon, lax.rem(d, nlon)), device_id_type=MESH
-        )
-
-    others(hello)
-    pl.semaphore_wait(barrier, n - 1)
-
-    def scatter_piece(d):
-        pltpu.make_async_remote_copy(
-            src_ref=tail_ref.at[d],
-            dst_ref=got.at[me],
-            send_sem=send.at[0],
-            recv_sem=recv.at[0],
-            device_id=(d // nlon, lax.rem(d, nlon)),
-            device_id_type=MESH,
-        ).start()
-
-    def wait_all(buffer, k):
-        pltpu.make_async_remote_copy(
-            src_ref=buffer.at[pl.ds(0, n - 1)],
-            dst_ref=buffer.at[pl.ds(0, n - 1)],
-            send_sem=send.at[k],
-            recv_sem=recv.at[k],
-            device_id=(lat, lon),
-            device_id_type=MESH,
-        ).wait()
-
-    others(scatter_piece)
-    got[me] = tail_ref[me]
-    square = jnp.sum(part_ref[...] * part_ref[...])
-    wait_all(got, 0)
-
-    total = lax.fori_loop(
-        1, n, lambda i, acc: acc + got[lax.rem(i, n)], got[0]
+    )(
+        height, mixed, gconv, x, g, cols, edge, corners, table, trowh, wd, small, extra, w1, shards,
     )
-    square = square + jnp.sum(total * total)
-    msg[0:piece, :] = total
-    msg[piece : piece + 1, :] = jnp.broadcast_to(square, (1, LANES))
-
-    def share(d):
-        pltpu.make_async_remote_copy(
-            src_ref=msg,
-            dst_ref=full.at[me],
-            send_sem=send.at[1],
-            recv_sem=recv.at[1],
-            device_id=(d // nlon, lax.rem(d, nlon)),
-            device_id_type=MESH,
-        ).start()
-
-    others(share)
-    full[me] = msg[...]
-    place[...] = jnp.zeros_like(place)
-    wait_all(full, 1)
-
-    def take(d, acc):
-        place[pl.ds(shard_rows + d * piece, piece), :] = full[d, 0:piece, :]
-        return acc + full[d, piece : piece + 1, :]
-
-    squares = lax.fori_loop(0, n, take, jnp.zeros((1, LANES), F32))
-    start = jnp.clip(me * shard_rows - TAIL_ROW + shard_rows, 0, shard_rows + n * piece)
-    grad_ref[...] = part_ref[...] + place[pl.ds(start, shard_rows), :]
-    scale_ref[...] = jnp.broadcast_to(jnp.sqrt(squares), scale_ref.shape)
-
-
-def finish(mesh, part, tail):
-    n, piece, _ = tail.shape
-    shard_rows = part.shape[0]
-    sd = jax.ShapeDtypeStruct
-    return pl.pallas_call(
-        partial(tail_kernel, mesh),
-        name="small_gradients",
-        out_shape=(sd(part.shape, F32), sd((8, LANES), F32)),
-        in_specs=[vmem_spec()] * 2,
-        out_specs=(vmem_spec(),) * 2,
-        scratch_shapes=[
-            pltpu.VMEM((n, piece, LANES), F32),
-            pltpu.VMEM((piece + 1, LANES), F32),
-            pltpu.VMEM((n, piece + 1, LANES), F32),
-            pltpu.VMEM((2 * shard_rows + n * piece + 8, LANES), F32),
-            pltpu.SemaphoreType.DMA((2,)),
-            pltpu.SemaphoreType.DMA((2,)),
-        ],
-        compiler_params=params(collective_id=3, has_side_effects=True),
-    )(part, tail)
 
 
 def stencil_table(support_vals, support_lon):
@@ -1381,7 +1397,7 @@
         ],
         2,
     )
-    conv, mean, inv, mixed, w1, w2, wd, small, trowh = stencil_fwd(
+    conv, mixed, w1, w2, wd, small, trowh = stencil_fwd(
         mesh, height, x, share, cols, edge, corners, trow, table, aug, chunks
     )
     shards = (2,) * len(bit_list(mesh)) + (shard_rows, LANES)
@@ -1389,12 +1405,10 @@
         height, conv, g, x, w1, w2, small, shards, chunks
     )
     piece = -(-(flat_rows - TAIL_ROW) // devices)
-    tail, part, gm = stencil_bwd(
-        mesh, height, mixed, gconv, gcol, grow, gcorn, table, trowh, wd, extra, w1, packed,
-        devices * piece, chunks,
+    grad_in, grad, norm = backward(
+        mesh, height, mixed, gconv, x, g, gcol, grow, gcorn, table, trowh, wd, small,
+        extra, w1, packed, piece, 9,
     )
-    grad_in, tail = norm_bwd(height, gm, x, mean, inv, g, small, tail, chunks)
-    grad, norm = finish(mesh, part, tail.reshape(devices, piece, LANES))
     grad_part = grad.reshape(shard)
     grad_norm = norm[0, :1]
     factor = 0.01 / jnp.maximum(grad_norm, 0.01)

time: 293 us -> 278 us (0.949)
  Pallas kernels: 268 us -> 242 us
  local copies, waits for them, and re-layouts: 12.9 us -> 23.6 us
    pallas_call x3 -> x1, Pallas kernels: 103 us -> 88.6 us  [backward(): pl.pallas_call(partial(backward_kernel, mesh, chunks, cells, width // edg...]
    pallas_call x1, Pallas kernels: 102 us -> 90.6 us  [mlp(): pl.pallas_call(partial(mlp_kernel, blocks), name='mlp', grid=(blocks,), o...]
    unnamed x23 -> x24, local copies, waits for them, and re-layouts: 1.45 us -> 12.1 us
where the time goes in v5:
time: 278 us
  Pallas kernels  242 us (87%)
  local copies, waits for them, and re-layouts  23.6 us (8%)
  other arithmetic  8.3 us (3%)
  between operations  3.61 us (1%)
    pallas_call x1, Pallas kernels, mlp(): pl.pallas_call(partial(mlp_kernel, blocks), name='mlp', grid=(blocks,), o...  90.6 us
    pallas_call x1, Pallas kernels, backward(): pl.pallas_call(partial(backward_kernel, mesh, chunks, cells, width // edg...  88.6 us
    pallas_call x1, Pallas kernels, stencil_fwd(): pl.pallas_call(partial(stencil_fwd_kernel, mesh, chunks, cells), name='st...  62.8 us
    unnamed x24, local copies, waits for them, and re-layouts  12.1 us

profile of v5, /device:TPU:0, one launch (start us, length us, event | category | flops | bytes accessed | tf_op | source)
XLA Modules:
  0.0 277.5 jit_solution(11549654430812459439)
XLA Ops:
  0.6 1.2 dynamic_slice.11.height_ref
  1.9 1.6 convert_bitcast_fusion.share
  3.5 0.9 slice_bitcast_fusion.1
  4.4 0.7 pad_maximum_fusion.cols
  6.4 3.5 %dynamic-slice_bitcast_fusion = (bf16[180,1,641]{2,1,0:T(2,128)(2,1)S(1)}, bf16[180,641]{1,0:T(8,128)(2,1)S(1)}) fusion(bf16[24,180,641]{2,0,1:T(8,128)(2,1)} %param.11, s32[]{:T(128)S(6)} %select_n.14), kind=kLoop, calls=%fused_computation.3 | loop fusion | bytes 692284 | tf_op jit(solution)/shard_map/jit(dynamic_index_in_dim)/dynamic_slice | solution.py:1386
  9.9 0.1 stack.38
  10.0 0.0 copy-start.8
  10.0 0.0 copy-start.9
  10.0 3.4 %fusion.4 = (bf16[180,1,641]{2,1,0:T(2,128)(2,1)S(1)}, bf16[180,641]{1,0:T(8,128)(2,1)S(1)}) fusion(bf16[180,24,641]{2,1,0:T(8,128)(2,1)} %bitcast.46), kind=kLoop, calls=%fused_computation.26 | loop fusion | bytes 692280 | tf_op jit(solution)/shard_map/slice | solution.py:1386
  13.4 0.0 copy-start.7
  13.4 0.1 stack.37
  13.5 0.9 maximum_bitcast_fusion.edge
  14.4 0.6 copy.42.corners
  15.1 0.0 copy-done.8
  15.1 0.0 copy-done.9
  15.2 0.1 broadcast_compare_fusion
  15.2 0.2 select_reduce_fusion
  15.5 0.2 copy.38
  15.7 0.0 copy-start
  15.7 0.6 select_maximum_fusion.trow
  16.4 0.0 copy-done.7
  16.4 0.7 copy.41
  17.1 0.1 pad.13.clone
  17.2 0.1 pad.12.clone
  17.2 1.6 maximum_maximum_fusion.aug
  18.8 0.0 copy-done
  18.8 62.8 %stencil_fwd.1 = (bf16[180,24,768]{2,1,0:T(8,128)(2,1)}, bf16[180,24,768]{2,1,0:T(8,128)(2,1)}, bf16[768,1408]{1,0:T(8,128)(2,1)}, bf16[1408,768]{1,0:T(8,128)(2...) custom-call(s32[1]{0:T(128)} %dynamic_slice.11.height_ref, bf16[180,24,641]{2,1,0:T(8,128)(2,1)} %bitcast.47, ...), custom_call_target="tpu_custom_call" | custom-call | tf_op jit(solution)/shard_map/stencil_fwd/pallas_call | solution.py:600
  81.7 90.6 %mlp.1 = (bf16[180,24,641]{2,1,0:T(8,128)(2,1)}, f32[6,4320,128]{2,1,0:T(8,128)}, bf16[6,2,32,768]{3,2,1,0:T(8,128)(2,1)}, bf16[2,2,24,768]{3,2,1,0:T(8,128)(2,1...) custom-call(s32[1]{0:T(128)} %dynamic_slice.11.height_ref, ...), custom_call_target="tpu_custom_call" | custom-call | flops 42600140800 | bytes 50000000 | tf_op jit(solution)/shard_map/mlp/pallas_call | solution.py:884
  172.3 0.0 copy-start.2
  172.3 0.0 copy-start.4
  172.3 0.0 copy-start.5
  172.3 0.0 copy-start.6
  172.3 88.6 %backward.1 = (f32[180,24,641]{2,1,0:T(8,128)}, f32[405,128]{1,0:T(8,128)}, f32[8,128]{1,0:T(8,128)}) custom-call(s32[1]{0:T(128)} %dynamic_slice.11.height_ref, bf16[180,24,768]{2,1,0:T(8,128)(2,1)} %get-tuple-element.31.mix_ref, f32[6,4320,128]{2,1,0:T(8,128)} %get-tuple-element.32.gconv_ref, bf16[180,24,641]{2,1,0:T(8,128)(2,1)} %bitcast.49, ...), custom_call_target="tpu_custom_call" | custom-call | tf_op jit(solution)/shard_map/backward/pallas_call | solution.py:1297
  260.9 1.2 slice.27
  263.5 0.0 copy-done.2
  263.6 0.0 copy-done.4
  263.6 0.0 copy-done.5
  263.6 1.8 fusion.2
  265.4 0.0 copy-start.1
  265.4 0.0 copy-done.6
  265.4 0.7 multiply_add_fusion
  266.1 0.0 copy-start.3
  266.1 10.7 %copy.51 = f32[24,180,641]{2,0,1:T(8,128)} copy(f32[24,180,641]{2,0,1:T(8,128)} %bitcast.50) | data formatting | bytes 22152960
  276.8 0.0 copy-done.1
  276.8 0.0 copy-done.3
  276.8 0.7 copy.52
  (13 shorter events, 0.2 us)
Async XLA Ops:
  10.0 5.1 %copy-start.8 = (f32[24,12,9]{0,1,2:T(8,128)S(1)}, f32[24,12,9]{0,1,2:T(8,128)}, u32[]{:S(2)}) copy-start(f32[24,12,9]{0,1,2:T(8,128)} %param.16) | copy-start | bytes 31108
  10.0 5.1 %copy-start.9 = (s32[24,12]{0,1:T(8,128)S(1)}, s32[24,12]{0,1:T(8,128)}, u32[]{:S(2)}) copy-start(s32[24,12]{0,1:T(8,128)} %param.15) | copy-start | bytes 3460
  13.4 3.0 %copy-start.7 = (bf16[8,24,180]{2,1,0:T(8,128)(2,1)S(1)}, bf16[8,24,180]{2,1,0:T(8,128)(2,1)}, u32[]{:S(2)}) copy-start(bf16[8,24,180]{2,1,0:T(8,128)(2,1)} %param.12) | copy-start | bytes 207364
  15.7 3.2 %copy-start = (f32[360,16]{1,0:T(8,128)}, f32[360,16]{1,0:T(8,128)S(1)}, u32[]{:S(2)}) copy-start(f32[360,16]{1,0:T(8,128)S(1)} %pad.8.table) | copy-start | bytes 69124
  172.3 91.3 %copy-start.2 = (f32[51840]{0:T(1024)S(1)}, f32[51840]{0:T(1024)}, u32[]{:S(2)}) copy-start(f32[51840]{0:T(1024)} %param.17) | copy-start | bytes 622084
  172.3 91.3 %copy-start.4 = (f32[51840]{0:T(1024)S(1)}, f32[51840]{0:T(1024)}, u32[]{:S(2)}) copy-start(f32[51840]{0:T(1024)} %param.19) | copy-start | bytes 622084
  172.3 91.3 %copy-start.5 = (f32[51840]{0:T(1024)S(1)}, f32[51840]{0:T(1024)}, u32[]{:S(2)}) copy-start(f32[51840]{0:T(1024)} %param.18) | copy-start | bytes 622084
  172.3 93.1 %copy-start.6 = (f32[51840]{0:T(1024)S(1)}, f32[51840]{0:T(1024)}, u32[]{:S(2)}) copy-start(f32[51840]{0:T(1024)} %param.20) | copy-start | bytes 622084
  265.4 11.4 %copy-start.1 = (f32[51840]{0:T(1024)}, f32[51840]{0:T(1024)S(1)}, u32[]{:S(2)}) copy-start(f32[51840]{0:T(1024)S(1)} %get-tuple-element.70) | copy-start | bytes 622084
  266.1 10.7 %copy-start.3 = (f32[405,128]{1,0:T(8,128)S(1)}, f32[405,128]{1,0:T(8,128)}, u32[]{:S(2)}) copy-start(f32[405,128]{1,0:T(8,128)} %get-tuple-element.41) | copy-start | bytes 622084

commit v6 on v5

--- a/solution.py
+++ b/solution.py
@@ -459,24 +459,42 @@
 
     @pl.when(step == chunks)
     def _():
-        if 0 in plan:
-            gather.advance(0)
-        lat, _, nlat, *_ = neighbours()
-        wait_halo(halos())
-        keep = (lat > 0, lat < nlat - 1)
-        for r in range(2):
-            trowh[r] = jnp.where(keep[r], trh[r], 0.0)
-
         base = gather.roots[0] * shard_rows + gather.start
         count = shard_rows - gather.start
         eflat[...] = jnp.zeros_like(eflat)
         for r in range(len(gather.roots)):
             eflat[r * count : (r + 1) * count, :] = early[r].astype(F32)
         unpack_small(eflat, base, wn, wd, small, wnf)
+        if 0 in plan:
+            gather.advance(0)
         k_scr[...] = jnp.dot(
             table[...], wd[...], preferred_element_type=F32, precision=HIGHEST
         ).reshape(k_scr.shape)
         gvec = small[2:3, :C]
+        groups = [(q, q * LANES, min((q + 1) * LANES, C)) for q in range(CB)]
+        hrow = iota((rows, LANES), 0)
+        lanes = slice((CB - 1) * LANES, CB * LANES)
+        mix_scr[:, :, lanes] = jnp.zeros((width, rows, LANES), BF16)
+
+        def scale(i, carry):
+            for u in range(REUSE):
+                column = i * REUSE + u
+                body = pl.ds((column + REACH) * SLOTS + 1, rows)
+                for q, lo, hi in groups:
+                    wide = slice(0, hi - lo)
+                    v = rounded(m_scr[q, body, wide] * gvec[:, lo:hi])
+                    v = jnp.where(hrow[:, wide] < height, v, 0.0)
+                    mix_scr[column, :, lo:hi] = v.astype(BF16)
+                    m_scr[q, body, wide] = v
+            return carry
+
+        lax.fori_loop(0, width // REUSE, scale, 0)
+        mix_copy().start()
+        lat, _, nlat, *_ = neighbours()
+        wait_halo(halos())
+        keep = (lat > 0, lat < nlat - 1)
+        for r in range(2):
+            trowh[r] = jnp.where(keep[r], trh[r], 0.0)
 
         def mix(v):
             center, inv = norm_parts(v.astype(F32))
@@ -487,23 +505,17 @@
 
         def put(column, top, low, fresh=None):
             at = column * SLOTS
-            hrow = iota((rows, LANES), 0)
-            for q in range(CB):
-                lo, hi = q * LANES, min((q + 1) * LANES, C)
+            for q, lo, hi in groups:
                 body = pl.ds(at + 1, rows)
                 wide = slice(0, hi - lo)
                 if fresh is None:
-                    v = rounded(m_scr[q, body, wide] * gvec[:, lo:hi])
-                    v = jnp.where(hrow[:, wide] < height, v, 0.0)
-                    mix_scr[column - REACH, :, lo:hi] = v.astype(BF16)
+                    v = m_scr[q, body, wide]
                 else:
                     v = jnp.where(hrow[:, wide] < height, fresh[:, lo:hi], 0.0)
                 m_scr[q, body, wide] = jnp.where(hrow[:, wide] == height, low[:, lo:hi], v)
                 m_scr[q, pl.ds(at, 1), wide] = top[:, lo:hi]
                 m_scr[q, pl.ds(at + rows + 1, 1), wide] = low[:, lo:hi]
 
-        lanes = slice((CB - 1) * LANES, CB * LANES)
-        mix_scr[:, :, lanes] = jnp.zeros((width, rows, LANES), BF16)
         for side in range(2):
             top, low = beside(lambda r: cornh[r, side])
             for i in range(REACH):
@@ -517,7 +529,6 @@
             return carry
 
         lax.fori_loop(0, chunks, strip, 0)
-        mix_copy().start()
 
     for k, (at, loop) in plan.items():
         if k > 0 and loop < 0:
@@ -1062,7 +1073,7 @@
         self.got[self.me] = self.pieces[self.me]
         self.place[...] = jnp.zeros_like(self.place)
 
-    def finish(self, part, grad_ref, norm_ref):
+    def finish(self, part, own_gain, grad_ref, norm_ref):
         n, piece = self.n, self.pieces.shape[1]
         shard_rows = part.shape[0]
         square = jnp.sum(part * part)
@@ -1071,15 +1082,19 @@
         square = square + jnp.sum(total * total)
         self.msg[0:piece, :] = total
         self.msg[piece : piece + 1, :] = jnp.broadcast_to(square, (1, LANES))
+        self.msg[piece + 1 :, :] = own_gain
         self.others(lambda d: self.msg, self.full, 1)
         self.full[self.me] = self.msg[...]
         self.wait_all(self.full, 1)
 
         def take(d, acc):
             self.place[pl.ds(shard_rows + d * piece, piece), :] = self.full[d, 0:piece, :]
-            return acc + self.full[d, piece : piece + 1, :]
-
-        squares = lax.fori_loop(0, n, take, jnp.zeros((1, LANES), F32))
+            return acc + self.full[d, piece:, :]
+
+        sums = lax.fori_loop(0, n, take, jnp.zeros((1 + CB, LANES), F32))
+        gain = sums[1:]
+        add_vector(self.place, OFF_GAIN + shard_rows * LANES, gain)
+        squares = sums[:1] + jnp.sum(gain * gain)
         start = jnp.clip(self.me * shard_rows - TAIL_ROW + shard_rows, 0, shard_rows + n * piece)
         grad_ref[...] = part + self.place[pl.ds(start, shard_rows), :]
         norm_ref[...] = jnp.broadcast_to(jnp.sqrt(squares), norm_ref.shape)
@@ -1141,6 +1156,17 @@
             return carry
 
         lax.fori_loop(0, width, stats, 0, unroll=10)
+        tail_scr[...] = jnp.zeros_like(tail_scr)
+        add_vector(tail_scr, OFF_B1, as_blocks(extra[NOISE : NOISE + 1, :], FF))
+        add_vector(tail_scr, OFF_B2, as_blocks(extra[NOISE + 1 : NOISE + 2, :], C))
+        ng = extra[0:NOISE, :]
+        hi = ng.astype(BF16)
+        mid = (ng - hi.astype(F32)).astype(BF16)
+        lo = (ng - hi.astype(F32) - mid.astype(F32)).astype(BF16)
+        parts = [dot(p, w1[...], ((1,), (1,))) for p in (hi, mid, lo)]
+        gn = parts[0] + parts[1] + parts[2]
+        for k in range(NOISE):
+            add_vector(tail_scr, OFF_NOISE + k * C, as_blocks(gn[k : k + 1, :], C))
 
     @pl.when(step == 1)
     def _():
@@ -1223,9 +1249,6 @@
     @pl.when(step == CB)
     def _():
         load_up().wait()
-        tail_scr[...] = jnp.zeros_like(tail_scr)
-        add_vector(tail_scr, OFF_B1, as_blocks(extra[NOISE : NOISE + 1, :], FF))
-        add_vector(tail_scr, OFF_B2, as_blocks(extra[NOISE + 1 : NOISE + 2, :], C))
         disco = jnp.concatenate(
             [
                 lax.dot_general(
@@ -1238,14 +1261,7 @@
         )
         for k in range(K):
             add_vector(tail_scr, OFF_DISCO + k * C, as_blocks(disco[k : k + 1, :], C))
-        ng = extra[0:NOISE, :]
-        hi = ng.astype(BF16)
-        mid = (ng - hi.astype(F32)).astype(BF16)
-        lo = (ng - hi.astype(F32) - mid.astype(F32)).astype(BF16)
-        parts = [dot(p, w1[...], ((1,), (1,))) for p in (hi, mid, lo)]
-        gn = parts[0] + parts[1] + parts[2]
-        for k in range(NOISE):
-            add_vector(tail_scr, OFF_NOISE + k * C, as_blocks(gn[k : k + 1, :], C))
+        tail.scatter(tail_scr)
 
     @pl.when(step > CB)
     def _():
@@ -1271,14 +1287,13 @@
 
     @pl.when(step == CB + chunks)
     def _():
-        add_vector(tail_scr, OFF_GAIN, as_blocks(jnp.sum(gg_scr[...], 0, keepdims=True), C))
-        tail.scatter(tail_scr)
+        own_gain = as_blocks(jnp.sum(gg_scr[...], 0, keepdims=True), C)
         taken = {e for events in plan.values() for e in events}
         for k in range(1, n):
             for colour in range(3):
                 if (colour, k) not in taken:
                     scatter.advance(colour, k)
-        tail.finish(scatter.result(), grad_ref, norm_ref)
+        tail.finish(scatter.result(), own_gain, grad_ref, norm_ref)
 
 
 def backward(
@@ -1333,8 +1348,8 @@
             pltpu.VMEM(corners.shape, BF16),
             pltpu.VMEM((devices, piece, LANES), F32),
             pltpu.VMEM((devices, piece, LANES), F32),
-            pltpu.VMEM((piece + 1, LANES), F32),
-            pltpu.VMEM((devices, piece + 1, LANES), F32),
+            pltpu.VMEM((piece + 1 + CB, LANES), F32),
+            pltpu.VMEM((devices, piece + 1 + CB, LANES), F32),
             pltpu.VMEM((2 * shard_rows + devices * piece + 8, LANES), F32),
             pltpu.VMEM((2,) * (n - 1) + (shard_rows, LANES), F32),
         ]

time: 278 us -> 273 us (0.982)
  Pallas kernels: 242 us -> 237 us
    pallas_call x1, Pallas kernels: 88.6 us -> 83.6 us  [backward(): pl.pallas_call(partial(backward_kernel, mesh, chunks, cells, width // edg...]
where the time goes in v6:
time: 273 us; the launch traced here: 272 us
  Pallas kernels  237 us (87%)
  local copies, waits for them, and re-layouts  23.6 us (9%)
  other arithmetic  8.3 us (3%)
  between operations  3.61 us (1%)
    pallas_call x1, Pallas kernels, mlp(): pl.pallas_call(partial(mlp_kernel, blocks), name='mlp', grid=(blocks,), o...  90.6 us
    pallas_call x1, Pallas kernels, backward(): pl.pallas_call(partial(backward_kernel, mesh, chunks, cells, width // edg...  83.6 us
    pallas_call x1, Pallas kernels, stencil_fwd(): pl.pallas_call(partial(stencil_fwd_kernel, mesh, chunks, cells), name='st...  62.7 us
    unnamed x24, local copies, waits for them, and re-layouts  12.1 us

profile of v6, /device:TPU:0, one launch (start us, length us, event | category | flops | bytes accessed | tf_op | source)
XLA Modules:
  0.0 272.4 jit_solution(8734875822560749769)
XLA Ops:
  0.6 1.2 dynamic_slice.11.height_ref
  1.9 1.6 convert_bitcast_fusion.share
  3.5 0.9 slice_bitcast_fusion.1
  4.4 0.7 pad_maximum_fusion.cols
  6.4 3.5 %dynamic-slice_bitcast_fusion = (bf16[180,1,641]{2,1,0:T(2,128)(2,1)S(1)}, bf16[180,641]{1,0:T(8,128)(2,1)S(1)}) fusion(bf16[24,180,641]{2,0,1:T(8,128)(2,1)} %param.11, s32[]{:T(128)S(6)} %select_n.14), kind=kLoop, calls=%fused_computation.3 | loop fusion | bytes 692284 | tf_op jit(solution)/shard_map/jit(dynamic_index_in_dim)/dynamic_slice | solution.py:1401
  9.9 0.1 stack.38
  10.0 0.0 copy-start.8
  10.0 0.0 copy-start.9
  10.0 3.4 %fusion.4 = (bf16[180,1,641]{2,1,0:T(2,128)(2,1)S(1)}, bf16[180,641]{1,0:T(8,128)(2,1)S(1)}) fusion(bf16[180,24,641]{2,1,0:T(8,128)(2,1)} %bitcast.46), kind=kLoop, calls=%fused_computation.26 | loop fusion | bytes 692280 | tf_op jit(solution)/shard_map/slice | solution.py:1401
  13.4 0.0 copy-start.7
  13.4 0.1 stack.37
  13.5 0.9 maximum_bitcast_fusion.edge
  14.4 0.6 copy.42.corners
  15.1 0.0 copy-done.8
  15.1 0.0 copy-done.9
  15.2 0.1 broadcast_compare_fusion
  15.2 0.2 select_reduce_fusion
  15.5 0.2 copy.38
  15.7 0.0 copy-start
  15.7 0.6 select_maximum_fusion.trow
  16.4 0.0 copy-done.7
  16.4 0.7 copy.41
  17.1 0.1 pad.13.clone
  17.2 0.1 pad.12.clone
  17.2 1.6 maximum_maximum_fusion.aug
  18.8 0.0 copy-done
  18.8 62.7 %stencil_fwd.1 = (bf16[180,24,768]{2,1,0:T(8,128)(2,1)}, bf16[180,24,768]{2,1,0:T(8,128)(2,1)}, bf16[768,1408]{1,0:T(8,128)(2,1)}, bf16[1408,768]{1,0:T(8,128)(2...) custom-call(s32[1]{0:T(128)} %dynamic_slice.11.height_ref, bf16[180,24,641]{2,1,0:T(8,128)(2,1)} %bitcast.47, ...), custom_call_target="tpu_custom_call" | custom-call | tf_op jit(solution)/shard_map/stencil_fwd/pallas_call | solution.py:611
  81.5 90.6 %mlp.1 = (bf16[180,24,641]{2,1,0:T(8,128)(2,1)}, f32[6,4320,128]{2,1,0:T(8,128)}, bf16[6,2,32,768]{3,2,1,0:T(8,128)(2,1)}, bf16[2,2,24,768]{3,2,1,0:T(8,128)(2,1...) custom-call(s32[1]{0:T(128)} %dynamic_slice.11.height_ref, ...), custom_call_target="tpu_custom_call" | custom-call | flops 42600140800 | bytes 50000000 | tf_op jit(solution)/shard_map/mlp/pallas_call | solution.py:895
  172.1 0.0 copy-start.2
  172.2 0.0 copy-start.4
  172.2 0.0 copy-start.5
  172.2 0.0 copy-start.6
  172.2 83.6 %backward.1 = (f32[180,24,641]{2,1,0:T(8,128)}, f32[405,128]{1,0:T(8,128)}, f32[8,128]{1,0:T(8,128)}) custom-call(s32[1]{0:T(128)} %dynamic_slice.11.height_ref, bf16[180,24,768]{2,1,0:T(8,128)(2,1)} %get-tuple-element.31.mix_ref, f32[6,4320,128]{2,1,0:T(8,128)} %get-tuple-element.32.gconv_ref, bf16[180,24,641]{2,1,0:T(8,128)(2,1)} %bitcast.49, ...), custom_call_target="tpu_custom_call" | custom-call | tf_op jit(solution)/shard_map/backward/pallas_call | solution.py:1312
  255.8 1.2 slice.27
  258.5 0.0 copy-done.2
  258.5 0.0 copy-done.4
  258.5 0.0 copy-done.5
  258.5 1.8 fusion.2
  260.3 0.0 copy-start.1
  260.3 0.0 copy-done.6
  260.3 0.7 multiply_add_fusion
  261.0 0.0 copy-start.3
  261.0 10.7 %copy.51 = f32[24,180,641]{2,0,1:T(8,128)} copy(f32[24,180,641]{2,0,1:T(8,128)} %bitcast.50) | data formatting | bytes 22152960
  271.7 0.0 copy-done.1
  271.7 0.0 copy-done.3
  271.7 0.7 copy.52
  (13 shorter events, 0.2 us)
Async XLA Ops:
  10.0 5.1 %copy-start.8 = (f32[24,12,9]{0,1,2:T(8,128)S(1)}, f32[24,12,9]{0,1,2:T(8,128)}, u32[]{:S(2)}) copy-start(f32[24,12,9]{0,1,2:T(8,128)} %param.16) | copy-start | bytes 31108
  10.0 5.1 %copy-start.9 = (s32[24,12]{0,1:T(8,128)S(1)}, s32[24,12]{0,1:T(8,128)}, u32[]{:S(2)}) copy-start(s32[24,12]{0,1:T(8,128)} %param.15) | copy-start | bytes 3460
  13.4 3.0 %copy-start.7 = (bf16[8,24,180]{2,1,0:T(8,128)(2,1)S(1)}, bf16[8,24,180]{2,1,0:T(8,128)(2,1)}, u32[]{:S(2)}) copy-start(bf16[8,24,180]{2,1,0:T(8,128)(2,1)} %param.12) | copy-start | bytes 207364
  15.7 3.2 %copy-start = (f32[360,16]{1,0:T(8,128)}, f32[360,16]{1,0:T(8,128)S(1)}, u32[]{:S(2)}) copy-start(f32[360,16]{1,0:T(8,128)S(1)} %pad.8.table) | copy-start | bytes 69124
  172.1 86.3 %copy-start.2 = (f32[51840]{0:T(1024)S(1)}, f32[51840]{0:T(1024)}, u32[]{:S(2)}) copy-start(f32[51840]{0:T(1024)} %param.17) | copy-start | bytes 622084
  172.2 86.3 %copy-start.4 = (f32[51840]{0:T(1024)S(1)}, f32[51840]{0:T(1024)}, u32[]{:S(2)}) copy-start(f32[51840]{0:T(1024)} %param.19) | copy-start | bytes 622084
  172.2 86.3 %copy-start.5 = (f32[51840]{0:T(1024)S(1)}, f32[51840]{0:T(1024)}, u32[]{:S(2)}) copy-start(f32[51840]{0:T(1024)} %param.18) | copy-start | bytes 622084
  172.2 88.1 %copy-start.6 = (f32[51840]{0:T(1024)S(1)}, f32[51840]{0:T(1024)}, u32[]{:S(2)}) copy-start(f32[51840]{0:T(1024)} %param.20) | copy-start | bytes 622084
  260.3 11.4 %copy-start.1 = (f32[51840]{0:T(1024)}, f32[51840]{0:T(1024)S(1)}, u32[]{:S(2)}) copy-start(f32[51840]{0:T(1024)S(1)} %get-tuple-element.70) | copy-start | bytes 622084
  261.0 10.7 %copy-start.3 = (f32[405,128]{1,0:T(8,128)S(1)}, f32[405,128]{1,0:T(8,128)}, u32[]{:S(2)}) copy-start(f32[405,128]{1,0:T(8,128)} %get-tuple-element.41) | copy-start | bytes 622084

commit v7 on v6

--- a/solution.py
+++ b/solution.py
@@ -311,7 +311,7 @@
         self.share, self.buf, self.early = share, buf, early
         self.send, self.recv, self.bsend, self.brecv = send, recv, bsend, brecv
         rows = share.shape[0]
-        cut = (rows * 2 // 3 + 15) // 16 * 16
+        cut = (rows // 2 + 15) // 16 * 16
         self.spans = [(0, cut), (cut, rows - cut)]
         self.roots, self.start = early_shards(1 << self.n, rows)
 
@@ -836,7 +836,12 @@
         return carry
 
     lax.fori_loop(0, FP // WIDE, third, 0)
-    weights(FP // WIDE * WIDE, FP % WIDE)
+    spare_lanes = pl.ds(main, LANES)
+    r1 = dot(conv_t[...], gh[:, spare_lanes])
+    r2 = dot(act[:, main : main + 16], g_scr[...], ((0,), (0,)))
+    one[FB - 1] += r1
+    for q in range(CB):
+        two[q, main + 8 : main + 24, :] += r2[:, q * LANES : (q + 1) * LANES]
 
     whole, left = divmod(cells, 8)
     for r, slot in ((0, 0), (1, height - 1)):

time: 273 us -> 268 us (0.982)
  Pallas kernels: 237 us -> 233 us
    pallas_call x1, Pallas kernels: 62.7 us -> 59.9 us  [stencil_fwd(): pl.pallas_call(partial(stencil_fwd_kernel, mesh, chunks, cells), name='st...]
where the time goes in v7:
time: 268 us
  Pallas kernels  233 us (87%)
  local copies, waits for them, and re-layouts  23.6 us (9%)
  other arithmetic  8.3 us (3%)
  between operations  3.61 us (1%)
    pallas_call x1, Pallas kernels, mlp(): pl.pallas_call(partial(mlp_kernel, blocks), name='mlp', grid=(blocks,), o...  90.4 us
    pallas_call x1, Pallas kernels, backward(): pl.pallas_call(partial(backward_kernel, mesh, chunks, cells, width // edg...  82.2 us
    pallas_call x1, Pallas kernels, stencil_fwd(): pl.pallas_call(partial(stencil_fwd_kernel, mesh, chunks, cells), name='st...  59.9 us
    unnamed x24, local copies, waits for them, and re-layouts  12.1 us

profile of v7, /device:TPU:0, one launch (start us, length us, event | category | flops | bytes accessed | tf_op | source)
XLA Modules:
  0.0 268.0 jit_solution(1104500528967620908)
XLA Ops:
  0.6 1.2 dynamic_slice.11.height_ref
  1.9 1.6 convert_bitcast_fusion.share
  3.5 0.9 slice_bitcast_fusion.1
  4.4 0.7 pad_maximum_fusion.cols
  6.4 3.5 %dynamic-slice_bitcast_fusion = (bf16[180,1,641]{2,1,0:T(2,128)(2,1)S(1)}, bf16[180,641]{1,0:T(8,128)(2,1)S(1)}) fusion(bf16[24,180,641]{2,0,1:T(8,128)(2,1)} %param.11, s32[]{:T(128)S(6)} %select_n.14), kind=kLoop, calls=%fused_computation.3 | loop fusion | bytes 692284 | tf_op jit(solution)/shard_map/jit(dynamic_index_in_dim)/dynamic_slice | solution.py:1406
  9.9 0.1 stack.38
  10.0 0.0 copy-start.8
  10.0 0.0 copy-start.9
  10.0 3.4 %fusion.4 = (bf16[180,1,641]{2,1,0:T(2,128)(2,1)S(1)}, bf16[180,641]{1,0:T(8,128)(2,1)S(1)}) fusion(bf16[180,24,641]{2,1,0:T(8,128)(2,1)} %bitcast.46), kind=kLoop, calls=%fused_computation.26 | loop fusion | bytes 692280 | tf_op jit(solution)/shard_map/slice | solution.py:1406
  13.4 0.0 copy-start.7
  13.4 0.1 stack.37
  13.5 0.9 maximum_bitcast_fusion.edge
  14.4 0.6 copy.42.corners
  15.1 0.0 copy-done.8
  15.1 0.0 copy-done.9
  15.2 0.1 broadcast_compare_fusion
  15.2 0.2 select_reduce_fusion
  15.5 0.2 copy.38
  15.7 0.0 copy-start
  15.7 0.6 select_maximum_fusion.trow
  16.4 0.0 copy-done.7
  16.4 0.7 copy.41
  17.1 0.1 pad.13.clone
  17.2 0.1 pad.12.clone
  17.2 1.6 maximum_maximum_fusion.aug
  18.8 0.0 copy-done
  18.8 59.9 %stencil_fwd.1 = (bf16[180,24,768]{2,1,0:T(8,128)(2,1)}, bf16[180,24,768]{2,1,0:T(8,128)(2,1)}, bf16[768,1408]{1,0:T(8,128)(2,1)}, bf16[1408,768]{1,0:T(8,128)(2...) custom-call(s32[1]{0:T(128)} %dynamic_slice.11.height_ref, bf16[180,24,641]{2,1,0:T(8,128)(2,1)} %bitcast.47, ...), custom_call_target="tpu_custom_call" | custom-call | tf_op jit(solution)/shard_map/stencil_fwd/pallas_call | solution.py:611
  78.7 90.4 %mlp.1 = (bf16[180,24,641]{2,1,0:T(8,128)(2,1)}, f32[6,4320,128]{2,1,0:T(8,128)}, bf16[6,2,32,768]{3,2,1,0:T(8,128)(2,1)}, bf16[2,2,24,768]{3,2,1,0:T(8,128)(2,1...) custom-call(s32[1]{0:T(128)} %dynamic_slice.11.height_ref, ...), custom_call_target="tpu_custom_call" | custom-call | flops 42600140800 | bytes 50000000 | tf_op jit(solution)/shard_map/mlp/pallas_call | solution.py:900
  169.1 0.0 copy-start.2
  169.1 0.0 copy-start.4
  169.1 0.0 copy-start.5
  169.1 0.0 copy-start.6
  169.2 82.2 %backward.1 = (f32[180,24,641]{2,1,0:T(8,128)}, f32[405,128]{1,0:T(8,128)}, f32[8,128]{1,0:T(8,128)}) custom-call(s32[1]{0:T(128)} %dynamic_slice.11.height_ref, bf16[180,24,768]{2,1,0:T(8,128)(2,1)} %get-tuple-element.31.mix_ref, f32[6,4320,128]{2,1,0:T(8,128)} %get-tuple-element.32.gconv_ref, bf16[180,24,641]{2,1,0:T(8,128)(2,1)} %bitcast.49, ...), custom_call_target="tpu_custom_call" | custom-call | tf_op jit(solution)/shard_map/backward/pallas_call | solution.py:1317
  251.4 1.2 slice.27
  254.0 0.0 copy-done.2
  254.0 0.0 copy-done.4
  254.1 0.0 copy-done.5
  254.1 1.8 fusion.2
  255.9 0.0 copy-start.1
  255.9 0.0 copy-done.6
  255.9 0.7 multiply_add_fusion
  256.6 0.0 copy-start.3
  256.6 10.7 %copy.51 = f32[24,180,641]{2,0,1:T(8,128)} copy(f32[24,180,641]{2,0,1:T(8,128)} %bitcast.50) | data formatting | bytes 22152960
  267.3 0.0 copy-done.1
  267.3 0.0 copy-done.3
  267.3 0.7 copy.52
  (13 shorter events, 0.2 us)
Async XLA Ops:
  10.0 5.1 %copy-start.8 = (f32[24,12,9]{0,1,2:T(8,128)S(1)}, f32[24,12,9]{0,1,2:T(8,128)}, u32[]{:S(2)}) copy-start(f32[24,12,9]{0,1,2:T(8,128)} %param.16) | copy-start | bytes 31108
  10.0 5.1 %copy-start.9 = (s32[24,12]{0,1:T(8,128)S(1)}, s32[24,12]{0,1:T(8,128)}, u32[]{:S(2)}) copy-start(s32[24,12]{0,1:T(8,128)} %param.15) | copy-start | bytes 3460
  13.4 3.0 %copy-start.7 = (bf16[8,24,180]{2,1,0:T(8,128)(2,1)S(1)}, bf16[8,24,180]{2,1,0:T(8,128)(2,1)}, u32[]{:S(2)}) copy-start(bf16[8,24,180]{2,1,0:T(8,128)(2,1)} %param.12) | copy-start | bytes 207364
  15.7 3.2 %copy-start = (f32[360,16]{1,0:T(8,128)}, f32[360,16]{1,0:T(8,128)S(1)}, u32[]{:S(2)}) copy-start(f32[360,16]{1,0:T(8,128)S(1)} %pad.8.table) | copy-start | bytes 69124
  169.1 84.9 %copy-start.2 = (f32[51840]{0:T(1024)S(1)}, f32[51840]{0:T(1024)}, u32[]{:S(2)}) copy-start(f32[51840]{0:T(1024)} %param.17) | copy-start | bytes 622084
  169.1 84.9 %copy-start.4 = (f32[51840]{0:T(1024)S(1)}, f32[51840]{0:T(1024)}, u32[]{:S(2)}) copy-start(f32[51840]{0:T(1024)} %param.19) | copy-start | bytes 622084
  169.1 84.9 %copy-start.5 = (f32[51840]{0:T(1024)S(1)}, f32[51840]{0:T(1024)}, u32[]{:S(2)}) copy-start(f32[51840]{0:T(1024)} %param.18) | copy-start | bytes 622084
  169.1 86.7 %copy-start.6 = (f32[51840]{0:T(1024)S(1)}, f32[51840]{0:T(1024)}, u32[]{:S(2)}) copy-start(f32[51840]{0:T(1024)} %param.20) | copy-start | bytes 622084
  255.9 11.4 %copy-start.1 = (f32[51840]{0:T(1024)}, f32[51840]{0:T(1024)S(1)}, u32[]{:S(2)}) copy-start(f32[51840]{0:T(1024)S(1)} %get-tuple-element.70) | copy-start | bytes 622084
  256.6 10.7 %copy-start.3 = (f32[405,128]{1,0:T(8,128)S(1)}, f32[405,128]{1,0:T(8,128)}, u32[]{:S(2)}) copy-start(f32[405,128]{1,0:T(8,128)} %get-tuple-element.41) | copy-start | bytes 622084
